TPU v7x, 32 devices: a whole 2x2x4 slice. The times are simulated.
32 devices in a mesh: dom: 2 (over y), wide: 16 (over z, x, core).
Axes of the slice: x: 2, y: 2, z: 4, core: 2. Of those that a mesh axis runs over, the one named last changes fastest.
Arguments:
- embeddings: bfloat16 [16384, 768], P(('dom', 'wide')), parts along dimension 0, may hold values from -6 to 6
- cluster_id: int32 [16384, 1], P(('dom', 'wide')), parts along dimension 0, may hold values from 0 to 7; in each aligned block of 512 rows (0 to 511, 512 to 1023, ...) at most 160 rows name the same one
Outputs:
- max_similarity: float32 [16384], P(('dom', 'wide')), parts along dimension 0
There are 2 independent parts, one for each index of `dom`. A program takes and returns all parts, laid end to end along the dimension named above; each array names one. Nothing has to cross between parts.
Inputs may be any that keep to these rules, and one draw needn't show every extreme that they name: `cluster_id`: among the 512 rows of one device (aligned blocks of 512 rows), no cluster appears more than 160 times; every cluster has some row.
All inputs are finite; a program needn't handle non-finite values.
Results may differ from a plain program's by a relative error of at most 0.0014.
Values may be sent and summed in bfloat16 or wider, within the bound.
No kernel may reach another device: no remote copies, remote signals or barrier semaphores. Data moves between devices by JAX's collectives and lax.ppermute only.
A program may use at most 64 MiB of HBM per device.

v0:
```python
import math

import jax
import jax.numpy as jnp
from jax import lax
from jax.sharding import PartitionSpec as P


def swapped(value, axis, bit):
    mask = 2**bit
    pairs = [(source, source ^ mask) for source in range(lax.axis_size(axis))]
    return lax.ppermute(value, axis, pairs)


def normalize(embedded):
    values = embedded.astype(jnp.float32)
    inverse = lax.rsqrt(jnp.mean(values * values, axis=1, keepdims=True) + 1e-06)
    return (values * inverse * (1.0 / math.sqrt(values.shape[1]))).astype(jnp.bfloat16)


def pair_scores(queries, key_rows):
    return jnp.einsum("qd,kd->qk", queries, key_rows, preferred_element_type=jnp.float32)


def masked_max(scores, allowed):
    return jnp.max(jnp.where(allowed, scores, -1.0), axis=1)


def per_device(embeddings, cluster_id):
    axis_size = lax.axis_size("wide")
    rows_dev = embeddings.shape[0]
    feature_dim = embeddings.shape[1]
    clusters = axis_size // 2
    capacity = (5 * rows_dev + 2 * axis_size - 1) // (2 * axis_size)
    buffer_rows = axis_size * capacity
    unit_rows = normalize(embeddings)
    labels = cluster_id[:, 0]
    my_index = lax.axis_index("wide")
    my_flip = my_index % 2
    position = lax.iota(jnp.int32, rows_dev)
    same_cluster = labels[:, None] == labels[None, :]
    earlier = position[None, :] < position[:, None]
    local_rank = jnp.sum((same_cluster & earlier).astype(jnp.int32), axis=1)
    target = 2 * labels + (local_rank + my_flip) % 2
    slot_index = target * capacity + local_rank // 2
    outgoing = jnp.zeros((buffer_rows, feature_dim), jnp.bfloat16).at[slot_index].set(unit_rows)
    cluster_count = jnp.sum(
        (labels[:, None] == lax.iota(jnp.int32, clusters)[None, :]).astype(jnp.int32), axis=0
    )
    parity = lax.iota(jnp.int32, axis_size) % 2
    send_count = (jnp.repeat(cluster_count, 2) + 1 - (parity + my_flip) % 2) // 2
    outgoing_blocks = outgoing.reshape(axis_size, capacity, feature_dim)
    count_blocks = send_count.reshape(axis_size, 1)
    received, counts = (
        lax.all_to_all(outgoing_blocks, "wide", split_axis=0, concat_axis=0, tiled=True),
        lax.all_to_all(count_blocks, "wide", split_axis=0, concat_axis=0, tiled=True),
    )
    own_rows = received.reshape(buffer_rows, feature_dim)
    partner, partner_counts = swapped((own_rows, counts), "wide", 0)
    side_bit = my_index % 2
    slot_pos = lax.iota(jnp.int32, capacity)
    sources = lax.iota(jnp.int32, axis_size)
    base_key = (sources[:, None] * (2 * capacity) + 2 * slot_pos[None, :]).reshape(-1)
    source_parity = jnp.repeat(sources % 2, capacity)
    own_key = base_key + (side_bit + source_parity) % 2
    partner_key = base_key + (1 - side_bit + source_parity) % 2
    own_live = (slot_pos[None, :] < counts).reshape(-1)
    partner_live = (slot_pos[None, :] < partner_counts).reshape(-1)
    blocks = 8
    query_rows = own_rows.reshape(blocks, -1, feature_dim)
    query_key = own_key.reshape(blocks, -1)

    def self_max(pieces):
        queries, keys_here = pieces
        return masked_max(
            pair_scores(queries, own_rows),
            own_live[None, :] & (own_key[None, :] < keys_here[:, None]),
        )

    self_best = lax.map(self_max, (query_rows, query_key)).reshape(-1)
    first = side_bit == 0
    left_rows = jnp.where(first, own_rows, partner)
    left_key = jnp.where(first, own_key, partner_key)
    left_live = jnp.where(first, own_live, partner_live)
    right_rows = jnp.where(first, partner, own_rows)
    right_key = jnp.where(first, partner_key, own_key)
    right_live = jnp.where(first, partner_live, own_live)
    half_rows = buffer_rows // 2
    start = side_bit * half_rows
    lower_rows = lax.dynamic_slice_in_dim(left_rows, start, half_rows, 0).reshape(
        blocks // 2, -1, feature_dim
    )
    lower_key = lax.dynamic_slice_in_dim(left_key, start, half_rows, 0).reshape(blocks // 2, -1)
    lower_live = lax.dynamic_slice_in_dim(left_live, start, half_rows, 0).reshape(blocks // 2, -1)

    def cross_max(pieces):
        queries, keys_here, live_here = pieces
        scores = pair_scores(queries, right_rows)
        row_best = masked_max(
            scores, right_live[None, :] & (right_key[None, :] < keys_here[:, None])
        )
        column_mask = live_here[:, None] & (keys_here[:, None] < right_key[None, :])
        column_best = jnp.max(jnp.where(column_mask, scores, -1.0), axis=0)
        return (row_best, column_best)

    row_best, column_best = lax.map(cross_max, (lower_rows, lower_key, lower_live))
    row_best = row_best.reshape(-1)
    column_best = jnp.max(column_best, axis=0)
    placed = lax.dynamic_update_slice_in_dim(
        jnp.full((buffer_rows,), -1.0, jnp.float32), row_best, start, 0
    )
    kept = jnp.where(first, placed, column_best)
    handed = jnp.where(first, column_best, placed)
    returned = swapped(handed, "wide", 0)
    best_all = jnp.maximum(self_best, jnp.maximum(kept, returned))
    back = lax.all_to_all(
        best_all.reshape(axis_size, capacity), "wide", split_axis=0, concat_axis=0, tiled=True
    )
    return back.reshape(-1)[slot_index]


def solution(mesh):
    placed = (P(("dom", "wide"), None), P(("dom", "wide"), None))
    return jax.shard_map(
        per_device, mesh=mesh, in_specs=placed, out_specs=P(("dom", "wide")), check_vma=False
    )
```

profile of v0, /device:TPU:0, one launch (start us, length us, event | category | flops | bytes accessed | tf_op | source)
XLA Modules:
  0.0 119.5 jit_solution(761466265437939160)
XLA Ops:
  0.0 1.0 convert_reduce_fusion
  1.0 1.4 %fusion.24 = f32[512]{0:T(512)S(1)} fusion(bf16[512,768]{1,0:T(8,128)(2,1)} %param.6), kind=kLoop, calls=%fused_computation.45 | loop fusion | flops 1179136 | bytes 788480 | tf_op jit(solution)/shard_map/reduce_sum | solution.py:17
  2.4 0.7 compare_select_fusion
  3.1 4.7 %scatter_custom_fusion = bf16[1280,768]{1,0:T(8,128)(2,1)} fusion(s32[512]{0:T(512)S(1)} %bitcast.57, bf16[]{:T(256)} %constant.137.clone.1, bf16[512,768]{1,0:T(8,128)(2,1)} %param.6, f32[]{:T(128)} %constant.146.clone.1, f32[512]{0:T(512)S(1)} %add_rsqrt_fusion), kind=kCustom, calls=%fused_computation.52 | custom fusion | flops 1572864 | bytes 2754566 | tf_op jit(solution)/shard_map/scatter | solution.py:46
  7.8 7.5 %all-to-all-start.1 = ((bf16[16,80,768]{2,1,0:T(8,128)(2,1)}), bf16[16,80,768]{2,1,0:T(8,128)(2,1)S(1)}, u32[]{:S(2)}, u32[]{:S(2)}) async-start(bf16[16,80,768]{2,1,0:T(8,128)(2,1)} %bitcast.46), calls=%async_computation.1 | async-start | bytes 3932160 | tf_op jit(solution)/shard_map/all_to_all | solution.py:55
  15.7 0.1 convert_reduce_fusion.1
  16.0 0.7 copy.5
  16.7 37.4 %all-to-all-done.1 = bf16[16,80,768]{2,1,0:T(8,128)(2,1)S(1)} async-done(((bf16[16,80,768]{2,1,0:T(8,128)(2,1)}), bf16[16,80,768]{2,1,0:T(8,128)(2,1)S(1)}, u32[]{:S(2)}, u32[]{:S(2)}) %all-to-all-start.1) | async-done | bytes 1966112 | tf_op jit(solution)/shard_map/all_to_all | solution.py:55
  54.0 10.7 %all-to-all-start = ((s32[16,1,1]{2,1,0:T(1,128)}), s32[16,1,1]{2,1,0:T(1,128)S(1)}, u32[]{:S(2)}, u32[]{:S(2)}) async-start(s32[16,1,1]{2,1,0:T(1,128)} %copy.5), calls=%async_computation | async-start | bytes 16384 | tf_op jit(solution)/shard_map/all_to_all | solution.py:56
  64.7 0.4 collective-permute-start.1
  65.9 5.3 %all-to-all-done = s32[16,1,1]{2,1,0:T(1,128)S(1)} async-done(((s32[16,1,1]{2,1,0:T(1,128)}), s32[16,1,1]{2,1,0:T(1,128)S(1)}, u32[]{:S(2)}, u32[]{:S(2)}) %all-to-all-start) | async-done | bytes 96 | tf_op jit(solution)/shard_map/all_to_all | solution.py:56
  71.2 0.4 reduce.1
  71.7 1.1 collective-permute-done
  72.8 0.1 select_n.191
  73.1 3.0 %broadcast_select_fusion = bf16[1280,768]{1,0:T(8,128)(2,1)} fusion(bf16[1280,768]{1,0:T(8,128)(2,1)} %collective-permute-done.1, pred[]{:T(512)} %eq.50, bf16[16,80,768]{2,1,0:T(8,128)(2,1)S(1)} %all-to-all-done.1), kind=kLoop, calls=%fused_computation.44 | loop fusion | flops 983040 | bytes 5898241 | tf_op jit(solution)/shard_map/jit(_where)/select_n | solution.py:85
  76.1 1.4 %dynamic-slice_select_fusion = bf16[640,768]{1,0:T(8,128)(2,1)S(1)} fusion(bf16[1280,768]{1,0:T(8,128)(2,1)} %collective-permute-done.1, s32[]{:T(128)S(6)} %select_n.186, bf16[1280,768]{1,0:T(8,128)(2,1)S(1)} %bitcast.41, pred[]{:T(512)} %eq.50), kind=kLoop, calls=%fused_computation.51 | loop fusion | flops 491520 | bytes 2949125 | tf_op jit(solution)/shard_map/jit(_where)/select_n | solution.py:82
  77.6 13.4 %while.26 = (s32[]{:T(128)}, f32[4,160]{1,0:T(4,128)S(1)}, f32[4,1280]{1,0:T(4,128)S(1)}, s32[4,160]{1,0:T(4,128)S(1)}, bf16[4,160,768]{2,1,0:T(8,128)(2,1)S(1)}...) while((s32[]{:T(128)}, f32[4,160]{1,0:T(4,128)S(1)}, ...), condition=%wide.region_10.11_spmd.clone.clone, body=%wide.region_7.10_spmd.clone.clone.sunk | while | flops 316246880 | bytes 2323947 | solution.py:106
  78.2 0.1 select_n.336
  78.3 2.5 %select_reduce_fusion.3 = (f32[1280]{0:T(1024)S(1)}, f32[160]{0:T(256)S(1)}) fusion(s32[1280]{0:T(1024)S(1)} %fusion.69, s32[160]{0:T(256)S(1)} %bitcast.54, pred[160]{0:T(512)(128)(4,1)S(1)} %dynamic-slice_reduce_fusion.2, pred[1280]{0:T(1024)(128)(4,1)S(1)} %select_n.336, bf16[1280,768]{1,0:T(8,128)(2,1)} %get-tuple-element.460, ...), kind=kOutput, calls=%fused_computation.19.clone.1 | convolution fusion | flops 316209760 | bytes 2229380 | tf_op jit(solution)/shard_map/while/body/eval_jaxpr/qd,kd->qk/dot_general | solution.py:22
  81.5 0.1 select_n.336
  81.6 2.5 %select_reduce_fusion.3 = (f32[1280]{0:T(1024)S(1)}, f32[160]{0:T(256)S(1)}) fusion(s32[1280]{0:T(1024)S(1)} %fusion.69, s32[160]{0:T(256)S(1)} %bitcast.54, pred[160]{0:T(512)(128)(4,1)S(1)} %dynamic-slice_reduce_fusion.2, pred[1280]{0:T(1024)(128)(4,1)S(1)} %select_n.336, bf16[1280,768]{1,0:T(8,128)(2,1)} %get-tuple-element.460, ...), kind=kOutput, calls=%fused_computation.19.clone.1 | convolution fusion | flops 316209760 | bytes 2229380 | tf_op jit(solution)/shard_map/while/body/eval_jaxpr/qd,kd->qk/dot_general | solution.py:22
  84.9 0.1 select_n.336
  85.0 2.5 %select_reduce_fusion.3 = (f32[1280]{0:T(1024)S(1)}, f32[160]{0:T(256)S(1)}) fusion(s32[1280]{0:T(1024)S(1)} %fusion.69, s32[160]{0:T(256)S(1)} %bitcast.54, pred[160]{0:T(512)(128)(4,1)S(1)} %dynamic-slice_reduce_fusion.2, pred[1280]{0:T(1024)(128)(4,1)S(1)} %select_n.336, bf16[1280,768]{1,0:T(8,128)(2,1)} %get-tuple-element.460, ...), kind=kOutput, calls=%fused_computation.19.clone.1 | convolution fusion | flops 316209760 | bytes 2229380 | tf_op jit(solution)/shard_map/while/body/eval_jaxpr/qd,kd->qk/dot_general | solution.py:22
  88.2 0.1 select_n.336
  88.3 2.5 %select_reduce_fusion.3 = (f32[1280]{0:T(1024)S(1)}, f32[160]{0:T(256)S(1)}) fusion(s32[1280]{0:T(1024)S(1)} %fusion.69, s32[160]{0:T(256)S(1)} %bitcast.54, pred[160]{0:T(512)(128)(4,1)S(1)} %dynamic-slice_reduce_fusion.2, pred[1280]{0:T(1024)(128)(4,1)S(1)} %select_n.336, bf16[1280,768]{1,0:T(8,128)(2,1)} %get-tuple-element.460, ...), kind=kOutput, calls=%fused_computation.19.clone.1 | convolution fusion | flops 316209760 | bytes 2229380 | tf_op jit(solution)/shard_map/while/body/eval_jaxpr/qd,kd->qk/dot_general | solution.py:22
  91.1 0.3 dynamic_update_slice.15
  91.4 11.8 %while.25 = (s32[]{:T(128)}, f32[8,160]{1,0:T(8,128)S(1)}, s32[8,160]{1,0:T(8,128)S(1)}, bf16[8,160,768]{2,1,0:T(8,128)(2,1)S(1)}, bf16[1280,768]{1,0:T(8,128)(2...) while((s32[]{:T(128)}, f32[8,160]{1,0:T(8,128)S(1)}, ...), condition=%wide.region_6.7_spmd.clone, body=%wide.region_4.6_spmd.clone.sunk | while | flops 315409760 | bytes 2276857 | solution.py:80
  91.8 0.1 and.250
  91.9 0.9 fusion.67
  93.3 0.1 and.250
  93.4 0.9 fusion.67
  94.8 0.1 and.250
  94.9 0.9 fusion.67
  96.3 0.1 and.250
  96.4 0.9 fusion.67
  97.8 0.1 and.250
  97.9 0.9 fusion.67
  99.2 0.1 and.250
  99.3 0.9 fusion.67
  100.8 0.9 fusion.67
  102.2 0.1 and.250
  102.3 0.9 fusion.67
  103.4 0.7 all_to_all.18
  104.1 3.5 %all-to-all-start.2 = ((f32[16,1,80]{2,1,0:T(1,128)}), f32[16,1,80]{2,1,0:T(1,128)S(1)}, u32[]{:S(2)}, u32[]{:S(2)}) async-start(f32[16,1,80]{2,1,0:T(1,128)} %all_to_all.18), calls=%async_computation.2 | async-start | bytes 16384 | tf_op jit(solution)/shard_map/all_to_all | solution.py:116
  107.6 6.4 %all-to-all-done.2 = f32[16,1,80]{2,1,0:T(1,128)S(1)} async-done(((f32[16,1,80]{2,1,0:T(1,128)}), f32[16,1,80]{2,1,0:T(1,128)S(1)}, u32[]{:S(2)}, u32[]{:S(2)}) %all-to-all-start.2) | async-done | bytes 5152 | tf_op jit(solution)/shard_map/all_to_all | solution.py:116
  114.0 0.5 broadcast.407
  114.5 0.7 reduce.7
  115.2 4.3 %gather_fusion = f32[512]{0:T(512)} fusion(f32[1280]{0:T(1024)S(1)} %reshape.313, s32[1024]{0:T(1024)S(1)} %pad_clamp_fusion), kind=kCustom, calls=%fused_computation | custom fusion | bytes 6144 | tf_op jit(solution)/shard_map/gather | solution.py:119
  (166 shorter events, 8.3 us)
Async XLA Ops:
  7.8 7.9 %copy-start = (s32[512,1]{0,1:T(1,128)S(1)}, s32[512,1]{0,1:T(1,128)}, u32[]{:S(2)}) copy-start(s32[512,1]{0,1:T(1,128)} %param.7) | copy-start | bytes 6148
  7.8 46.2 %all-to-all-start.1 = ((bf16[16,80,768]{2,1,0:T(8,128)(2,1)}), bf16[16,80,768]{2,1,0:T(8,128)(2,1)S(1)}, u32[]{:S(2)}, u32[]{:S(2)}) async-start(bf16[16,80,768]{2,1,0:T(8,128)(2,1)} %bitcast.46), calls=%async_computation.1 | async-start | bytes 3932160 | tf_op jit(solution)/shard_map/all_to_all | solution.py:55
  54.0 17.1 %all-to-all-start = ((s32[16,1,1]{2,1,0:T(1,128)}), s32[16,1,1]{2,1,0:T(1,128)S(1)}, u32[]{:S(2)}, u32[]{:S(2)}) async-start(s32[16,1,1]{2,1,0:T(1,128)} %copy.5), calls=%async_computation | async-start | bytes 16384 | tf_op jit(solution)/shard_map/all_to_all | solution.py:56
  64.7 8.4 %collective-permute-start.1 = (bf16[1280,768]{1,0:T(8,128)(2,1)S(1)}, bf16[1280,768]{1,0:T(8,128)(2,1)}, u32[]{:S(2)}, u32[]{:S(2)}) collective-permute-start(bf16[1280,768]{1,0:T(8,128)(2,1)S(1)} %bitcast.40), channel_id=1, source_target_pairs={{0,1},{1,0},{2,3},{3,2},{4,5},{5,4},{6,7},{7,6},{8,9},{9,8},{10,11... | collective-permute-start | bytes 5898248 | tf_op jit(solution)/shard_map/ppermute | solution.py:12
  71.5 1.2 %collective-permute-start = (s32[16,1]{0,1:T(1,128)S(1)}, s32[16,1]{0,1:T(1,128)S(1)}, u32[]{:S(2)}, u32[]{:S(2)}) collective-permute-start(s32[16,1]{0,1:T(1,128)S(1)} %bitcast.48), channel_id=1, source_target_pairs={{0,1},{1,0},{2,3},{3,2},{4,5},{5,4},{6,7},{7,6},{8,9},{9,8},{10,11... | collective-permute-start | bytes 200 | tf_op jit(solution)/shard_map/ppermute | solution.py:12
  91.3 12.0 %collective-permute-start.2 = (f32[1280]{0:T(1024)S(1)}, f32[1280]{0:T(1024)S(1)}, u32[]{:S(2)}, u32[]{:S(2)}) collective-permute-start(f32[1280]{0:T(1024)S(1)} %broadcast_select_fusion.1), channel_id=1, source_target_pairs={{0,1},{1,0},{2,3},{3,2},{4,5},{5,4},{6,7},{7,6},{8,9},{9,8},{10,11... | collective-permute-start | bytes 15368 | tf_op jit(solution)/shard_map/ppermute | solution.py:12
  104.1 9.9 %all-to-all-start.2 = ((f32[16,1,80]{2,1,0:T(1,128)}), f32[16,1,80]{2,1,0:T(1,128)S(1)}, u32[]{:S(2)}, u32[]{:S(2)}) async-start(f32[16,1,80]{2,1,0:T(1,128)} %all_to_all.18), calls=%async_computation.2 | async-start | bytes 16384 | tf_op jit(solution)/shard_map/all_to_all | solution.py:116
where the time goes:
time: 120 us; the launch traced here: 119 us
  waiting for transfers between devices  50.1 us (42%)
  starting transfers between devices  22.2 us (18%)
  matrix products  17.4 us (14%)
  other arithmetic  15.8 us (13%)
  local copies, waits for them, and re-layouts  13.3 us (11%)
    all_to_all x1, waiting for transfers between devices, per_device(): lax.all_to_all(outgoing_blocks, 'wide', split_axis=0, concat_axis=0, tile...  37.4 us
    dot_general x12, matrix products, pair_scores(): jnp.einsum('qd,kd->qk', queries, key_rows, preferred_element_type=jnp.flo...  17.4 us
    all_to_all x1, starting transfers between devices, per_device(): lax.all_to_all(count_blocks, 'wide', split_axis=0, concat_axis=0, tiled=T...  10.7 us
    all_to_all x1, starting transfers between devices, per_device(): lax.all_to_all(outgoing_blocks, 'wide', split_axis=0, concat_axis=0, tile...  7.52 us
    all_to_all x1, waiting for transfers between devices, per_device(): lax.all_to_all(best_all.reshape(axis_size, capacity), 'wide', split_axis=...  6.38 us
    all_to_all x1, waiting for transfers between devices, per_device(): lax.all_to_all(count_blocks, 'wide', split_axis=0, concat_axis=0, tiled=T...  5.28 us
    scatter x1, other arithmetic, per_device(): jnp.zeros((buffer_rows, feature_dim), jnp.bfloat16).at[slot_index]  4.71 us
    gather x1, local copies, waits for them, and re-layouts, per_device(): return back.reshape(-1)[slot_index]  4.27 us
  transfers between devices with their start and end apart: 6, of which 4 were waited for; matrix products, arithmetic and copies ran while one was open for 12% of the time, Pallas kernels for 0%

commit v1 on v0

--- a/solution.py
+++ b/solution.py
@@ -1,8 +1,11 @@
+import functools
 import math
 
 import jax
 import jax.numpy as jnp
 from jax import lax
+from jax.experimental import pallas as pl
+from jax.experimental.pallas import tpu as pltpu
 from jax.sharding import PartitionSpec as P
 
 
@@ -26,7 +29,7 @@
     return jnp.max(jnp.where(allowed, scores, -1.0), axis=1)
 
 
-def per_device(embeddings, cluster_id):
+def routed(embeddings, cluster_id):
     axis_size = lax.axis_size("wide")
     rows_dev = embeddings.shape[0]
     feature_dim = embeddings.shape[1]
@@ -119,6 +122,179 @@
     return back.reshape(-1)[slot_index]
 
 
+LAYERS = 4
+TAG_ROWS = 16
+PARAMS = pltpu.CompilerParams(vmem_limit_bytes=16 * 1024 * 1024)
+
+
+def tag_kernel(rows_ref, label_ref, *out_refs):
+    rows, width = rows_ref.shape
+    codes = (label_ref[...] + 1).astype(jnp.float32)
+    whole_ref, head_ref, tail_ref = out_refs
+    cut = head_ref.shape[0] - TAG_ROWS
+    for part_ref, low, high in ((head_ref, 0, cut), (tail_ref, cut, rows)):
+        values = rows_ref[low:high, :].astype(jnp.float32)
+        inverse = lax.rsqrt(jnp.mean(values * values, axis=1, keepdims=True) + 1e-06)
+        unit = (values * inverse * (1.0 / math.sqrt(width))).astype(jnp.bfloat16)
+        whole_ref[low:high, :] = unit
+        part_ref[: high - low, :] = unit
+    for ref, low, high in ((whole_ref, 0, rows), (head_ref, 0, cut), (tail_ref, cut, rows)):
+        count = high - low
+        line = jnp.broadcast_to(codes[:, low:high], (TAG_ROWS, count)).astype(jnp.bfloat16)
+        ref[count:, :count] = line
+        if count < width:
+            ref[count:, count:] = jnp.zeros((TAG_ROWS, width - count), jnp.bfloat16)
+
+
+def tagged(embeddings, labels, cut):
+    rows, width = embeddings.shape
+    counts = (rows, cut, rows - cut)
+    return pl.pallas_call(
+        tag_kernel,
+        out_shape=[pltpu.VMEM((count + TAG_ROWS, width), jnp.bfloat16) for count in counts],
+        compiler_params=PARAMS,
+        name="tagged",
+    )(embeddings, labels.reshape(1, rows))
+
+
+def code_row(block_ref):
+    rows = block_ref.shape[0] - TAG_ROWS
+    return block_ref[rows:, :rows].astype(jnp.float32)[:1]
+
+
+def best_kernel(tasks, n_keys, n_queries, n_begun, *refs):
+    key_refs = refs[:n_keys]
+    query_refs = refs[n_keys : n_keys + n_queries]
+    begun_refs = refs[n_keys + n_queries : n_keys + n_queries + n_begun]
+    out_refs = refs[n_keys + n_queries + n_begun :]
+    index = lax.axis_index("wide")
+    switches = {"core": index % 2 == 1, "column": (index // 2) % 2 == 0}
+    key_codes = []
+    for ref in key_refs:
+        count = ref.shape[0] - TAG_ROWS
+        key_codes.append(jnp.transpose(jnp.broadcast_to(code_row(ref), (128, count))))
+    for q, query_ref in enumerate(query_refs):
+        rows = query_ref.shape[0] - TAG_ROWS
+        queries = query_ref[:rows, :]
+        row_code = code_row(query_ref)
+        best = [None] * (rows // 128)
+        for k, mode in tasks[q]:
+            code = row_code
+            if mode in switches:
+                code = jnp.where(switches[mode], row_code, -1.0)
+            count = key_refs[k].shape[0] - TAG_ROWS
+            scores = lax.dot_general(
+                key_refs[k][:count, :],
+                queries,
+                (((1,), (1,)), ((), ())),
+                preferred_element_type=jnp.float32,
+            )
+            for b in range(rows // 128):
+                low = b * 128
+                allowed = key_codes[k] == code[:, low : low + 128]
+                if mode == "before":
+                    key_at = lax.broadcasted_iota(jnp.int32, (count, 128), 0)
+                    query_at = lax.broadcasted_iota(jnp.int32, (count, 128), 1) + low
+                    allowed = allowed & (key_at < query_at)
+                kept = jnp.where(allowed, scores[:, low : low + 128], -1.0)
+                part = jnp.max(kept.reshape(count // 8, 8, 128), axis=0)
+                best[b] = part if best[b] is None else jnp.maximum(best[b], part)
+        for b, part in enumerate(best):
+            low = b * 128
+            line = jnp.max(part, axis=0, keepdims=True)
+            if q < n_begun:
+                line = jnp.maximum(line, begun_refs[q][:, low : low + 128])
+            out_refs[q][:, low : low + 128] = line
+
+
+def best_of(tasks, keys, queries, begun):
+    arrays = [
+        pltpu.with_memory_space_constraint(value, pltpu.VMEM)
+        for value in list(keys) + list(queries) + list(begun)
+    ]
+    key_rows = [value.shape[0] - TAG_ROWS for value in keys]
+    width = queries[0].shape[1]
+    pairs = sum(
+        key_rows[k] * (query.shape[0] - TAG_ROWS)
+        for query, listed in zip(queries, tasks)
+        for k, _ in listed
+    )
+    return pl.pallas_call(
+        functools.partial(best_kernel, tasks, len(keys), len(queries), len(begun)),
+        out_shape=[pltpu.VMEM((1, value.shape[0] - TAG_ROWS), jnp.float32) for value in queries],
+        in_specs=[pl.BlockSpec(memory_space=pltpu.VMEM)] * len(arrays),
+        cost_estimate=pl.CostEstimate(
+            flops=2 * pairs * width,
+            transcendentals=0,
+            bytes_accessed=sum(value.nbytes for value in arrays),
+        ),
+        compiler_params=PARAMS,
+    )(*arrays)
+
+
+def every(keys):
+    return [(k, "all") for k in keys]
+
+
+def layered(embeddings, cluster_id):
+    rows = embeddings.shape[0]
+    mine, head, tail = tagged(embeddings, cluster_id[:, 0], rows * 3 // 4)
+    spots = [(z, x, c) for z in range(LAYERS) for x in range(2) for c in range(2)]
+
+    def at(z, x, c):
+        return (z * 2 + x) * 2 + c
+
+    def sent(value, hops):
+        return lax.ppermute(value, "wide", hops)
+
+    across = [(at(z, x, c), at(z, 1 - x, c)) for z, x, c in spots]
+    beside = [(at(z, x, c), at(z, x, 1 - c)) for z, x, c in spots]
+    rise = [(at(z, x, c), at(z + 1, x, c)) for z, x, c in spots if z + 1 < LAYERS]
+    relay = [(at(z, x, c), at(z + 1, x, c)) for z, x, c in spots if z == 1]
+    fall = [(at(z, x, c), at(z - 1, x, c)) for z, x, c in spots if z == LAYERS - 1]
+    slant = [(at(z, x, c), at(z - 1, 1 - x, c)) for z, x, c in spots if z == LAYERS - 1]
+
+    below_head = sent(head, rise)
+    above = sent(mine, fall)
+    side = sent(mine, across)
+    below_tail = sent(tail, rise)
+    twin = sent(mine, beside)
+    far = sent(mine, slant)
+    below = [
+        below_head, sent(below_head, beside),
+        below_tail, sent(below_tail, beside),
+    ]
+    deep_head = sent(below_head, relay)
+    deep_tail = sent(below_tail, relay)
+    deep_first = [deep_head, sent(deep_head, beside)]
+    deep_last = [deep_tail, sent(deep_tail, beside)]
+
+    own = best_of([[(0, "before"), (1, "core")]], [mine, twin], [mine], [])
+    here = best_of(
+        [every([2, 3, 4, 5]), [(0, "column"), (1, "column")] + every([2, 3, 4, 5]), every([2, 3, 4, 5])],
+        [mine, twin] + below, [mine, side, above], own,
+    )
+    deeper = best_of([every([0, 1])] * 3, deep_first, [mine, side, above], here)
+    last = best_of(
+        [every([0, 1])] * 3 + [every(range(8))],
+        deep_last + deep_first + below, [mine, side, above, far], deeper,
+    )
+    lift = [(t, s) for s, t in fall]
+    tilt = [(t, s) for s, t in slant]
+    from_slant = sent(last[3], tilt)
+    from_side = sent(last[1], across)
+    from_below = sent(last[2], lift)
+    top = lax.axis_index("wide") // 4 == LAYERS - 1
+    outer = jnp.where(top, jnp.maximum(from_below, from_slant), -1.0)
+    return jnp.maximum(jnp.maximum(last[0], from_side), outer)[0]
+
+
+def per_device(embeddings, cluster_id):
+    if lax.axis_size("wide") == 4 * LAYERS:
+        return layered(embeddings, cluster_id)
+    return routed(embeddings, cluster_id)
+
+
 def solution(mesh):
     placed = (P(("dom", "wide"), None), P(("dom", "wide"), None))
     return jax.shard_map(

time: 120 us -> 81.6 us (0.68)
  the two profiles are of different devices: /device:TPU:0 before, /device:TPU:24 now
where the time goes in v1:
time: 81.6 us; the launch traced here: 81.3 us
  waiting for transfers between devices  34.5 us (42%)
  starting transfers between devices  32.6 us (40%)
  Pallas kernels  11.6 us (14%)
  local copies, waits for them, and re-layouts  1.81 us (2%)
    ppermute x15, waiting for transfers between devices, sent(): return lax.ppermute(value, 'wide', hops)  34.5 us
    ppermute x15, starting transfers between devices, sent(): return lax.ppermute(value, 'wide', hops)  32.6 us
    pallas_call x4, Pallas kernels, best_of(): pl.pallas_call(functools.partial(best_kernel, tasks, len(keys), len(queri...  11.3 us
    unnamed x4, local copies, waits for them, and re-layouts  1.81 us
  transfers between devices with their start and end apart: 15, of which 5 were waited for; matrix products, arithmetic and copies ran while one was open for 0% of the time, Pallas kernels for 9%

profile of v1, /device:TPU:24, one launch (start us, length us, event | category | flops | bytes accessed | tf_op | source)
XLA Modules:
  0.0 81.3 jit_solution(3651564857787704744)
XLA Ops:
  0.0 0.0 copy-start
  0.0 1.1 %copy-done = bf16[512,768]{1,0:T(8,128)(2,1)S(1)} copy-done((bf16[512,768]{1,0:T(8,128)(2,1)S(1)}, bf16[512,768]{1,0:T(8,128)(2,1)}, u32[]{:S(2)}) %copy-start) | copy-done | bytes 786456
  1.1 0.0 copy-start.1
  1.1 0.7 copy-done.1
  1.8 0.3 tagged.1
  2.1 1.3 %collective-permute-start.3 = (bf16[400,768]{1,0:T(8,128)(2,1)S(1)}, bf16[400,768]{1,0:T(8,128)(2,1)S(1)}, u32[]{:S(2)}, u32[]{:S(2)}) collective-permute-start(bf16[400,768]{1,0:T(8,128)(2,1)S(1)} %get-tuple-element.19), channel_id=1, source_target_pairs={{0,4},{1,5},{2,6},{3,7},{4,8},{5,9},{6,10},{7,11},{8,12},{9,13},{1... | collective-permute-start | bytes 1843208 | tf_op jit(solution)/shard_map/ppermute | solution.py:248
  3.4 1.3 %collective-permute-start = (bf16[144,768]{1,0:T(8,128)(2,1)S(1)}, bf16[144,768]{1,0:T(8,128)(2,1)S(1)}, u32[]{:S(2)}, u32[]{:S(2)}) collective-permute-start(bf16[144,768]{1,0:T(8,128)(2,1)S(1)} %get-tuple-element.18), channel_id=1, source_target_pairs={{0,4},{1,5},{2,6},{3,7},{4,8},{5,9},{6,10},{7,11},{8,12},{9,13},{1... | collective-permute-start | bytes 663560 | tf_op jit(solution)/shard_map/ppermute | solution.py:248
  4.7 0.1 collective-permute-start.11
  4.8 19.5 %collective-permute-done.refs_4_.refs_6_ = bf16[144,768]{1,0:T(8,128)(2,1)S(1)} collective-permute-done((bf16[144,768]{1,0:T(8,128)(2,1)S(1)}, bf16[144,768]{1,0:T(8,128)(2,1)S(1)}, u32[]{:S(2)}, u32[]{:S(2)}) %collective-permute-start) | collective-permute-done | bytes 221216 | tf_op jit(solution)/shard_map/ppermute | solution.py:248
  24.4 0.0 collective-permute-start.7
  24.4 0.0 collective-permute-done.3.refs_2_.refs_4_
  24.4 0.7 collective-permute-start.4
  25.1 0.7 collective-permute-start.1
  25.8 1.6 %collective-permute-start.8 = (bf16[528,768]{1,0:T(8,128)(2,1)S(1)}, bf16[528,768]{1,0:T(8,128)(2,1)S(1)}, u32[]{:S(2)}, u32[]{:S(2)}) collective-permute-start(bf16[528,768]{1,0:T(8,128)(2,1)S(1)} %get-tuple-element.20.refs_0_.refs_2_.refs_6_.refs_8_), channel_id=1, source_target_pairs={{0,2},{1,3},{2,0},{3,1},{4,6},{5,7},{6,4},{7,5},{8,10},{9,11},{10,... | collective-permute-start | bytes 2433032 | tf_op jit(solution)/shard_map/ppermute | solution.py:248
  27.3 0.0 collective-permute-done.7.refs_5_.refs_7_
  27.3 3.6 %collective-permute-start.9 = (bf16[528,768]{1,0:T(8,128)(2,1)S(1)}, bf16[528,768]{1,0:T(8,128)(2,1)S(1)}, u32[]{:S(2)}, u32[]{:S(2)}) collective-permute-start(bf16[528,768]{1,0:T(8,128)(2,1)S(1)} %get-tuple-element.20.refs_0_.refs_2_.refs_6_.refs_8_), channel_id=1, source_target_pairs={{12,8},{13,9},{14,10},{15,11},{28,24},{29,25},{30,26},{31,27}} | collective-permute-start | bytes 2433032 | tf_op jit(solution)/shard_map/ppermute | solution.py:248
  30.9 0.0 collective-permute-done.1.refs_0_
  30.9 0.1 collective-permute-start.6
  31.0 0.0 collective-permute-done.11.refs_1_
  31.0 19.6 %collective-permute-start.10 = (bf16[528,768]{1,0:T(8,128)(2,1)S(1)}, bf16[528,768]{1,0:T(8,128)(2,1)S(1)}, u32[]{:S(2)}, u32[]{:S(2)}) collective-permute-start(bf16[528,768]{1,0:T(8,128)(2,1)S(1)} %get-tuple-element.20.refs_0_.refs_2_.refs_6_.refs_8_), channel_id=1, source_target_pairs={{12,10},{13,11},{14,8},{15,9},{28,26},{29,27},{30,24},{31,25}} | collective-permute-start | bytes 2433032 | tf_op jit(solution)/shard_map/ppermute | solution.py:248
  50.6 0.0 collective-permute-done.4.refs_0_.refs_2_
  50.6 0.3 collective-permute-start.5
  50.9 1.0 %shard_map.28.refs_9_ = f32[1,512]{1,0:T(1,128)S(1)} custom-call(bf16[528,768]{1,0:T(8,128)(2,1)S(1)} %get-tuple-element.20.refs_0_.refs_2_.refs_6_.refs_8_, bf16[528,768]{1,0:T(8,128)(2,1)S(1)} %collective-permute-done.11.refs_1_, bf16[528,768]{1,0:T(8,128)(2,1)S(1)} %get-tuple-element.20.refs_0_.refs_2_.refs_6_.refs_8_), custom_call_target="tpu_custom_call" | custom-call | flops 805306368 | bytes 2433024 | tf_op jit(solution)/shard_map/pallas_call | solution.py:222
  51.9 0.0 collective-permute-done.8.refs_7_.refs_3_.refs_9_
  51.9 0.3 collective-permute-start.2
  52.3 0.0 collective-permute-done.9.refs_8_.refs_4_.refs_10_
  52.3 0.0 collective-permute-done.6.refs_3_.refs_5_
  52.3 4.3 %shard_map.29 = (f32[1,512]{1,0:T(1,128)S(1)}, f32[1,512]{1,0:T(1,128)S(1)}, f32[1,512]{1,0:T(1,128)S(1)}) custom-call(bf16[528,768]{1,0:T(8,128)(2,1)S(1)} %get-tuple-element.20.refs_0_.refs_2_.refs_6_.refs_8_, bf16[528,768]{1,0:T(8,128)(2,1)S(1)} %collective-permute-done.11.refs_1_, bf16[400,768]{1,0:T(8,128)(2,1)S(1)} %collective-permute-done.3.refs_2_.refs_4_, ...), custom_call_target="tpu_custom_call" | custom-call | flops 3221225472 | bytes 5728256 | tf_op jit(solution)/shard_map/pallas_call | solution.py:222
  56.6 0.0 collective-permute-done.5.refs_1_.refs_3_
  56.7 2.0 %shard_map.30 = (f32[1,512]{1,0:T(1,128)S(1)}, f32[1,512]{1,0:T(1,128)S(1)}, f32[1,512]{1,0:T(1,128)S(1)}) custom-call(bf16[400,768]{1,0:T(8,128)(2,1)S(1)} %collective-permute-done.4.refs_0_.refs_2_, bf16[400,768]{1,0:T(8,128)(2,1)S(1)} %collective-permute-done.5.refs_1_.refs_3_, bf16[528,768]{1,0:T(8,128)(2,1)S(1)} %get-tuple-element.20.refs_0_.refs_2_.refs_6_.refs_8_, ...), custom_call_target="tpu_custom_call" | custom-call | flops 1811939328 | bytes 3667968 | tf_op jit(solution)/shard_map/pallas_call | solution.py:222
  58.7 0.0 collective-permute-done.2.refs_1_
  58.7 9.8 %collective-permute-done.10.refs_11_ = bf16[528,768]{1,0:T(8,128)(2,1)S(1)} collective-permute-done((bf16[528,768]{1,0:T(8,128)(2,1)S(1)}, bf16[528,768]{1,0:T(8,128)(2,1)S(1)}, u32[]{:S(2)}, u32[]{:S(2)}) %collective-permute-start.10) | collective-permute-done | bytes 811040 | tf_op jit(solution)/shard_map/ppermute | solution.py:248
  68.5 3.9 %shard_map.31 = (f32[1,512]{1,0:T(1,128)S(1)}, f32[1,512]{1,0:T(1,128)S(1)}, f32[1,512]{1,0:T(1,128)S(1)}, f32[1,512]{1,0:T(1,128)S(1)}) custom-call(bf16[144,768]{1,0:T(8,128)(2,1)S(1)} %collective-permute-done.1.refs_0_, bf16[144,768]{1,0:T(8,128)(2,1)S(1)} %collective-permute-done.2.refs_1_, bf16[400,768]{1,0:T(8,128)(2,1)S(1)} %collective-permute-done.4.refs_0_.refs_2_, ...), custom_call_target="tpu_custom_call" | custom-call | flops 2214592512 | bytes 6592512 | tf_op jit(solution)/shard_map/pallas_call | solution.py:222
  72.4 0.6 collective-permute-start.12
  73.0 1.3 %collective-permute-start.13 = (f32[1,512]{1,0:T(1,128)S(1)}, f32[1,512]{1,0:T(1,128)S(1)}, u32[]{:S(2)}, u32[]{:S(2)}) collective-permute-start(f32[1,512]{1,0:T(1,128)S(1)} %get-tuple-element.29), channel_id=1, source_target_pairs={{8,12},{9,13},{10,14},{11,15},{24,28},{25,29},{26,30},{27,31}} | collective-permute-start | bytes 6152 | tf_op jit(solution)/shard_map/ppermute | solution.py:248
  74.3 1.3 %collective-permute-start.14 = (f32[1,512]{1,0:T(1,128)S(1)}, f32[1,512]{1,0:T(1,128)S(1)}, u32[]{:S(2)}, u32[]{:S(2)}) collective-permute-start(f32[1,512]{1,0:T(1,128)S(1)} %get-tuple-element.30), channel_id=1, source_target_pairs={{10,12},{11,13},{8,14},{9,15},{26,28},{27,29},{24,30},{25,31}} | collective-permute-start | bytes 6152 | tf_op jit(solution)/shard_map/ppermute | solution.py:248
  75.6 0.5 collective-permute-done.12
  76.1 3.2 %collective-permute-done.13 = f32[1,512]{1,0:T(1,128)S(1)} collective-permute-done((f32[1,512]{1,0:T(1,128)S(1)}, f32[1,512]{1,0:T(1,128)S(1)}, u32[]{:S(2)}, u32[]{:S(2)}) %collective-permute-start.13) | collective-permute-done | bytes 2080 | tf_op jit(solution)/shard_map/ppermute | solution.py:248
  79.3 1.5 %collective-permute-done.14 = f32[1,512]{1,0:T(1,128)S(1)} collective-permute-done((f32[1,512]{1,0:T(1,128)S(1)}, f32[1,512]{1,0:T(1,128)S(1)}, u32[]{:S(2)}, u32[]{:S(2)}) %collective-permute-start.14) | collective-permute-done | bytes 2080 | tf_op jit(solution)/shard_map/ppermute | solution.py:248
  80.7 0.6 fusion
Async XLA Ops:
  0.0 1.1 %copy-start = (bf16[512,768]{1,0:T(8,128)(2,1)S(1)}, bf16[512,768]{1,0:T(8,128)(2,1)}, u32[]{:S(2)}) copy-start(bf16[512,768]{1,0:T(8,128)(2,1)} %rows_ref.1) | copy-start | bytes 2359300
  1.1 0.7 copy-start.1
  2.1 22.2 %collective-permute-start.3 = (bf16[400,768]{1,0:T(8,128)(2,1)S(1)}, bf16[400,768]{1,0:T(8,128)(2,1)S(1)}, u32[]{:S(2)}, u32[]{:S(2)}) collective-permute-start(bf16[400,768]{1,0:T(8,128)(2,1)S(1)} %get-tuple-element.19), channel_id=1, source_target_pairs={{0,4},{1,5},{2,6},{3,7},{4,8},{5,9},{6,10},{7,11},{8,12},{9,13},{1... | collective-permute-start | bytes 1843208 | tf_op jit(solution)/shard_map/ppermute | solution.py:248
  3.4 20.9 %collective-permute-start = (bf16[144,768]{1,0:T(8,128)(2,1)S(1)}, bf16[144,768]{1,0:T(8,128)(2,1)S(1)}, u32[]{:S(2)}, u32[]{:S(2)}) collective-permute-start(bf16[144,768]{1,0:T(8,128)(2,1)S(1)} %get-tuple-element.18), channel_id=1, source_target_pairs={{0,4},{1,5},{2,6},{3,7},{4,8},{5,9},{6,10},{7,11},{8,12},{9,13},{1... | collective-permute-start | bytes 663560 | tf_op jit(solution)/shard_map/ppermute | solution.py:248
  4.7 26.3 %collective-permute-start.11 = (bf16[528,768]{1,0:T(8,128)(2,1)S(1)}, bf16[528,768]{1,0:T(8,128)(2,1)S(1)}, u32[]{:S(2)}, u32[]{:S(2)}) collective-permute-start(bf16[528,768]{1,0:T(8,128)(2,1)S(1)} %get-tuple-element.20.refs_0_.refs_2_.refs_6_.refs_8_), channel_id=1, source_target_pairs={{0,1},{1,0},{2,3},{3,2},{4,5},{5,4},{6,7},{7,6},{8,9},{9,8},{10,11... | collective-permute-start | bytes 2433032 | tf_op jit(solution)/shard_map/ppermute | solution.py:248
  24.4 2.9 %collective-permute-start.7 = (bf16[144,768]{1,0:T(8,128)(2,1)S(1)}, bf16[144,768]{1,0:T(8,128)(2,1)S(1)}, u32[]{:S(2)}, u32[]{:S(2)}) collective-permute-start(bf16[144,768]{1,0:T(8,128)(2,1)S(1)} %collective-permute-done.refs_4_.refs_6_), channel_id=1, source_target_pairs={{0,1},{1,0},{2,3},{3,2},{4,5},{5,4},{6,7},{7,6},{8,9},{9,8},{10,11... | collective-permute-start | bytes 663560 | tf_op jit(solution)/shard_map/ppermute | solution.py:248
  24.4 26.2 %collective-permute-start.4 = (bf16[400,768]{1,0:T(8,128)(2,1)S(1)}, bf16[400,768]{1,0:T(8,128)(2,1)S(1)}, u32[]{:S(2)}, u32[]{:S(2)}) collective-permute-start(bf16[400,768]{1,0:T(8,128)(2,1)S(1)} %collective-permute-done.3.refs_2_.refs_4_), channel_id=1, source_target_pairs={{4,8},{5,9},{6,10},{7,11},{20,24},{21,25},{22,26},{23,27}} | collective-permute-start | bytes 1843208 | tf_op jit(solution)/shard_map/ppermute | solution.py:248
  25.1 5.9 %collective-permute-start.1 = (bf16[144,768]{1,0:T(8,128)(2,1)S(1)}, bf16[144,768]{1,0:T(8,128)(2,1)S(1)}, u32[]{:S(2)}, u32[]{:S(2)}) collective-permute-start(bf16[144,768]{1,0:T(8,128)(2,1)S(1)} %collective-permute-done.refs_4_.refs_6_), channel_id=1, source_target_pairs={{4,8},{5,9},{6,10},{7,11},{20,24},{21,25},{22,26},{23,27}} | collective-permute-start | bytes 663560 | tf_op jit(solution)/shard_map/ppermute | solution.py:248
  25.8 26.2 %collective-permute-start.8 = (bf16[528,768]{1,0:T(8,128)(2,1)S(1)}, bf16[528,768]{1,0:T(8,128)(2,1)S(1)}, u32[]{:S(2)}, u32[]{:S(2)}) collective-permute-start(bf16[528,768]{1,0:T(8,128)(2,1)S(1)} %get-tuple-element.20.refs_0_.refs_2_.refs_6_.refs_8_), channel_id=1, source_target_pairs={{0,2},{1,3},{2,0},{3,1},{4,6},{5,7},{6,4},{7,5},{8,10},{9,11},{10,... | collective-permute-start | bytes 2433032 | tf_op jit(solution)/shard_map/ppermute | solution.py:248
  27.3 25.0 %collective-permute-start.9 = (bf16[528,768]{1,0:T(8,128)(2,1)S(1)}, bf16[528,768]{1,0:T(8,128)(2,1)S(1)}, u32[]{:S(2)}, u32[]{:S(2)}) collective-permute-start(bf16[528,768]{1,0:T(8,128)(2,1)S(1)} %get-tuple-element.20.refs_0_.refs_2_.refs_6_.refs_8_), channel_id=1, source_target_pairs={{12,8},{13,9},{14,10},{15,11},{28,24},{29,25},{30,26},{31,27}} | collective-permute-start | bytes 2433032 | tf_op jit(solution)/shard_map/ppermute | solution.py:248
  30.9 21.4 %collective-permute-start.6 = (bf16[400,768]{1,0:T(8,128)(2,1)S(1)}, bf16[400,768]{1,0:T(8,128)(2,1)S(1)}, u32[]{:S(2)}, u32[]{:S(2)}) collective-permute-start(bf16[400,768]{1,0:T(8,128)(2,1)S(1)} %collective-permute-done.3.refs_2_.refs_4_), channel_id=1, source_target_pairs={{0,1},{1,0},{2,3},{3,2},{4,5},{5,4},{6,7},{7,6},{8,9},{9,8},{10,11... | collective-permute-start | bytes 1843208 | tf_op jit(solution)/shard_map/ppermute | solution.py:248
  31.0 37.5 %collective-permute-start.10 = (bf16[528,768]{1,0:T(8,128)(2,1)S(1)}, bf16[528,768]{1,0:T(8,128)(2,1)S(1)}, u32[]{:S(2)}, u32[]{:S(2)}) collective-permute-start(bf16[528,768]{1,0:T(8,128)(2,1)S(1)} %get-tuple-element.20.refs_0_.refs_2_.refs_6_.refs_8_), channel_id=1, source_target_pairs={{12,10},{13,11},{14,8},{15,9},{28,26},{29,27},{30,24},{31,25}} | collective-permute-start | bytes 2433032 | tf_op jit(solution)/shard_map/ppermute | solution.py:248
  50.6 6.0 %collective-permute-start.5 = (bf16[400,768]{1,0:T(8,128)(2,1)S(1)}, bf16[400,768]{1,0:T(8,128)(2,1)S(1)}, u32[]{:S(2)}, u32[]{:S(2)}) collective-permute-start(bf16[400,768]{1,0:T(8,128)(2,1)S(1)} %collective-permute-done.4.refs_0_.refs_2_), channel_id=1, source_target_pairs={{0,1},{1,0},{2,3},{3,2},{4,5},{5,4},{6,7},{7,6},{8,9},{9,8},{10,11... | collective-permute-start | bytes 1843208 | tf_op jit(solution)/shard_map/ppermute | solution.py:248
  51.9 6.8 %collective-permute-start.2 = (bf16[144,768]{1,0:T(8,128)(2,1)S(1)}, bf16[144,768]{1,0:T(8,128)(2,1)S(1)}, u32[]{:S(2)}, u32[]{:S(2)}) collective-permute-start(bf16[144,768]{1,0:T(8,128)(2,1)S(1)} %collective-permute-done.1.refs_0_), channel_id=1, source_target_pairs={{0,1},{1,0},{2,3},{3,2},{4,5},{5,4},{6,7},{7,6},{8,9},{9,8},{10,11... | collective-permute-start | bytes 663560 | tf_op jit(solution)/shard_map/ppermute | solution.py:248
  72.4 3.7 %collective-permute-start.12 = (f32[1,512]{1,0:T(1,128)S(1)}, f32[1,512]{1,0:T(1,128)S(1)}, u32[]{:S(2)}, u32[]{:S(2)}) collective-permute-start(f32[1,512]{1,0:T(1,128)S(1)} %get-tuple-element.28), channel_id=1, source_target_pairs={{0,2},{1,3},{2,0},{3,1},{4,6},{5,7},{6,4},{7,5},{8,10},{9,11},{10,... | collective-permute-start | bytes 6152 | tf_op jit(solution)/shard_map/ppermute | solution.py:248
  73.0 6.2 %collective-permute-start.13 = (f32[1,512]{1,0:T(1,128)S(1)}, f32[1,512]{1,0:T(1,128)S(1)}, u32[]{:S(2)}, u32[]{:S(2)}) collective-permute-start(f32[1,512]{1,0:T(1,128)S(1)} %get-tuple-element.29), channel_id=1, source_target_pairs={{8,12},{9,13},{10,14},{11,15},{24,28},{25,29},{26,30},{27,31}} | collective-permute-start | bytes 6152 | tf_op jit(solution)/shard_map/ppermute | solution.py:248
  74.3 6.4 %collective-permute-start.14 = (f32[1,512]{1,0:T(1,128)S(1)}, f32[1,512]{1,0:T(1,128)S(1)}, u32[]{:S(2)}, u32[]{:S(2)}) collective-permute-start(f32[1,512]{1,0:T(1,128)S(1)} %get-tuple-element.30), channel_id=1, source_target_pairs={{10,12},{11,13},{8,14},{9,15},{26,28},{27,29},{24,30},{25,31}} | collective-permute-start | bytes 6152 | tf_op jit(solution)/shard_map/ppermute | solution.py:248

commit v2 on v0

--- a/solution.py
+++ b/solution.py
@@ -1,8 +1,11 @@
+import functools
 import math
 
 import jax
 import jax.numpy as jnp
 from jax import lax
+from jax.experimental import pallas as pl
+from jax.experimental.pallas import tpu as pltpu
 from jax.sharding import PartitionSpec as P
 
 
@@ -26,7 +29,7 @@
     return jnp.max(jnp.where(allowed, scores, -1.0), axis=1)
 
 
-def per_device(embeddings, cluster_id):
+def routed(embeddings, cluster_id):
     axis_size = lax.axis_size("wide")
     rows_dev = embeddings.shape[0]
     feature_dim = embeddings.shape[1]
@@ -119,6 +122,299 @@
     return back.reshape(-1)[slot_index]
 
 
+LAYERS = 4
+TAG_ROWS = 8
+LANES = 128
+PARAMS = pltpu.CompilerParams(vmem_limit_bytes=16 * 1024 * 1024)
+
+
+def tag_kernel(rows_hbm, label_hbm, whole_ref, head_ref, tail_ref, rows_ref, label_ref, done):
+    rows, width = rows_ref.shape
+    cut = head_ref.shape[0] - TAG_ROWS
+    spans = [(low, low + rows // 4) for low in range(0, rows, rows // 4)]
+    labels = pltpu.make_async_copy(label_hbm, label_ref, done.at[len(spans)])
+    labels.start()
+    copies = []
+    for at, (low, high) in enumerate(spans):
+        part = pl.ds(low, high - low)
+        copies.append(pltpu.make_async_copy(rows_hbm.at[part], rows_ref.at[part], done.at[at]))
+        copies[-1].start()
+    labels.wait()
+    codes = (label_ref[...] + 1).astype(jnp.float32)
+    line = jnp.broadcast_to(codes, (TAG_ROWS, rows)).astype(jnp.bfloat16)
+    for ref, count in ((whole_ref, rows), (head_ref, cut)):
+        ref[count:, :rows] = line
+        if rows < width:
+            ref[count:, rows:] = jnp.zeros((TAG_ROWS, width - rows), jnp.bfloat16)
+    for copy, (low, high) in zip(copies, spans):
+        copy.wait()
+        values = rows_ref[low:high, :].astype(jnp.float32)
+        inverse = lax.rsqrt(jnp.mean(values * values, axis=1, keepdims=True) + 1e-06)
+        unit = (values * inverse * (1.0 / math.sqrt(width))).astype(jnp.bfloat16)
+        whole_ref[low:high, :] = unit
+        if high <= cut:
+            head_ref[low:high, :] = unit
+        else:
+            tail_ref[low - cut : high - cut, :] = unit
+
+
+def tagged(embeddings, labels):
+    rows, width = embeddings.shape
+    labels = labels.reshape(1, rows)
+    cut = rows * 3 // 4
+    shapes = ((rows + TAG_ROWS, width), (cut + TAG_ROWS, width), (rows - cut, width))
+    return pl.pallas_call(
+        tag_kernel,
+        out_shape=[pltpu.VMEM(shape, jnp.bfloat16) for shape in shapes],
+        in_specs=[pl.BlockSpec(memory_space=pltpu.HBM)] * 2,
+        scratch_shapes=[
+            pltpu.VMEM((rows, width), jnp.bfloat16),
+            pltpu.VMEM((1, rows), jnp.int32),
+            pltpu.SemaphoreType.DMA((5,)),
+        ],
+        compiler_params=PARAMS,
+        name="tagged",
+    )(*[pltpu.with_memory_space_constraint(value, pltpu.HBM) for value in (embeddings, labels)])
+
+
+class Block:
+    def __init__(self, rows_ref, tag_ref, low, count):
+        self.rows_ref = rows_ref
+        self.tag_ref = tag_ref
+        self.low = low
+        self.count = count
+
+    def rows(self):
+        return self.rows_ref[: self.count, :]
+
+    def codes(self):
+        tags = self.tag_ref[self.tag_ref.shape[0] - TAG_ROWS :, self.low : self.low + self.count]
+        return tags.astype(jnp.float32)[:1]
+
+    def columns(self):
+        return jnp.transpose(jnp.broadcast_to(self.codes(), (LANES, self.count)))
+
+
+def whole(ref):
+    return [Block(ref, ref, 0, ref.shape[0] - TAG_ROWS)]
+
+
+def split(head_ref, tail_ref):
+    cut = head_ref.shape[0] - TAG_ROWS
+    return [
+        Block(head_ref, head_ref, 0, cut),
+        Block(tail_ref, head_ref, cut, tail_ref.shape[0]),
+    ]
+
+
+def halves(upper_ref, lower_ref):
+    count = upper_ref.shape[0]
+    return [Block(upper_ref, lower_ref, 0, count), Block(lower_ref, lower_ref, count, count)]
+
+
+def raise_best(out_ref, low, query, keys, switch=None, before=False):
+    codes = query.codes()
+    if switch is not None:
+        codes = jnp.where(switch, codes, -1.0)
+    queries = query.rows()
+    best = [None] * (query.count // LANES)
+    merged = len(keys) > 1 and all(key.count < 2 * LANES for key in keys)
+    pieces = [keys] if merged else [[key] for key in keys]
+    for piece in pieces:
+        rows = jnp.concatenate([key.rows() for key in piece], axis=0) if merged else piece[0].rows()
+        columns = [key.columns() for key in piece]
+        columns = jnp.concatenate(columns, axis=0) if merged else columns[0]
+        count = rows.shape[0]
+        scores = lax.dot_general(
+            rows, queries, (((1,), (1,)), ((), ())), preferred_element_type=jnp.float32
+        )
+        for b in range(query.count // LANES):
+            span = slice(b * LANES, (b + 1) * LANES)
+            allowed = columns == codes[:, span]
+            if before:
+                key_at = lax.broadcasted_iota(jnp.int32, (count, LANES), 0)
+                query_at = lax.broadcasted_iota(jnp.int32, (count, LANES), 1) + b * LANES
+                allowed = allowed & (key_at < query_at)
+            kept = jnp.where(allowed, scores[:, span], -1.0)
+            part = jnp.max(kept.reshape(count // 8, 8, LANES), axis=0)
+            best[b] = part if best[b] is None else jnp.maximum(best[b], part)
+    for b, part in enumerate(best):
+        span = slice(low + b * LANES, low + (b + 1) * LANES)
+        line = jnp.max(part, axis=0, keepdims=True)
+        out_ref[:, span] = jnp.maximum(out_ref[:, span], line)
+
+
+def raise_all(outs, queries, keys):
+    for out_ref, blocks in zip(outs, queries):
+        for block in blocks:
+            raise_best(out_ref, block.low, block, keys)
+
+
+def place():
+    index = lax.axis_index("wide")
+    return index // 4, (index // 2) % 2, index % 2
+
+
+def own_kernel(mine_ref, twin_ref, out_ref):
+    core = place()[2]
+    out_ref[...] = jnp.full(out_ref.shape, -1.0, jnp.float32)
+    mine = whole(mine_ref)[0]
+    raise_best(out_ref, 0, mine, whole(mine_ref), before=True)
+
+    @pl.when(core == 1)
+    def _():
+        raise_best(out_ref, 0, mine, whole(twin_ref))
+
+
+def here_kernel(
+    own_ref, mine_ref, twin_ref, side_ref, ridge_ref, ridge_twin_ref,
+    head_ref, head_twin_ref, tail_ref, tail_twin_ref, mine_out, side_out, above_out,
+):
+    layer, column, _ = place()
+    mine_out[...] = own_ref[...]
+    for ref in (side_out, above_out):
+        ref[...] = jnp.full(ref.shape, -1.0, jnp.float32)
+    near = [whole(mine_ref), whole(side_ref)]
+
+    @pl.when(column == 0)
+    def _():
+        raise_all([side_out], [whole(side_ref)], whole(mine_ref) + whole(twin_ref))
+
+    @pl.when(layer % 2 == 1)
+    def _():
+        keys = split(head_ref, tail_ref) + split(head_twin_ref, tail_twin_ref)
+        raise_all([mine_out, side_out], near, keys)
+
+    @pl.when(layer == 2)
+    def _():
+        keys = whole(ridge_ref) + whole(ridge_twin_ref)
+        above = split(head_ref, tail_ref)
+        raise_all([mine_out, side_out, above_out], near + [above], keys)
+
+
+VIEWS = {
+    "whole": whole,
+    "split": split,
+    "halves": halves,
+    "end": lambda head_ref, tail_ref: split(head_ref, tail_ref)[1:],
+}
+
+
+def seen(views, refs):
+    listed = []
+    for view, count in views:
+        listed.append(VIEWS[view](*refs[:count]))
+        refs = refs[count:]
+    return listed, refs
+
+
+def deep_kernel(queries, keys, started, *refs):
+    layer = place()[0]
+    begun, refs = (refs[: len(queries)], refs[len(queries) :]) if started else ((), refs)
+    query_blocks, refs = seen(queries, refs)
+    key_blocks, outs = seen(keys, refs)
+    for at, ref in enumerate(outs):
+        ref[...] = begun[at][...] if started else jnp.full(ref.shape, -1.0, jnp.float32)
+
+    @pl.when(layer == 2)
+    def _():
+        raise_all(outs, query_blocks, [block for blocks in key_blocks for block in blocks])
+
+
+def scored(body, outputs, pairs, *arrays):
+    width = arrays[-1].shape[1]
+    return pl.pallas_call(
+        body,
+        out_shape=[pltpu.VMEM((1, count), jnp.float32) for count in outputs],
+        in_specs=[pl.BlockSpec(memory_space=pltpu.VMEM)] * len(arrays),
+        cost_estimate=pl.CostEstimate(
+            flops=2 * pairs * width,
+            transcendentals=0,
+            bytes_accessed=sum(value.nbytes for value in arrays),
+        ),
+        compiler_params=PARAMS,
+    )(*[pltpu.with_memory_space_constraint(value, pltpu.VMEM) for value in arrays])
+
+
+def deepened(begun, queries, keys):
+    def views(blocks):
+        return tuple((view, len(arrays)) for view, *arrays in blocks)
+
+    rows = [sum(value.shape[0] for value in arrays) // LANES * LANES for _, *arrays in queries]
+    ends = [arrays[-1].shape[0] // LANES * LANES for _, *arrays in keys]
+    started = begun is not None
+    body = functools.partial(deep_kernel, views(queries), views(keys), started)
+    arrays = [value for _, *values in (*queries, *keys) for value in values]
+    pairs = sum(rows) * sum(ends)
+    return scored(body, rows, pairs, *(begun if started else ()), *arrays)
+
+
+def layered(embeddings, cluster_id):
+    rows = embeddings.shape[0]
+    mine, head, tail = tagged(embeddings, cluster_id[:, 0])
+    spots = [(z, x, c) for z in range(LAYERS) for x in range(2) for c in range(2)]
+
+    def hops(move):
+        def at(z, x, c):
+            return (z * 2 + x) * 2 + c
+
+        return [(at(*spot), at(*move(*spot))) for spot in spots]
+
+    across = hops(lambda z, x, c: (z, 1 - x, c))
+    beside = hops(lambda z, x, c: (z, x, 1 - c))
+    outer = hops(lambda z, x, c: (z ^ 1, x, c))
+    inner = hops(lambda z, x, c: (z, x, 1 - c) if z in (0, 3) else (3 - z, x, c))
+    lift = [hop for hop in outer if hop[0] // 4 == 2]
+    tilt = [(source, target ^ 2) for source, target in lift]
+
+    def sent(value, pairs):
+        return lax.ppermute(value, "wide", pairs)
+
+    near_head = sent(head, outer)
+    ridge = sent(mine, inner)
+    side = sent(mine, across)
+    near_tail = sent(tail, outer)
+    twin = sent(mine, beside)
+    deep_head = sent(near_head, inner)
+    upper = sent(near_head[: rows // 2], across)
+    lower = sent(side[rows // 2 :], outer)
+    near_head_twin = sent(near_head, beside)
+    deep_tail = sent(near_tail, inner)
+    near_tail_twin = sent(near_tail, beside)
+    ridge_twin = sent(ridge, beside)
+    deep_head_twin = sent(deep_head, beside)
+    deep_tail_twin = sent(deep_tail, beside)
+
+    square = rows * rows
+    (own,) = scored(own_kernel, [rows], 2 * square, mine, twin)
+    first, second, third = scored(
+        here_kernel, [rows] * 3, 8 * square,
+        own, mine, twin, side, ridge, ridge_twin, near_head, near_head_twin, near_tail, near_tail_twin,
+    )
+    flat = [("whole", mine), ("whole", side)]
+    steep = [("split", near_head, near_tail), ("halves", upper, lower)]
+    (fourth,) = deepened(None, steep[1:], [("whole", ridge), ("whole", ridge_twin)])
+    best = deepened([first, second, third, fourth], flat + steep, [("whole", deep_head)])
+    other = [("whole", deep_head_twin)]
+    best_steep = deepened(best[2:], steep, other)
+    best_flat = deepened(best[:2], flat, other)
+    ends = [("end", deep_head, deep_tail), ("end", deep_head_twin, deep_tail_twin)]
+    third, fourth = deepened(best_steep, steep, ends)
+    first, second = deepened(best_flat, flat, ends)
+    from_below = sent(third, lift)
+    from_slant = sent(fourth, tilt)
+    from_side = sent(second, across)
+    top = lax.axis_index("wide") // 4 == LAYERS - 1
+    under = jnp.where(top, jnp.maximum(from_below, from_slant), -1.0)
+    return jnp.maximum(jnp.maximum(first, from_side), under)[0]
+
+
+def per_device(embeddings, cluster_id):
+    if lax.axis_size("wide") == 4 * LAYERS:
+        return layered(embeddings, cluster_id)
+    return routed(embeddings, cluster_id)
+
+
 def solution(mesh):
     placed = (P(("dom", "wide"), None), P(("dom", "wide"), None))
     return jax.shard_map(

time: 120 us -> 65.2 us (0.54)
  the two profiles are of different devices: /device:TPU:0 before, /device:TPU:26 now
where the time goes in v2:
time: 65.2 us; the launch traced here: 65 us
  waiting for transfers between devices  35.7 us (55%)
  starting transfers between devices  23.9 us (37%)
  Pallas kernels  4.64 us (7%)
    ppermute x17, waiting for transfers between devices, sent(): return lax.ppermute(value, 'wide', pairs)  35.7 us
    ppermute x17, starting transfers between devices, sent(): return lax.ppermute(value, 'wide', pairs)  23.9 us
    pallas_call x8, Pallas kernels, scored(): pl.pallas_call(body, out_shape=[pltpu.VMEM((1, count), jnp.float32) for c...  3.11 us
    pallas_call x1, Pallas kernels, tagged(): pl.pallas_call(tag_kernel, out_shape=[pltpu.VMEM(shape, jnp.bfloat16) for...  1.53 us
  transfers between devices with their start and end apart: 17, of which 8 were waited for; matrix products, arithmetic and copies ran while one was open for 0% of the time, Pallas kernels for 5%

profile of v2, /device:TPU:26, one launch (start us, length us, event | category | flops | bytes accessed | tf_op | source)
XLA Modules:
  0.0 65.0 jit_solution(6241613752437629433)
XLA Ops:
  0.0 1.5 %tagged.1 = (bf16[520,768]{1,0:T(8,128)(2,1)S(1)}, bf16[392,768]{1,0:T(8,128)(2,1)S(1)}, bf16[128,768]{1,0:T(8,128)(2,1)S(1)}) custom-call(bf16[512,768]{1,0:T(8,128)(2,1)} %rows_hbm.1, s32[1,512]{1,0:T(1,128)} %bitcast.2), custom_call_target="tpu_custom_call" | custom-call | tf_op jit(solution)/shard_map/tagged/pallas_call | solution.py:166
  1.5 0.1 collective-permute-start.2
  1.6 0.9 %collective-permute-start.4 = (bf16[392,768]{1,0:T(8,128)(2,1)S(1)}, bf16[392,768]{1,0:T(8,128)(2,1)S(1)}, u32[]{:S(2)}, u32[]{:S(2)}) collective-permute-start(bf16[392,768]{1,0:T(8,128)(2,1)S(1)} %get-tuple-element.24), channel_id=1, source_target_pairs={{0,4},{1,5},{2,6},{3,7},{4,0},{5,1},{6,2},{7,3},{8,12},{9,13},{10,... | collective-permute-start | bytes 1806344 | tf_op jit(solution)/shard_map/ppermute | solution.py:371
  2.5 0.5 collective-permute-start.1
  3.0 1.2 %collective-permute-start.6 = (bf16[128,768]{1,0:T(8,128)(2,1)S(1)}, bf16[128,768]{1,0:T(8,128)(2,1)S(1)}, u32[]{:S(2)}, u32[]{:S(2)}) collective-permute-start(bf16[128,768]{1,0:T(8,128)(2,1)S(1)} %get-tuple-element.25), channel_id=1, source_target_pairs={{0,4},{1,5},{2,6},{3,7},{4,0},{5,1},{6,2},{7,3},{8,12},{9,13},{10,... | collective-permute-start | bytes 589832 | tf_op jit(solution)/shard_map/ppermute | solution.py:371
  4.2 0.0 collective-permute-start
  4.3 17.6 %collective-permute-done.6.tail_ref.refs_7_.refs_3_ = bf16[128,768]{1,0:T(8,128)(2,1)S(1)} collective-permute-done((bf16[128,768]{1,0:T(8,128)(2,1)S(1)}, bf16[128,768]{1,0:T(8,128)(2,1)S(1)}, u32[]{:S(2)}, u32[]{:S(2)}) %collective-permute-start.6) | collective-permute-done | bytes 196640 | tf_op jit(solution)/shard_map/ppermute | solution.py:371
  21.8 0.0 collective-permute-start.7
  21.8 0.0 collective-permute-done.2.ridge_ref.refs_2_
  21.8 0.5 collective-permute-start.3
  22.3 0.0 collective-permute-done.4.head_ref.refs_6_.refs_2_
  22.3 0.1 collective-permute-start.10
  22.4 0.9 %collective-permute-done.7.tail_twin_ref = bf16[128,768]{1,0:T(8,128)(2,1)S(1)} collective-permute-done((bf16[128,768]{1,0:T(8,128)(2,1)S(1)}, bf16[128,768]{1,0:T(8,128)(2,1)S(1)}, u32[]{:S(2)}, u32[]{:S(2)}) %collective-permute-start.7) | collective-permute-done | bytes 196640 | tf_op jit(solution)/shard_map/ppermute | solution.py:371
  23.3 0.1 collective-permute-start.5
  23.4 0.0 collective-permute-done.1.side_ref.refs_5_.refs_3_
  23.4 0.4 collective-permute-start.12
  23.8 1.5 %collective-permute-done.10.refs_10_.refs_4_.refs_6_ = bf16[392,768]{1,0:T(8,128)(2,1)S(1)} collective-permute-done((bf16[392,768]{1,0:T(8,128)(2,1)S(1)}, bf16[392,768]{1,0:T(8,128)(2,1)S(1)}, u32[]{:S(2)}, u32[]{:S(2)}) %collective-permute-start.10) | collective-permute-done | bytes 602144 | tf_op jit(solution)/shard_map/ppermute | solution.py:371
  25.3 0.2 collective-permute-start.11
  25.5 0.9 %collective-permute-done.12.refs_5_.refs_7_ = bf16[128,768]{1,0:T(8,128)(2,1)S(1)} collective-permute-done((bf16[128,768]{1,0:T(8,128)(2,1)S(1)}, bf16[128,768]{1,0:T(8,128)(2,1)S(1)}, u32[]{:S(2)}, u32[]{:S(2)}) %collective-permute-start.12) | collective-permute-done | bytes 196640 | tf_op jit(solution)/shard_map/ppermute | solution.py:371
  26.4 16.0 %collective-permute-start.9 = (bf16[264,768]{1,0:T(8,128)(2,1)S(1)}, bf16[264,768]{1,0:T(8,128)(2,1)S(1)}, u32[]{:S(2)}, u32[]{:S(2)}) collective-permute-start(bf16[264,768]{1,0:T(8,128)(2,1)S(1)} %slice.9), channel_id=1, source_target_pairs={{0,4},{1,5},{2,6},{3,7},{4,0},{5,1},{6,2},{7,3},{8,12},{9,13},{10,... | collective-permute-start | bytes 1216520 | tf_op jit(solution)/shard_map/ppermute | solution.py:371
  42.4 0.0 collective-permute-done.twin_ref
  42.5 0.6 collective-permute-start.8
  43.1 0.6 shard_map.28.own_ref
  43.7 0.0 collective-permute-done.5.head_twin_ref
  43.7 0.1 collective-permute-start.13
  43.8 0.0 collective-permute-done.3.ridge_twin_ref.refs_3_
  43.8 2.4 %shard_map.29 = (f32[1,512]{1,0:T(1,128)S(1)}, f32[1,512]{1,0:T(1,128)S(1)}, f32[1,512]{1,0:T(1,128)S(1)}) custom-call(f32[1,512]{1,0:T(1,128)S(1)} %shard_map.28.own_ref, bf16[520,768]{1,0:T(8,128)(2,1)S(1)} %get-tuple-element.23.mine_ref.refs_4_.refs_2_, bf16[520,768]{1,0:T(8,128)(2,1)S(1)} %collective-permute-done.twin_ref, ...), custom_call_target="tpu_custom_call" | custom-call | flops 3221225472 | bytes 5593088 | tf_op jit(solution)/shard_map/pallas_call | solution.py:326
  46.2 6.3 %collective-permute-done.8.refs_0_.refs_8_.refs_4_ = bf16[256,768]{1,0:T(8,128)(2,1)S(1)} collective-permute-done((bf16[256,768]{1,0:T(8,128)(2,1)S(1)}, bf16[256,768]{1,0:T(8,128)(2,1)S(1)}, u32[]{:S(2)}, u32[]{:S(2)}) %collective-permute-start.8) | collective-permute-done | bytes 393248 | tf_op jit(solution)/shard_map/ppermute | solution.py:371
  52.5 0.0 collective-permute-done.9.refs_1_.refs_9_.refs_5_
  52.5 0.0 collective-permute-done.11.refs_4_.refs_6_.refs_8_
  52.5 0.0 collective-permute-done.13.refs_7_.refs_9_
  52.6 0.6 collective-permute-start.14
  53.2 1.3 %collective-permute-start.15 = (f32[1,512]{1,0:T(1,128)S(1)}, f32[1,512]{1,0:T(1,128)S(1)}, u32[]{:S(2)}, u32[]{:S(2)}) collective-permute-start(f32[1,512]{1,0:T(1,128)S(1)} %get-tuple-element.39), channel_id=1, source_target_pairs={{8,12},{9,13},{10,14},{11,15},{24,28},{25,29},{26,30},{27,31}} | collective-permute-start | bytes 6152 | tf_op jit(solution)/shard_map/ppermute | solution.py:371
  54.5 1.3 %collective-permute-start.16 = (f32[1,512]{1,0:T(1,128)S(1)}, f32[1,512]{1,0:T(1,128)S(1)}, u32[]{:S(2)}, u32[]{:S(2)}) collective-permute-start(f32[1,512]{1,0:T(1,128)S(1)} %get-tuple-element.40), channel_id=1, source_target_pairs={{8,14},{9,15},{10,12},{11,13},{24,30},{25,31},{26,28},{27,29}} | collective-permute-start | bytes 6152 | tf_op jit(solution)/shard_map/ppermute | solution.py:371
  55.8 0.4 collective-permute-done.14
  56.2 5.9 %collective-permute-done.15 = f32[1,512]{1,0:T(1,128)S(1)} collective-permute-done((f32[1,512]{1,0:T(1,128)S(1)}, f32[1,512]{1,0:T(1,128)S(1)}, u32[]{:S(2)}, u32[]{:S(2)}) %collective-permute-start.15) | collective-permute-done | bytes 2080 | tf_op jit(solution)/shard_map/ppermute | solution.py:371
  62.2 2.2 %collective-permute-done.16 = f32[1,512]{1,0:T(1,128)S(1)} collective-permute-done((f32[1,512]{1,0:T(1,128)S(1)}, f32[1,512]{1,0:T(1,128)S(1)}, u32[]{:S(2)}, u32[]{:S(2)}) %collective-permute-start.16) | collective-permute-done | bytes 2080 | tf_op jit(solution)/shard_map/ppermute | solution.py:371
  64.4 0.6 fusion
  (8 shorter events, 0.1 us)
Async XLA Ops:
  1.5 20.3 %collective-permute-start.2 = (bf16[520,768]{1,0:T(8,128)(2,1)S(1)}, bf16[520,768]{1,0:T(8,128)(2,1)S(1)}, u32[]{:S(2)}, u32[]{:S(2)}) collective-permute-start(bf16[520,768]{1,0:T(8,128)(2,1)S(1)} %get-tuple-element.23.mine_ref.refs_4_.refs_2_), channel_id=1, source_target_pairs={{0,1},{1,0},{2,3},{3,2},{4,8},{5,9},{6,10},{7,11},{8,4},{9,5},{10,... | collective-permute-start | bytes 2396168 | tf_op jit(solution)/shard_map/ppermute | solution.py:371
  1.6 20.7 %collective-permute-start.4 = (bf16[392,768]{1,0:T(8,128)(2,1)S(1)}, bf16[392,768]{1,0:T(8,128)(2,1)S(1)}, u32[]{:S(2)}, u32[]{:S(2)}) collective-permute-start(bf16[392,768]{1,0:T(8,128)(2,1)S(1)} %get-tuple-element.24), channel_id=1, source_target_pairs={{0,4},{1,5},{2,6},{3,7},{4,0},{5,1},{6,2},{7,3},{8,12},{9,13},{10,... | collective-permute-start | bytes 1806344 | tf_op jit(solution)/shard_map/ppermute | solution.py:371
  2.5 20.9 %collective-permute-start.1 = (bf16[520,768]{1,0:T(8,128)(2,1)S(1)}, bf16[520,768]{1,0:T(8,128)(2,1)S(1)}, u32[]{:S(2)}, u32[]{:S(2)}) collective-permute-start(bf16[520,768]{1,0:T(8,128)(2,1)S(1)} %get-tuple-element.23.mine_ref.refs_4_.refs_2_), channel_id=1, source_target_pairs={{0,2},{1,3},{2,0},{3,1},{4,6},{5,7},{6,4},{7,5},{8,10},{9,11},{10,... | collective-permute-start | bytes 2396168 | tf_op jit(solution)/shard_map/ppermute | solution.py:371
  3.0 18.8 %collective-permute-start.6 = (bf16[128,768]{1,0:T(8,128)(2,1)S(1)}, bf16[128,768]{1,0:T(8,128)(2,1)S(1)}, u32[]{:S(2)}, u32[]{:S(2)}) collective-permute-start(bf16[128,768]{1,0:T(8,128)(2,1)S(1)} %get-tuple-element.25), channel_id=1, source_target_pairs={{0,4},{1,5},{2,6},{3,7},{4,0},{5,1},{6,2},{7,3},{8,12},{9,13},{10,... | collective-permute-start | bytes 589832 | tf_op jit(solution)/shard_map/ppermute | solution.py:371
  4.2 38.2 %collective-permute-start = (bf16[520,768]{1,0:T(8,128)(2,1)S(1)}, bf16[520,768]{1,0:T(8,128)(2,1)S(1)}, u32[]{:S(2)}, u32[]{:S(2)}) collective-permute-start(bf16[520,768]{1,0:T(8,128)(2,1)S(1)} %get-tuple-element.23.mine_ref.refs_4_.refs_2_), channel_id=1, source_target_pairs={{0,1},{1,0},{2,3},{3,2},{4,5},{5,4},{6,7},{7,6},{8,9},{9,8},{10,11... | collective-permute-start | bytes 2396168 | tf_op jit(solution)/shard_map/ppermute | solution.py:371
  21.8 1.4 %collective-permute-start.7 = (bf16[128,768]{1,0:T(8,128)(2,1)S(1)}, bf16[128,768]{1,0:T(8,128)(2,1)S(1)}, u32[]{:S(2)}, u32[]{:S(2)}) collective-permute-start(bf16[128,768]{1,0:T(8,128)(2,1)S(1)} %collective-permute-done.6.tail_ref.refs_7_.refs_3_), channel_id=1, source_target_pairs={{0,1},{1,0},{2,3},{3,2},{4,5},{5,4},{6,7},{7,6},{8,9},{9,8},{10,11... | collective-permute-start | bytes 589832 | tf_op jit(solution)/shard_map/ppermute | solution.py:371
  21.8 21.9 %collective-permute-start.3 = (bf16[520,768]{1,0:T(8,128)(2,1)S(1)}, bf16[520,768]{1,0:T(8,128)(2,1)S(1)}, u32[]{:S(2)}, u32[]{:S(2)}) collective-permute-start(bf16[520,768]{1,0:T(8,128)(2,1)S(1)} %collective-permute-done.2.ridge_ref.refs_2_), channel_id=1, source_target_pairs={{0,1},{1,0},{2,3},{3,2},{4,5},{5,4},{6,7},{7,6},{8,9},{9,8},{10,11... | collective-permute-start | bytes 2396168 | tf_op jit(solution)/shard_map/ppermute | solution.py:371
  22.3 2.9 %collective-permute-start.10 = (bf16[392,768]{1,0:T(8,128)(2,1)S(1)}, bf16[392,768]{1,0:T(8,128)(2,1)S(1)}, u32[]{:S(2)}, u32[]{:S(2)}) collective-permute-start(bf16[392,768]{1,0:T(8,128)(2,1)S(1)} %collective-permute-done.4.head_ref.refs_6_.refs_2_), channel_id=1, source_target_pairs={{0,1},{1,0},{2,3},{3,2},{4,8},{5,9},{6,10},{7,11},{8,4},{9,5},{10,... | collective-permute-start | bytes 1806344 | tf_op jit(solution)/shard_map/ppermute | solution.py:371
  23.3 20.4 %collective-permute-start.5 = (bf16[392,768]{1,0:T(8,128)(2,1)S(1)}, bf16[392,768]{1,0:T(8,128)(2,1)S(1)}, u32[]{:S(2)}, u32[]{:S(2)}) collective-permute-start(bf16[392,768]{1,0:T(8,128)(2,1)S(1)} %collective-permute-done.4.head_ref.refs_6_.refs_2_), channel_id=1, source_target_pairs={{0,1},{1,0},{2,3},{3,2},{4,5},{5,4},{6,7},{7,6},{8,9},{9,8},{10,11... | collective-permute-start | bytes 1806344 | tf_op jit(solution)/shard_map/ppermute | solution.py:371
  23.4 3.0 %collective-permute-start.12 = (bf16[128,768]{1,0:T(8,128)(2,1)S(1)}, bf16[128,768]{1,0:T(8,128)(2,1)S(1)}, u32[]{:S(2)}, u32[]{:S(2)}) collective-permute-start(bf16[128,768]{1,0:T(8,128)(2,1)S(1)} %collective-permute-done.6.tail_ref.refs_7_.refs_3_), channel_id=1, source_target_pairs={{0,1},{1,0},{2,3},{3,2},{4,8},{5,9},{6,10},{7,11},{8,4},{9,5},{10,... | collective-permute-start | bytes 589832 | tf_op jit(solution)/shard_map/ppermute | solution.py:371
  25.3 27.2 %collective-permute-start.11 = (bf16[392,768]{1,0:T(8,128)(2,1)S(1)}, bf16[392,768]{1,0:T(8,128)(2,1)S(1)}, u32[]{:S(2)}, u32[]{:S(2)}) collective-permute-start(bf16[392,768]{1,0:T(8,128)(2,1)S(1)} %collective-permute-done.10.refs_10_.refs_4_.refs_6_), channel_id=1, source_target_pairs={{0,1},{1,0},{2,3},{3,2},{4,5},{5,4},{6,7},{7,6},{8,9},{9,8},{10,11... | collective-permute-start | bytes 1806344 | tf_op jit(solution)/shard_map/ppermute | solution.py:371
  26.4 26.1 %collective-permute-start.9 = (bf16[264,768]{1,0:T(8,128)(2,1)S(1)}, bf16[264,768]{1,0:T(8,128)(2,1)S(1)}, u32[]{:S(2)}, u32[]{:S(2)}) collective-permute-start(bf16[264,768]{1,0:T(8,128)(2,1)S(1)} %slice.9), channel_id=1, source_target_pairs={{0,4},{1,5},{2,6},{3,7},{4,0},{5,1},{6,2},{7,3},{8,12},{9,13},{10,... | collective-permute-start | bytes 1216520 | tf_op jit(solution)/shard_map/ppermute | solution.py:371
  42.5 10.0 %collective-permute-start.8 = (bf16[256,768]{1,0:T(8,128)(2,1)S(1)}, bf16[256,768]{1,0:T(8,128)(2,1)S(1)}, u32[]{:S(2)}, u32[]{:S(2)}) collective-permute-start(bf16[256,768]{1,0:T(8,128)(2,1)S(1)} %slice.8), channel_id=1, source_target_pairs={{0,2},{1,3},{2,0},{3,1},{4,6},{5,7},{6,4},{7,5},{8,10},{9,11},{10,... | collective-permute-start | bytes 1179656 | tf_op jit(solution)/shard_map/ppermute | solution.py:371
  43.7 8.9 %collective-permute-start.13 = (bf16[128,768]{1,0:T(8,128)(2,1)S(1)}, bf16[128,768]{1,0:T(8,128)(2,1)S(1)}, u32[]{:S(2)}, u32[]{:S(2)}) collective-permute-start(bf16[128,768]{1,0:T(8,128)(2,1)S(1)} %collective-permute-done.12.refs_5_.refs_7_), channel_id=1, source_target_pairs={{0,1},{1,0},{2,3},{3,2},{4,5},{5,4},{6,7},{7,6},{8,9},{9,8},{10,11... | collective-permute-start | bytes 589832 | tf_op jit(solution)/shard_map/ppermute | solution.py:371
  52.6 3.7 %collective-permute-start.14 = (f32[1,512]{1,0:T(1,128)S(1)}, f32[1,512]{1,0:T(1,128)S(1)}, u32[]{:S(2)}, u32[]{:S(2)}) collective-permute-start(f32[1,512]{1,0:T(1,128)S(1)} %get-tuple-element.34), channel_id=1, source_target_pairs={{0,2},{1,3},{2,0},{3,1},{4,6},{5,7},{6,4},{7,5},{8,10},{9,11},{10,... | collective-permute-start | bytes 6152 | tf_op jit(solution)/shard_map/ppermute | solution.py:371
  53.2 9.0 %collective-permute-start.15 = (f32[1,512]{1,0:T(1,128)S(1)}, f32[1,512]{1,0:T(1,128)S(1)}, u32[]{:S(2)}, u32[]{:S(2)}) collective-permute-start(f32[1,512]{1,0:T(1,128)S(1)} %get-tuple-element.39), channel_id=1, source_target_pairs={{8,12},{9,13},{10,14},{11,15},{24,28},{25,29},{26,30},{27,31}} | collective-permute-start | bytes 6152 | tf_op jit(solution)/shard_map/ppermute | solution.py:371
  54.5 10.0 %collective-permute-start.16 = (f32[1,512]{1,0:T(1,128)S(1)}, f32[1,512]{1,0:T(1,128)S(1)}, u32[]{:S(2)}, u32[]{:S(2)}) collective-permute-start(f32[1,512]{1,0:T(1,128)S(1)} %get-tuple-element.40), channel_id=1, source_target_pairs={{8,14},{9,15},{10,12},{11,13},{24,30},{25,31},{26,28},{27,29}} | collective-permute-start | bytes 6152 | tf_op jit(solution)/shard_map/ppermute | solution.py:371

commit v3 on v2

--- a/solution.py
+++ b/solution.py
@@ -128,7 +128,15 @@
 PARAMS = pltpu.CompilerParams(vmem_limit_bytes=16 * 1024 * 1024)
 
 
-def tag_kernel(rows_hbm, label_hbm, whole_ref, head_ref, tail_ref, rows_ref, label_ref, done):
+def unit_of(rows):
+    values = rows.astype(jnp.float32)
+    inverse = lax.rsqrt(jnp.mean(values * values, axis=1, keepdims=True) + 1e-06)
+    return (values * inverse * (1.0 / math.sqrt(rows.shape[1]))).astype(jnp.bfloat16)
+
+
+def tag_kernel(
+    rows_hbm, label_hbm, whole_ref, head_ref, tail_ref, mark_ref, rows_ref, label_ref, done
+):
     rows, width = rows_ref.shape
     cut = head_ref.shape[0] - TAG_ROWS
     spans = [(low, low + rows // 4) for low in range(0, rows, rows // 4)]
@@ -142,15 +150,14 @@
     labels.wait()
     codes = (label_ref[...] + 1).astype(jnp.float32)
     line = jnp.broadcast_to(codes, (TAG_ROWS, rows)).astype(jnp.bfloat16)
+    mark_ref[...] = line
     for ref, count in ((whole_ref, rows), (head_ref, cut)):
         ref[count:, :rows] = line
         if rows < width:
             ref[count:, rows:] = jnp.zeros((TAG_ROWS, width - rows), jnp.bfloat16)
     for copy, (low, high) in zip(copies, spans):
         copy.wait()
-        values = rows_ref[low:high, :].astype(jnp.float32)
-        inverse = lax.rsqrt(jnp.mean(values * values, axis=1, keepdims=True) + 1e-06)
-        unit = (values * inverse * (1.0 / math.sqrt(width))).astype(jnp.bfloat16)
+        unit = unit_of(rows_ref[low:high, :])
         whole_ref[low:high, :] = unit
         if high <= cut:
             head_ref[low:high, :] = unit
@@ -161,8 +168,8 @@
 def tagged(embeddings, labels):
     rows, width = embeddings.shape
     labels = labels.reshape(1, rows)
-    cut = rows * 3 // 4
-    shapes = ((rows + TAG_ROWS, width), (cut + TAG_ROWS, width), (rows - cut, width))
+    cut = rows // 2
+    shapes = ((rows + TAG_ROWS, width), (cut + TAG_ROWS, width), (rows - cut, width), (TAG_ROWS, rows))
     return pl.pallas_call(
         tag_kernel,
         out_shape=[pltpu.VMEM(shape, jnp.bfloat16) for shape in shapes],
@@ -175,6 +182,25 @@
         compiler_params=PARAMS,
         name="tagged",
     )(*[pltpu.with_memory_space_constraint(value, pltpu.HBM) for value in (embeddings, labels)])
+
+
+def ridge_kernel(rows_ref, mark_ref, out_ref):
+    rows, width = rows_ref.shape
+    out_ref[:rows, :] = unit_of(rows_ref[...])
+    out_ref[rows:, :rows] = mark_ref[...]
+    if rows < width:
+        out_ref[rows:, rows:] = jnp.zeros((TAG_ROWS, width - rows), jnp.bfloat16)
+
+
+def arrived(rows, marks):
+    count, width = rows.shape
+    return pl.pallas_call(
+        ridge_kernel,
+        out_shape=pltpu.VMEM((count + TAG_ROWS, width), jnp.bfloat16),
+        in_specs=[pl.BlockSpec(memory_space=pltpu.VMEM)] * 2,
+        compiler_params=PARAMS,
+        name="arrived",
+    )(*[pltpu.with_memory_space_constraint(value, pltpu.VMEM) for value in (rows, marks)])
 
 
 class Block:
@@ -351,7 +377,6 @@
 
 def layered(embeddings, cluster_id):
     rows = embeddings.shape[0]
-    mine, head, tail = tagged(embeddings, cluster_id[:, 0])
     spots = [(z, x, c) for z in range(LAYERS) for x in range(2) for c in range(2)]
 
     def hops(move):
@@ -370,11 +395,13 @@
     def sent(value, pairs):
         return lax.ppermute(value, "wide", pairs)
 
+    raw_ridge = sent(embeddings, inner)
+    mine, head, tail, marks = tagged(embeddings, cluster_id[:, 0])
     near_head = sent(head, outer)
-    ridge = sent(mine, inner)
     side = sent(mine, across)
     near_tail = sent(tail, outer)
     twin = sent(mine, beside)
+    ridge = arrived(raw_ridge, sent(marks, inner))
     deep_head = sent(near_head, inner)
     upper = sent(near_head[: rows // 2], across)
     lower = sent(side[rows // 2 :], outer)
@@ -387,20 +414,22 @@
 
     square = rows * rows
     (own,) = scored(own_kernel, [rows], 2 * square, mine, twin)
-    first, second, third = scored(
+    best = scored(
         here_kernel, [rows] * 3, 8 * square,
         own, mine, twin, side, ridge, ridge_twin, near_head, near_head_twin, near_tail, near_tail_twin,
     )
     flat = [("whole", mine), ("whole", side)]
     steep = [("split", near_head, near_tail), ("halves", upper, lower)]
-    (fourth,) = deepened(None, steep[1:], [("whole", ridge), ("whole", ridge_twin)])
-    best = deepened([first, second, third, fourth], flat + steep, [("whole", deep_head)])
-    other = [("whole", deep_head_twin)]
-    best_steep = deepened(best[2:], steep, other)
-    best_flat = deepened(best[:2], flat, other)
-    ends = [("end", deep_head, deep_tail), ("end", deep_head_twin, deep_tail_twin)]
-    third, fourth = deepened(best_steep, steep, ends)
-    first, second = deepened(best_flat, flat, ends)
+    deep, deep_twin = ("whole", deep_head), ("whole", deep_head_twin)
+    third, fourth = ("end", deep_head, deep_tail), ("end", deep_head_twin, deep_tail_twin)
+    best = deepened(best, flat + steep[:1], [deep])
+    best = deepened(best, flat + steep[:1], [deep_twin])
+    keys = [("whole", ridge), ("whole", ridge_twin), deep, deep_twin]
+    best_flat, best_steep = best[:2], best[2:] + deepened(None, steep[1:], keys)
+    best_flat = deepened(best_flat, flat, [third])
+    best_steep = deepened(best_steep, steep, [third])
+    first, second = deepened(best_flat, flat, [fourth])
+    third, fourth = deepened(best_steep, steep, [fourth])
     from_below = sent(third, lift)
     from_slant = sent(fourth, tilt)
     from_side = sent(second, across)

time: 65.2 us -> 62.1 us (0.952)
  the two profiles are of different devices: /device:TPU:26 before, /device:TPU:28 now
where the time goes in v3:
time: 62.1 us; the launch traced here: 61.9 us
  starting transfers between devices  33.2 us (53%)
  waiting for transfers between devices  22.5 us (36%)
  Pallas kernels  5.44 us (9%)
    ppermute x18, starting transfers between devices, sent(): return lax.ppermute(value, 'wide', pairs)  33.2 us
    ppermute x18, waiting for transfers between devices, sent(): return lax.ppermute(value, 'wide', pairs)  22.5 us
    pallas_call x9, Pallas kernels, scored(): pl.pallas_call(body, out_shape=[pltpu.VMEM((1, count), jnp.float32) for c...  3.6 us
    pallas_call x1, Pallas kernels, tagged(): pl.pallas_call(tag_kernel, out_shape=[pltpu.VMEM(shape, jnp.bfloat16) for...  1.53 us
  transfers between devices with their start and end apart: 18, of which 6 were waited for; matrix products, arithmetic and copies ran while one was open for 0% of the time, Pallas kernels for 9%

profile of v3, /device:TPU:28, one launch (start us, length us, event | category | flops | bytes accessed | tf_op | source)
XLA Modules:
  0.0 61.9 jit_solution(10423283083924996587)
XLA Ops:
  0.0 0.0 collective-permute-start.2
  0.0 1.5 %tagged.1 = (bf16[520,768]{1,0:T(8,128)(2,1)S(1)}, bf16[264,768]{1,0:T(8,128)(2,1)S(1)}, bf16[256,768]{1,0:T(8,128)(2,1)S(1)}, bf16[8,512]{1,0:T(8,128)(2,1)S(1)}) custom-call(bf16[512,768]{1,0:T(8,128)(2,1)} %rows_hbm.1, s32[1,512]{1,0:T(1,128)} %bitcast.2), custom_call_target="tpu_custom_call" | custom-call | tf_op jit(solution)/shard_map/tagged/pallas_call | solution.py:173
  1.5 0.6 collective-permute-start
  2.1 1.5 %collective-permute-start.1 = (bf16[520,768]{1,0:T(8,128)(2,1)S(1)}, bf16[520,768]{1,0:T(8,128)(2,1)S(1)}, u32[]{:S(2)}, u32[]{:S(2)}) collective-permute-start(bf16[520,768]{1,0:T(8,128)(2,1)S(1)} %get-tuple-element.26.mine_ref.refs_3_.refs_2_), channel_id=1, source_target_pairs={{0,2},{1,3},{2,0},{3,1},{4,6},{5,7},{6,4},{7,5},{8,10},{9,11},{10,... | collective-permute-start | bytes 2396168 | tf_op jit(solution)/shard_map/ppermute | solution.py:396
  3.6 0.5 collective-permute-start.5
  4.1 0.0 collective-permute-start.3
  4.1 1.2 %collective-permute-done.3.mark_ref = bf16[8,512]{1,0:T(8,128)(2,1)S(1)} collective-permute-done((bf16[8,512]{1,0:T(8,128)(2,1)S(1)}, bf16[8,512]{1,0:T(8,128)(2,1)S(1)}, u32[]{:S(2)}, u32[]{:S(2)}) %collective-permute-start.3) | collective-permute-done | bytes 8224 | tf_op jit(solution)/shard_map/ppermute | solution.py:396
  5.3 14.8 %collective-permute-start.7 = (bf16[256,768]{1,0:T(8,128)(2,1)S(1)}, bf16[256,768]{1,0:T(8,128)(2,1)S(1)}, u32[]{:S(2)}, u32[]{:S(2)}) collective-permute-start(bf16[256,768]{1,0:T(8,128)(2,1)S(1)} %get-tuple-element.29), channel_id=1, source_target_pairs={{0,4},{1,5},{2,6},{3,7},{4,0},{5,1},{6,2},{7,3},{8,12},{9,13},{10,... | collective-permute-start | bytes 1179656 | tf_op jit(solution)/shard_map/ppermute | solution.py:396
  20.1 0.0 collective-permute-done.2.rows_ref
  20.1 0.3 arrived.1.ridge_ref.refs_2_
  20.4 0.1 collective-permute-start.4
  20.5 0.0 collective-permute-done.5.head_ref.refs_5_.refs_2_
  20.5 0.5 collective-permute-start.9
  21.0 7.4 %collective-permute-done.7.tail_ref.refs_6_.refs_3_ = bf16[256,768]{1,0:T(8,128)(2,1)S(1)} collective-permute-done((bf16[256,768]{1,0:T(8,128)(2,1)S(1)}, bf16[256,768]{1,0:T(8,128)(2,1)S(1)}, u32[]{:S(2)}, u32[]{:S(2)}) %collective-permute-start.7) | collective-permute-done | bytes 393248 | tf_op jit(solution)/shard_map/ppermute | solution.py:396
  28.4 0.0 collective-permute-start.6
  28.4 0.0 collective-permute-done.twin_ref
  28.4 0.5 collective-permute-start.8
  28.9 0.0 collective-permute-done.1.side_ref.refs_4_.refs_3_
  28.9 0.1 collective-permute-start.11
  29.0 0.0 collective-permute-done.9.refs_7_.refs_4_.refs_6_
  29.0 0.5 collective-permute-start.10
  29.5 0.6 shard_map.28.own_ref
  30.2 0.5 collective-permute-done.8.tail_twin_ref
  30.7 1.5 %collective-permute-start.14 = (bf16[256,768]{1,0:T(8,128)(2,1)S(1)}, bf16[256,768]{1,0:T(8,128)(2,1)S(1)}, u32[]{:S(2)}, u32[]{:S(2)}) collective-permute-start(bf16[256,768]{1,0:T(8,128)(2,1)S(1)} %slice.8), channel_id=1, source_target_pairs={{0,2},{1,3},{2,0},{3,1},{4,6},{5,7},{6,4},{7,5},{8,10},{9,11},{10,... | collective-permute-start | bytes 1179656 | tf_op jit(solution)/shard_map/ppermute | solution.py:396
  32.2 0.0 collective-permute-done.11.refs_5_.refs_7_
  32.2 0.0 collective-permute-start.12
  32.2 0.0 collective-permute-done.6.head_twin_ref
  32.2 9.6 %collective-permute-start.15 = (bf16[264,768]{1,0:T(8,128)(2,1)S(1)}, bf16[264,768]{1,0:T(8,128)(2,1)S(1)}, u32[]{:S(2)}, u32[]{:S(2)}) collective-permute-start(bf16[264,768]{1,0:T(8,128)(2,1)S(1)} %slice.9), channel_id=1, source_target_pairs={{0,4},{1,5},{2,6},{3,7},{4,0},{5,1},{6,2},{7,3},{8,12},{9,13},{10,... | collective-permute-start | bytes 1216520 | tf_op jit(solution)/shard_map/ppermute | solution.py:396
  41.7 0.0 collective-permute-done.4.ridge_twin_ref.refs_3_
  41.7 2.9 %shard_map.29 = (f32[1,512]{1,0:T(1,128)S(1)}, f32[1,512]{1,0:T(1,128)S(1)}, f32[1,512]{1,0:T(1,128)S(1)}) custom-call(f32[1,512]{1,0:T(1,128)S(1)} %shard_map.28.own_ref, bf16[520,768]{1,0:T(8,128)(2,1)S(1)} %get-tuple-element.26.mine_ref.refs_3_.refs_2_, bf16[520,768]{1,0:T(8,128)(2,1)S(1)} %collective-permute-done.twin_ref, ...), custom_call_target="tpu_custom_call" | custom-call | flops 3221225472 | bytes 5593088 | tf_op jit(solution)/shard_map/pallas_call | solution.py:352
  44.7 0.0 collective-permute-done.10.refs_7_.refs_4_.refs_5_.refs_6_
  44.7 0.0 collective-permute-done.12.refs_5_.refs_7_
  44.8 0.5 collective-permute-start.13
  45.3 0.0 collective-permute-done.14.refs_0_.refs_4_
  45.3 6.5 %collective-permute-done.15.refs_1_.refs_5_ = bf16[264,768]{1,0:T(8,128)(2,1)S(1)} collective-permute-done((bf16[264,768]{1,0:T(8,128)(2,1)S(1)}, bf16[264,768]{1,0:T(8,128)(2,1)S(1)}, u32[]{:S(2)}, u32[]{:S(2)}) %collective-permute-start.15) | collective-permute-done | bytes 405536 | tf_op jit(solution)/shard_map/ppermute | solution.py:396
  51.8 1.3 %collective-permute-start.16 = (f32[1,512]{1,0:T(1,128)S(1)}, f32[1,512]{1,0:T(1,128)S(1)}, u32[]{:S(2)}, u32[]{:S(2)}) collective-permute-start(f32[1,512]{1,0:T(1,128)S(1)} %get-tuple-element.45), channel_id=1, source_target_pairs={{8,12},{9,13},{10,14},{11,15},{24,28},{25,29},{26,30},{27,31}} | collective-permute-start | bytes 6152 | tf_op jit(solution)/shard_map/ppermute | solution.py:396
  53.1 1.3 %collective-permute-start.17 = (f32[1,512]{1,0:T(1,128)S(1)}, f32[1,512]{1,0:T(1,128)S(1)}, u32[]{:S(2)}, u32[]{:S(2)}) collective-permute-start(f32[1,512]{1,0:T(1,128)S(1)} %get-tuple-element.46), channel_id=1, source_target_pairs={{8,14},{9,15},{10,12},{11,13},{24,30},{25,31},{26,28},{27,29}} | collective-permute-start | bytes 6152 | tf_op jit(solution)/shard_map/ppermute | solution.py:396
  54.4 0.0 collective-permute-done.13
  54.4 4.7 %collective-permute-done.16 = f32[1,512]{1,0:T(1,128)S(1)} collective-permute-done((f32[1,512]{1,0:T(1,128)S(1)}, f32[1,512]{1,0:T(1,128)S(1)}, u32[]{:S(2)}, u32[]{:S(2)}) %collective-permute-start.16) | collective-permute-done | bytes 2080 | tf_op jit(solution)/shard_map/ppermute | solution.py:396
  59.1 2.2 %collective-permute-done.17 = f32[1,512]{1,0:T(1,128)S(1)} collective-permute-done((f32[1,512]{1,0:T(1,128)S(1)}, f32[1,512]{1,0:T(1,128)S(1)}, u32[]{:S(2)}, u32[]{:S(2)}) %collective-permute-start.17) | collective-permute-done | bytes 2080 | tf_op jit(solution)/shard_map/ppermute | solution.py:396
  61.4 0.6 fusion
  (9 shorter events, 0.2 us)
Async XLA Ops:
  0.0 20.1 %collective-permute-start.2 = (bf16[512,768]{1,0:T(8,128)(2,1)}, bf16[512,768]{1,0:T(8,128)(2,1)S(1)}, u32[]{:S(2)}, u32[]{:S(2)}) collective-permute-start(bf16[512,768]{1,0:T(8,128)(2,1)} %rows_hbm.1), channel_id=1, source_target_pairs={{0,1},{1,0},{2,3},{3,2},{4,8},{5,9},{6,10},{7,11},{8,4},{9,5},{10,... | collective-permute-start | bytes 2359304 | tf_op jit(solution)/shard_map/ppermute | solution.py:396
  1.5 26.8 %collective-permute-start = (bf16[520,768]{1,0:T(8,128)(2,1)S(1)}, bf16[520,768]{1,0:T(8,128)(2,1)S(1)}, u32[]{:S(2)}, u32[]{:S(2)}) collective-permute-start(bf16[520,768]{1,0:T(8,128)(2,1)S(1)} %get-tuple-element.26.mine_ref.refs_3_.refs_2_), channel_id=1, source_target_pairs={{0,1},{1,0},{2,3},{3,2},{4,5},{5,4},{6,7},{7,6},{8,9},{9,8},{10,11... | collective-permute-start | bytes 2396168 | tf_op jit(solution)/shard_map/ppermute | solution.py:396
  2.1 26.8 %collective-permute-start.1 = (bf16[520,768]{1,0:T(8,128)(2,1)S(1)}, bf16[520,768]{1,0:T(8,128)(2,1)S(1)}, u32[]{:S(2)}, u32[]{:S(2)}) collective-permute-start(bf16[520,768]{1,0:T(8,128)(2,1)S(1)} %get-tuple-element.26.mine_ref.refs_3_.refs_2_), channel_id=1, source_target_pairs={{0,2},{1,3},{2,0},{3,1},{4,6},{5,7},{6,4},{7,5},{8,10},{9,11},{10,... | collective-permute-start | bytes 2396168 | tf_op jit(solution)/shard_map/ppermute | solution.py:396
  3.6 16.9 %collective-permute-start.5 = (bf16[264,768]{1,0:T(8,128)(2,1)S(1)}, bf16[264,768]{1,0:T(8,128)(2,1)S(1)}, u32[]{:S(2)}, u32[]{:S(2)}) collective-permute-start(bf16[264,768]{1,0:T(8,128)(2,1)S(1)} %get-tuple-element.28), channel_id=1, source_target_pairs={{0,4},{1,5},{2,6},{3,7},{4,0},{5,1},{6,2},{7,3},{8,12},{9,13},{10,... | collective-permute-start | bytes 1216520 | tf_op jit(solution)/shard_map/ppermute | solution.py:396
  4.1 1.2 %collective-permute-start.3 = (bf16[8,512]{1,0:T(8,128)(2,1)S(1)}, bf16[8,512]{1,0:T(8,128)(2,1)S(1)}, u32[]{:S(2)}, u32[]{:S(2)}) collective-permute-start(bf16[8,512]{1,0:T(8,128)(2,1)S(1)} %get-tuple-element.27), channel_id=1, source_target_pairs={{0,1},{1,0},{2,3},{3,2},{4,8},{5,9},{6,10},{7,11},{8,4},{9,5},{10,... | collective-permute-start | bytes 24584 | tf_op jit(solution)/shard_map/ppermute | solution.py:396
  5.3 23.1 %collective-permute-start.7 = (bf16[256,768]{1,0:T(8,128)(2,1)S(1)}, bf16[256,768]{1,0:T(8,128)(2,1)S(1)}, u32[]{:S(2)}, u32[]{:S(2)}) collective-permute-start(bf16[256,768]{1,0:T(8,128)(2,1)S(1)} %get-tuple-element.29), channel_id=1, source_target_pairs={{0,4},{1,5},{2,6},{3,7},{4,0},{5,1},{6,2},{7,3},{8,12},{9,13},{10,... | collective-permute-start | bytes 1179656 | tf_op jit(solution)/shard_map/ppermute | solution.py:396
  20.4 21.3 %collective-permute-start.4 = (bf16[520,768]{1,0:T(8,128)(2,1)S(1)}, bf16[520,768]{1,0:T(8,128)(2,1)S(1)}, u32[]{:S(2)}, u32[]{:S(2)}) collective-permute-start(bf16[520,768]{1,0:T(8,128)(2,1)S(1)} %arrived.1.ridge_ref.refs_2_), channel_id=1, source_target_pairs={{0,1},{1,0},{2,3},{3,2},{4,5},{5,4},{6,7},{7,6},{8,9},{9,8},{10,11... | collective-permute-start | bytes 2396168 | tf_op jit(solution)/shard_map/ppermute | solution.py:396
  20.5 8.5 %collective-permute-start.9 = (bf16[264,768]{1,0:T(8,128)(2,1)S(1)}, bf16[264,768]{1,0:T(8,128)(2,1)S(1)}, u32[]{:S(2)}, u32[]{:S(2)}) collective-permute-start(bf16[264,768]{1,0:T(8,128)(2,1)S(1)} %collective-permute-done.5.head_ref.refs_5_.refs_2_), channel_id=1, source_target_pairs={{0,1},{1,0},{2,3},{3,2},{4,8},{5,9},{6,10},{7,11},{8,4},{9,5},{10,... | collective-permute-start | bytes 1216520 | tf_op jit(solution)/shard_map/ppermute | solution.py:396
  28.4 3.8 %collective-permute-start.6 = (bf16[264,768]{1,0:T(8,128)(2,1)S(1)}, bf16[264,768]{1,0:T(8,128)(2,1)S(1)}, u32[]{:S(2)}, u32[]{:S(2)}) collective-permute-start(bf16[264,768]{1,0:T(8,128)(2,1)S(1)} %collective-permute-done.5.head_ref.refs_5_.refs_2_), channel_id=1, source_target_pairs={{0,1},{1,0},{2,3},{3,2},{4,5},{5,4},{6,7},{7,6},{8,9},{9,8},{10,11... | collective-permute-start | bytes 1216520 | tf_op jit(solution)/shard_map/ppermute | solution.py:396
  28.4 2.3 %collective-permute-start.8 = (bf16[256,768]{1,0:T(8,128)(2,1)S(1)}, bf16[256,768]{1,0:T(8,128)(2,1)S(1)}, u32[]{:S(2)}, u32[]{:S(2)}) collective-permute-start(bf16[256,768]{1,0:T(8,128)(2,1)S(1)} %collective-permute-done.7.tail_ref.refs_6_.refs_3_), channel_id=1, source_target_pairs={{0,1},{1,0},{2,3},{3,2},{4,5},{5,4},{6,7},{7,6},{8,9},{9,8},{10,11... | collective-permute-start | bytes 1179656 | tf_op jit(solution)/shard_map/ppermute | solution.py:396
  28.9 3.3 %collective-permute-start.11 = (bf16[256,768]{1,0:T(8,128)(2,1)S(1)}, bf16[256,768]{1,0:T(8,128)(2,1)S(1)}, u32[]{:S(2)}, u32[]{:S(2)}) collective-permute-start(bf16[256,768]{1,0:T(8,128)(2,1)S(1)} %collective-permute-done.7.tail_ref.refs_6_.refs_3_), channel_id=1, source_target_pairs={{0,1},{1,0},{2,3},{3,2},{4,8},{5,9},{6,10},{7,11},{8,4},{9,5},{10,... | collective-permute-start | bytes 1179656 | tf_op jit(solution)/shard_map/ppermute | solution.py:396
  29.0 15.6 %collective-permute-start.10 = (bf16[264,768]{1,0:T(8,128)(2,1)S(1)}, bf16[264,768]{1,0:T(8,128)(2,1)S(1)}, u32[]{:S(2)}, u32[]{:S(2)}) collective-permute-start(bf16[264,768]{1,0:T(8,128)(2,1)S(1)} %collective-permute-done.9.refs_7_.refs_4_.refs_6_), channel_id=1, source_target_pairs={{0,1},{1,0},{2,3},{3,2},{4,5},{5,4},{6,7},{7,6},{8,9},{9,8},{10,11... | collective-permute-start | bytes 1216520 | tf_op jit(solution)/shard_map/ppermute | solution.py:396
  30.7 14.6 %collective-permute-start.14 = (bf16[256,768]{1,0:T(8,128)(2,1)S(1)}, bf16[256,768]{1,0:T(8,128)(2,1)S(1)}, u32[]{:S(2)}, u32[]{:S(2)}) collective-permute-start(bf16[256,768]{1,0:T(8,128)(2,1)S(1)} %slice.8), channel_id=1, source_target_pairs={{0,2},{1,3},{2,0},{3,1},{4,6},{5,7},{6,4},{7,5},{8,10},{9,11},{10,... | collective-permute-start | bytes 1179656 | tf_op jit(solution)/shard_map/ppermute | solution.py:396
  32.2 12.6 %collective-permute-start.12 = (bf16[256,768]{1,0:T(8,128)(2,1)S(1)}, bf16[256,768]{1,0:T(8,128)(2,1)S(1)}, u32[]{:S(2)}, u32[]{:S(2)}) collective-permute-start(bf16[256,768]{1,0:T(8,128)(2,1)S(1)} %collective-permute-done.11.refs_5_.refs_7_), channel_id=1, source_target_pairs={{0,1},{1,0},{2,3},{3,2},{4,5},{5,4},{6,7},{7,6},{8,9},{9,8},{10,11... | collective-permute-start | bytes 1179656 | tf_op jit(solution)/shard_map/ppermute | solution.py:396
  32.2 19.6 %collective-permute-start.15 = (bf16[264,768]{1,0:T(8,128)(2,1)S(1)}, bf16[264,768]{1,0:T(8,128)(2,1)S(1)}, u32[]{:S(2)}, u32[]{:S(2)}) collective-permute-start(bf16[264,768]{1,0:T(8,128)(2,1)S(1)} %slice.9), channel_id=1, source_target_pairs={{0,4},{1,5},{2,6},{3,7},{4,0},{5,1},{6,2},{7,3},{8,12},{9,13},{10,... | collective-permute-start | bytes 1216520 | tf_op jit(solution)/shard_map/ppermute | solution.py:396
  44.8 9.7 %collective-permute-start.13 = (f32[1,512]{1,0:T(1,128)S(1)}, f32[1,512]{1,0:T(1,128)S(1)}, u32[]{:S(2)}, u32[]{:S(2)}) collective-permute-start(f32[1,512]{1,0:T(1,128)S(1)} %get-tuple-element.41), channel_id=1, source_target_pairs={{0,2},{1,3},{2,0},{3,1},{4,6},{5,7},{6,4},{7,5},{8,10},{9,11},{10,... | collective-permute-start | bytes 6152 | tf_op jit(solution)/shard_map/ppermute | solution.py:396
  51.8 7.3 %collective-permute-start.16 = (f32[1,512]{1,0:T(1,128)S(1)}, f32[1,512]{1,0:T(1,128)S(1)}, u32[]{:S(2)}, u32[]{:S(2)}) collective-permute-start(f32[1,512]{1,0:T(1,128)S(1)} %get-tuple-element.45), channel_id=1, source_target_pairs={{8,12},{9,13},{10,14},{11,15},{24,28},{25,29},{26,30},{27,31}} | collective-permute-start | bytes 6152 | tf_op jit(solution)/shard_map/ppermute | solution.py:396
  53.1 8.2 %collective-permute-start.17 = (f32[1,512]{1,0:T(1,128)S(1)}, f32[1,512]{1,0:T(1,128)S(1)}, u32[]{:S(2)}, u32[]{:S(2)}) collective-permute-start(f32[1,512]{1,0:T(1,128)S(1)} %get-tuple-element.46), channel_id=1, source_target_pairs={{8,14},{9,15},{10,12},{11,13},{24,30},{25,31},{26,28},{27,29}} | collective-permute-start | bytes 6152 | tf_op jit(solution)/shard_map/ppermute | solution.py:396

commit v4 on v3

--- a/solution.py
+++ b/solution.py
@@ -135,7 +135,7 @@
 
 
 def tag_kernel(
-    rows_hbm, label_hbm, whole_ref, head_ref, tail_ref, mark_ref, rows_ref, label_ref, done
+    rows_hbm, label_hbm, whole_ref, head_ref, tail_ref, low_ref, mark_ref, rows_ref, label_ref, done
 ):
     rows, width = rows_ref.shape
     cut = head_ref.shape[0] - TAG_ROWS
@@ -151,7 +151,7 @@
     codes = (label_ref[...] + 1).astype(jnp.float32)
     line = jnp.broadcast_to(codes, (TAG_ROWS, rows)).astype(jnp.bfloat16)
     mark_ref[...] = line
-    for ref, count in ((whole_ref, rows), (head_ref, cut)):
+    for ref, count in ((whole_ref, rows), (head_ref, cut), (low_ref, rows - cut)):
         ref[count:, :rows] = line
         if rows < width:
             ref[count:, rows:] = jnp.zeros((TAG_ROWS, width - rows), jnp.bfloat16)
@@ -163,13 +163,15 @@
             head_ref[low:high, :] = unit
         else:
             tail_ref[low - cut : high - cut, :] = unit
+            low_ref[low - cut : high - cut, :] = unit
 
 
 def tagged(embeddings, labels):
     rows, width = embeddings.shape
     labels = labels.reshape(1, rows)
     cut = rows // 2
-    shapes = ((rows + TAG_ROWS, width), (cut + TAG_ROWS, width), (rows - cut, width), (TAG_ROWS, rows))
+    shapes = ((rows + TAG_ROWS, width), (cut + TAG_ROWS, width), (rows - cut, width))
+    shapes += ((rows - cut + TAG_ROWS, width), (TAG_ROWS, rows))
     return pl.pallas_call(
         tag_kernel,
         out_shape=[pltpu.VMEM(shape, jnp.bfloat16) for shape in shapes],
@@ -231,6 +233,12 @@
         Block(head_ref, head_ref, 0, cut),
         Block(tail_ref, head_ref, cut, tail_ref.shape[0]),
     ]
+
+
+def paired(head_ref, low_ref):
+    cut = head_ref.shape[0] - TAG_ROWS
+    count = low_ref.shape[0] - TAG_ROWS
+    return [Block(head_ref, head_ref, 0, cut), Block(low_ref, low_ref, cut, count)]
 
 
 def halves(upper_ref, lower_ref):
@@ -293,18 +301,18 @@
 
 
 def here_kernel(
-    own_ref, mine_ref, twin_ref, side_ref, ridge_ref, ridge_twin_ref,
+    own_ref, mine_ref, twin_ref, side_ref, side_low_ref, ridge_ref, ridge_twin_ref,
     head_ref, head_twin_ref, tail_ref, tail_twin_ref, mine_out, side_out, above_out,
 ):
     layer, column, _ = place()
     mine_out[...] = own_ref[...]
     for ref in (side_out, above_out):
         ref[...] = jnp.full(ref.shape, -1.0, jnp.float32)
-    near = [whole(mine_ref), whole(side_ref)]
+    near = [whole(mine_ref), paired(side_ref, side_low_ref)]
 
     @pl.when(column == 0)
     def _():
-        raise_all([side_out], [whole(side_ref)], whole(mine_ref) + whole(twin_ref))
+        raise_all([side_out], near[1:], whole(mine_ref) + whole(twin_ref))
 
     @pl.when(layer % 2 == 1)
     def _():
@@ -322,7 +330,9 @@
     "whole": whole,
     "split": split,
     "halves": halves,
+    "paired": paired,
     "end": lambda head_ref, tail_ref: split(head_ref, tail_ref)[1:],
+    "low": lambda upper_ref, lower_ref: halves(upper_ref, lower_ref)[1:],
 }
 
 
@@ -334,7 +344,7 @@
     return listed, refs
 
 
-def deep_kernel(queries, keys, started, *refs):
+def deep_kernel(queries, keys, started, worker, *refs):
     layer = place()[0]
     begun, refs = (refs[: len(queries)], refs[len(queries) :]) if started else ((), refs)
     query_blocks, refs = seen(queries, refs)
@@ -342,7 +352,7 @@
     for at, ref in enumerate(outs):
         ref[...] = begun[at][...] if started else jnp.full(ref.shape, -1.0, jnp.float32)
 
-    @pl.when(layer == 2)
+    @pl.when(layer == worker)
     def _():
         raise_all(outs, query_blocks, [block for blocks in key_blocks for block in blocks])
 
@@ -362,14 +372,14 @@
     )(*[pltpu.with_memory_space_constraint(value, pltpu.VMEM) for value in arrays])
 
 
-def deepened(begun, queries, keys):
+def deepened(begun, queries, keys, worker=2):
     def views(blocks):
         return tuple((view, len(arrays)) for view, *arrays in blocks)
 
     rows = [sum(value.shape[0] for value in arrays) // LANES * LANES for _, *arrays in queries]
     ends = [arrays[-1].shape[0] // LANES * LANES for _, *arrays in keys]
     started = begun is not None
-    body = functools.partial(deep_kernel, views(queries), views(keys), started)
+    body = functools.partial(deep_kernel, views(queries), views(keys), started, worker)
     arrays = [value for _, *values in (*queries, *keys) for value in values]
     pairs = sum(rows) * sum(ends)
     return scored(body, rows, pairs, *(begun if started else ()), *arrays)
@@ -389,6 +399,7 @@
     beside = hops(lambda z, x, c: (z, x, 1 - c))
     outer = hops(lambda z, x, c: (z ^ 1, x, c))
     inner = hops(lambda z, x, c: (z, x, 1 - c) if z in (0, 3) else (3 - z, x, c))
+    cross = hops(lambda z, x, c: (z if z in (0, 3) else 3 - z, x, 1 - c))
     lift = [hop for hop in outer if hop[0] // 4 == 2]
     tilt = [(source, target ^ 2) for source, target in lift]
 
@@ -396,15 +407,16 @@
         return lax.ppermute(value, "wide", pairs)
 
     raw_ridge = sent(embeddings, inner)
-    mine, head, tail, marks = tagged(embeddings, cluster_id[:, 0])
+    mine, head, tail, low, marks = tagged(embeddings, cluster_id[:, 0])
     near_head = sent(head, outer)
-    side = sent(mine, across)
+    side_low = sent(low, across)
     near_tail = sent(tail, outer)
+    side = sent(head, across)
     twin = sent(mine, beside)
     ridge = arrived(raw_ridge, sent(marks, inner))
     deep_head = sent(near_head, inner)
     upper = sent(near_head[: rows // 2], across)
-    lower = sent(side[rows // 2 :], outer)
+    lower = sent(side_low, outer)
     near_head_twin = sent(near_head, beside)
     deep_tail = sent(near_tail, inner)
     near_tail_twin = sent(near_tail, beside)
@@ -416,26 +428,30 @@
     (own,) = scored(own_kernel, [rows], 2 * square, mine, twin)
     best = scored(
         here_kernel, [rows] * 3, 8 * square,
-        own, mine, twin, side, ridge, ridge_twin, near_head, near_head_twin, near_tail, near_tail_twin,
-    )
-    flat = [("whole", mine), ("whole", side)]
+        own, mine, twin, side, side_low, ridge, ridge_twin, near_head, near_head_twin, near_tail, near_tail_twin,
+    )
+    flat = [("whole", mine), ("paired", side, side_low)]
     steep = [("split", near_head, near_tail), ("halves", upper, lower)]
     deep, deep_twin = ("whole", deep_head), ("whole", deep_head_twin)
     third, fourth = ("end", deep_head, deep_tail), ("end", deep_head_twin, deep_tail_twin)
     best = deepened(best, flat + steep[:1], [deep])
     best = deepened(best, flat + steep[:1], [deep_twin])
     keys = [("whole", ridge), ("whole", ridge_twin), deep, deep_twin]
-    best_flat, best_steep = best[:2], best[2:] + deepened(None, steep[1:], keys)
-    best_flat = deepened(best_flat, flat, [third])
-    best_steep = deepened(best_steep, steep, [third])
-    first, second = deepened(best_flat, flat, [fourth])
-    third, fourth = deepened(best_steep, steep, [fourth])
+    first, second = best[:2]
+    from_side = sent(second, across)
+    best = best[2:] + deepened(None, steep[1:], keys)
+    ends = [("end", near_head, near_tail), ("low", upper, lower)]
+    lent, lent_twin = deepened(None, keys[:2], ends, worker=1)
+    from_lent = sent(lent, inner)
+    from_twin = sent(lent_twin, cross)
+    best = deepened(best, steep, [third])
+    third, fourth = deepened(best, steep, [fourth])
     from_below = sent(third, lift)
     from_slant = sent(fourth, tilt)
-    from_side = sent(second, across)
     top = lax.axis_index("wide") // 4 == LAYERS - 1
     under = jnp.where(top, jnp.maximum(from_below, from_slant), -1.0)
-    return jnp.maximum(jnp.maximum(first, from_side), under)[0]
+    early = jnp.maximum(jnp.maximum(first, from_side), jnp.maximum(from_lent, from_twin))
+    return jnp.maximum(early, under)[0]
 
 
 def per_device(embeddings, cluster_id):

time: 62.1 us -> 72.5 us (1.17)
  the two profiles are of different devices: /device:TPU:28 before, /device:TPU:14 now
where the time goes in v4:
time: 72.5 us; the launch traced here: 72.3 us
  waiting for transfers between devices  50.4 us (70%)
  starting transfers between devices  15.7 us (22%)
  Pallas kernels  5.49 us (8%)
    ppermute x21, waiting for transfers between devices, sent(): return lax.ppermute(value, 'wide', pairs)  50.4 us
    ppermute x21, starting transfers between devices, sent(): return lax.ppermute(value, 'wide', pairs)  15.7 us
    pallas_call x8, Pallas kernels, scored(): pl.pallas_call(body, out_shape=[pltpu.VMEM((1, count), jnp.float32) for c...  3.63 us
    pallas_call x1, Pallas kernels, tagged(): pl.pallas_call(tag_kernel, out_shape=[pltpu.VMEM(shape, jnp.bfloat16) for...  1.56 us
  transfers between devices with their start and end apart: 21, of which 10 were waited for; matrix products, arithmetic and copies ran while one was open for 0% of the time, Pallas kernels for 8%

profile of v4, /device:TPU:14, one launch (start us, length us, event | category | flops | bytes accessed | tf_op | source)
XLA Modules:
  0.0 72.3 jit_solution(12421919712333749752)
XLA Ops:
  0.0 1.6 %collective-permute-start.3 = (bf16[512,768]{1,0:T(8,128)(2,1)}, bf16[512,768]{1,0:T(8,128)(2,1)S(1)}, u32[]{:S(2)}, u32[]{:S(2)}) collective-permute-start(bf16[512,768]{1,0:T(8,128)(2,1)} %rows_hbm.1), channel_id=1, source_target_pairs={{0,1},{1,0},{2,3},{3,2},{4,8},{5,9},{6,10},{7,11},{8,4},{9,5},{10,... | collective-permute-start | bytes 2359304 | tf_op jit(solution)/shard_map/ppermute | solution.py:407
  1.6 1.6 %tagged.1 = (bf16[520,768]{1,0:T(8,128)(2,1)S(1)}, bf16[264,768]{1,0:T(8,128)(2,1)S(1)}, bf16[256,768]{1,0:T(8,128)(2,1)S(1)}, bf16[264,768]{1,0:T(8,128)(2,1)S(1)}, bf16[8,512]{1,0:T(8,128)(2,1)S(1)}) custom-call(bf16[512,768]{1,0:T(8,128)(2,1)} %rows_hbm.1, s32[1,512]{1,0:T(1,128)} %bitcast.2), custom_call_target="tpu_custom_call" | custom-call | tf_op jit(solution)/shard_map/tagged/pallas_call | solution.py:175
  3.1 0.1 collective-permute-start
  3.2 0.1 collective-permute-start.8
  3.3 2.0 %collective-permute-start.6 = (bf16[264,768]{1,0:T(8,128)(2,1)S(1)}, bf16[264,768]{1,0:T(8,128)(2,1)S(1)}, u32[]{:S(2)}, u32[]{:S(2)}) collective-permute-start(bf16[264,768]{1,0:T(8,128)(2,1)S(1)} %get-tuple-element.26), channel_id=1, source_target_pairs={{0,4},{1,5},{2,6},{3,7},{4,0},{5,1},{6,2},{7,3},{8,12},{9,13},{10,... | collective-permute-start | bytes 1216520 | tf_op jit(solution)/shard_map/ppermute | solution.py:407
  5.3 0.4 collective-permute-start.4
  5.8 13.9 %collective-permute-done.4.mark_ref = bf16[8,512]{1,0:T(8,128)(2,1)S(1)} collective-permute-done((bf16[8,512]{1,0:T(8,128)(2,1)S(1)}, bf16[8,512]{1,0:T(8,128)(2,1)S(1)}, u32[]{:S(2)}, u32[]{:S(2)}) %collective-permute-start.4) | collective-permute-done | bytes 8224 | tf_op jit(solution)/shard_map/ppermute | solution.py:407
  19.7 0.5 collective-permute-start.1
  20.2 0.0 collective-permute-done.3.rows_ref
  20.2 1.5 %collective-permute-start.2 = (bf16[264,768]{1,0:T(8,128)(2,1)S(1)}, bf16[264,768]{1,0:T(8,128)(2,1)S(1)}, u32[]{:S(2)}, u32[]{:S(2)}) collective-permute-start(bf16[264,768]{1,0:T(8,128)(2,1)S(1)} %get-tuple-element.27), channel_id=1, source_target_pairs={{0,2},{1,3},{2,0},{3,1},{4,6},{5,7},{6,4},{7,5},{8,10},{9,11},{10,... | collective-permute-start | bytes 1216520 | tf_op jit(solution)/shard_map/ppermute | solution.py:407
  21.7 0.3 arrived.1.ridge_ref.refs_0_.refs_2_
  22.0 0.0 collective-permute-done.8.tail_ref.refs_7_.refs_3_
  22.0 0.1 collective-permute-start.5
  22.1 1.3 %collective-permute-done.6.head_ref.refs_6_.refs_2_ = bf16[264,768]{1,0:T(8,128)(2,1)S(1)} collective-permute-done((bf16[264,768]{1,0:T(8,128)(2,1)S(1)}, bf16[264,768]{1,0:T(8,128)(2,1)S(1)}, u32[]{:S(2)}, u32[]{:S(2)}) %collective-permute-start.6) | collective-permute-done | bytes 405536 | tf_op jit(solution)/shard_map/ppermute | solution.py:407
  23.4 0.4 collective-permute-start.10
  23.9 8.0 %collective-permute-done.1.side_ref.refs_4_ = bf16[264,768]{1,0:T(8,128)(2,1)S(1)} collective-permute-done((bf16[264,768]{1,0:T(8,128)(2,1)S(1)}, bf16[264,768]{1,0:T(8,128)(2,1)S(1)}, u32[]{:S(2)}, u32[]{:S(2)}) %collective-permute-start.1) | collective-permute-done | bytes 405536 | tf_op jit(solution)/shard_map/ppermute | solution.py:407
  31.9 0.0 collective-permute-start.7
  31.9 6.7 %collective-permute-done.2.side_low_ref.refs_5_ = bf16[264,768]{1,0:T(8,128)(2,1)S(1)} collective-permute-done((bf16[264,768]{1,0:T(8,128)(2,1)S(1)}, bf16[264,768]{1,0:T(8,128)(2,1)S(1)}, u32[]{:S(2)}, u32[]{:S(2)}) %collective-permute-start.2) | collective-permute-done | bytes 405536 | tf_op jit(solution)/shard_map/ppermute | solution.py:407
  38.6 0.0 collective-permute-start.9
  38.6 0.0 collective-permute-done.twin_ref
  38.6 1.6 %collective-permute-start.17 = (bf16[256,768]{1,0:T(8,128)(2,1)S(1)}, bf16[256,768]{1,0:T(8,128)(2,1)S(1)}, u32[]{:S(2)}, u32[]{:S(2)}) collective-permute-start(bf16[256,768]{1,0:T(8,128)(2,1)S(1)} %collective-permute-done.8.tail_ref.refs_7_.refs_3_), channel_id=1, source_target_pairs={{0,1},{1,0},{2,3},{3,2},{4,8},{5,9},{6,10},{7,11},{8,4},{9,5},{10,... | collective-permute-start | bytes 1179656 | tf_op jit(solution)/shard_map/ppermute | solution.py:407
  40.2 0.0 collective-permute-done.10.refs_8_.refs_4_.refs_6_
  40.2 0.3 collective-permute-start.11
  40.5 0.6 shard_map.28.own_ref
  41.2 0.0 collective-permute-done.9.tail_twin_ref
  41.2 0.6 collective-permute-start.13
  41.8 8.4 %collective-permute-done.17.refs_7_ = bf16[256,768]{1,0:T(8,128)(2,1)S(1)} collective-permute-done((bf16[256,768]{1,0:T(8,128)(2,1)S(1)}, bf16[256,768]{1,0:T(8,128)(2,1)S(1)}, u32[]{:S(2)}, u32[]{:S(2)}) %collective-permute-start.17) | collective-permute-done | bytes 393248 | tf_op jit(solution)/shard_map/ppermute | solution.py:407
  50.2 0.0 collective-permute-start.14
  50.2 0.0 collective-permute-done.7.head_twin_ref
  50.2 0.0 collective-permute-start.18
  50.2 0.0 collective-permute-done.5.ridge_twin_ref.refs_1_.refs_3_
  50.2 1.9 %shard_map.29 = (f32[1,512]{1,0:T(1,128)S(1)}, f32[1,512]{1,0:T(1,128)S(1)}, f32[1,512]{1,0:T(1,128)S(1)}) custom-call(f32[1,512]{1,0:T(1,128)S(1)} %shard_map.28.own_ref, bf16[520,768]{1,0:T(8,128)(2,1)S(1)} %get-tuple-element.25.mine_ref.refs_3_, bf16[520,768]{1,0:T(8,128)(2,1)S(1)} %collective-permute-done.twin_ref, ...), custom_call_target="tpu_custom_call" | custom-call | flops 3221225472 | bytes 5605376 | tf_op jit(solution)/shard_map/pallas_call | solution.py:362
  52.1 0.0 collective-permute-done.11.refs_8_.refs_5_.refs_6_
  52.2 1.0 %collective-permute-done.13.refs_4_.refs_0_ = bf16[256,768]{1,0:T(8,128)(2,1)S(1)} collective-permute-done((bf16[256,768]{1,0:T(8,128)(2,1)S(1)}, bf16[256,768]{1,0:T(8,128)(2,1)S(1)}, u32[]{:S(2)}, u32[]{:S(2)}) %collective-permute-start.13) | collective-permute-done | bytes 393248 | tf_op jit(solution)/shard_map/ppermute | solution.py:407
  53.1 8.0 %collective-permute-done.14.refs_5_.refs_1_ = bf16[264,768]{1,0:T(8,128)(2,1)S(1)} collective-permute-done((bf16[264,768]{1,0:T(8,128)(2,1)S(1)}, bf16[264,768]{1,0:T(8,128)(2,1)S(1)}, u32[]{:S(2)}, u32[]{:S(2)}) %collective-permute-start.14) | collective-permute-done | bytes 405536 | tf_op jit(solution)/shard_map/ppermute | solution.py:407
  61.1 0.0 collective-permute-done.18.refs_7_
  61.1 0.7 collective-permute-start.19
  61.8 0.7 collective-permute-start.20
  62.5 1.0 %shard_map.32 = (f32[1,512]{1,0:T(1,128)S(1)}, f32[1,512]{1,0:T(1,128)S(1)}) custom-call(bf16[520,768]{1,0:T(8,128)(2,1)S(1)} %arrived.1.ridge_ref.refs_0_.refs_2_, bf16[520,768]{1,0:T(8,128)(2,1)S(1)} %collective-permute-done.5.ridge_twin_ref.refs_1_.refs_3_, bf16[264,768]{1,0:T(8,128)(2,1)S(1)} %collective-permute-done.6.head_ref.refs_6_.refs_2_, ...), custom_call_target="tpu_custom_call" | custom-call | flops 805306368 | bytes 3194880 | tf_op jit(solution)/shard_map/pallas_call | solution.py:362
  63.5 4.6 %collective-permute-start.15 = (f32[1,512]{1,0:T(1,128)S(1)}, f32[1,512]{1,0:T(1,128)S(1)}, u32[]{:S(2)}, u32[]{:S(2)}) collective-permute-start(f32[1,512]{1,0:T(1,128)S(1)} %get-tuple-element.38), channel_id=1, source_target_pairs={{0,1},{1,0},{2,3},{3,2},{4,8},{5,9},{6,10},{7,11},{8,4},{9,5},{10,... | collective-permute-start | bytes 6152 | tf_op jit(solution)/shard_map/ppermute | solution.py:407
  68.1 0.0 collective-permute-start.16
  68.1 0.5 collective-permute-start.12
  68.7 0.0 collective-permute-done.19
  68.7 0.0 collective-permute-done.20
  68.7 1.0 %collective-permute-done.15 = f32[1,512]{1,0:T(1,128)S(1)} collective-permute-done((f32[1,512]{1,0:T(1,128)S(1)}, f32[1,512]{1,0:T(1,128)S(1)}, u32[]{:S(2)}, u32[]{:S(2)}) %collective-permute-start.15) | collective-permute-done | bytes 2080 | tf_op jit(solution)/shard_map/ppermute | solution.py:407
  69.7 1.4 %collective-permute-done.16 = f32[1,512]{1,0:T(1,128)S(1)} collective-permute-done((f32[1,512]{1,0:T(1,128)S(1)}, f32[1,512]{1,0:T(1,128)S(1)}, u32[]{:S(2)}, u32[]{:S(2)}) %collective-permute-start.16) | collective-permute-done | bytes 2080 | tf_op jit(solution)/shard_map/ppermute | solution.py:407
  71.1 0.6 collective-permute-done.12
  71.7 0.6 fusion
  (6 shorter events, 0.1 us)
Async XLA Ops:
  0.0 20.2 %collective-permute-start.3 = (bf16[512,768]{1,0:T(8,128)(2,1)}, bf16[512,768]{1,0:T(8,128)(2,1)S(1)}, u32[]{:S(2)}, u32[]{:S(2)}) collective-permute-start(bf16[512,768]{1,0:T(8,128)(2,1)} %rows_hbm.1), channel_id=1, source_target_pairs={{0,1},{1,0},{2,3},{3,2},{4,8},{5,9},{6,10},{7,11},{8,4},{9,5},{10,... | collective-permute-start | bytes 2359304 | tf_op jit(solution)/shard_map/ppermute | solution.py:407
  3.1 35.5 %collective-permute-start = (bf16[520,768]{1,0:T(8,128)(2,1)S(1)}, bf16[520,768]{1,0:T(8,128)(2,1)S(1)}, u32[]{:S(2)}, u32[]{:S(2)}) collective-permute-start(bf16[520,768]{1,0:T(8,128)(2,1)S(1)} %get-tuple-element.25.mine_ref.refs_3_), channel_id=1, source_target_pairs={{0,1},{1,0},{2,3},{3,2},{4,5},{5,4},{6,7},{7,6},{8,9},{9,8},{10,11... | collective-permute-start | bytes 2396168 | tf_op jit(solution)/shard_map/ppermute | solution.py:407
  3.2 18.8 %collective-permute-start.8 = (bf16[256,768]{1,0:T(8,128)(2,1)S(1)}, bf16[256,768]{1,0:T(8,128)(2,1)S(1)}, u32[]{:S(2)}, u32[]{:S(2)}) collective-permute-start(bf16[256,768]{1,0:T(8,128)(2,1)S(1)} %get-tuple-element.29), channel_id=1, source_target_pairs={{0,4},{1,5},{2,6},{3,7},{4,0},{5,1},{6,2},{7,3},{8,12},{9,13},{10,... | collective-permute-start | bytes 1179656 | tf_op jit(solution)/shard_map/ppermute | solution.py:407
  3.3 20.1 %collective-permute-start.6 = (bf16[264,768]{1,0:T(8,128)(2,1)S(1)}, bf16[264,768]{1,0:T(8,128)(2,1)S(1)}, u32[]{:S(2)}, u32[]{:S(2)}) collective-permute-start(bf16[264,768]{1,0:T(8,128)(2,1)S(1)} %get-tuple-element.26), channel_id=1, source_target_pairs={{0,4},{1,5},{2,6},{3,7},{4,0},{5,1},{6,2},{7,3},{8,12},{9,13},{10,... | collective-permute-start | bytes 1216520 | tf_op jit(solution)/shard_map/ppermute | solution.py:407
  5.3 14.4 %collective-permute-start.4 = (bf16[8,512]{1,0:T(8,128)(2,1)S(1)}, bf16[8,512]{1,0:T(8,128)(2,1)S(1)}, u32[]{:S(2)}, u32[]{:S(2)}) collective-permute-start(bf16[8,512]{1,0:T(8,128)(2,1)S(1)} %get-tuple-element.28), channel_id=1, source_target_pairs={{0,1},{1,0},{2,3},{3,2},{4,8},{5,9},{6,10},{7,11},{8,4},{9,5},{10,... | collective-permute-start | bytes 24584 | tf_op jit(solution)/shard_map/ppermute | solution.py:407
  19.7 12.2 %collective-permute-start.1 = (bf16[264,768]{1,0:T(8,128)(2,1)S(1)}, bf16[264,768]{1,0:T(8,128)(2,1)S(1)}, u32[]{:S(2)}, u32[]{:S(2)}) collective-permute-start(bf16[264,768]{1,0:T(8,128)(2,1)S(1)} %get-tuple-element.26), channel_id=1, source_target_pairs={{0,2},{1,3},{2,0},{3,1},{4,6},{5,7},{6,4},{7,5},{8,10},{9,11},{10,... | collective-permute-start | bytes 1216520 | tf_op jit(solution)/shard_map/ppermute | solution.py:407
  20.2 18.4 %collective-permute-start.2 = (bf16[264,768]{1,0:T(8,128)(2,1)S(1)}, bf16[264,768]{1,0:T(8,128)(2,1)S(1)}, u32[]{:S(2)}, u32[]{:S(2)}) collective-permute-start(bf16[264,768]{1,0:T(8,128)(2,1)S(1)} %get-tuple-element.27), channel_id=1, source_target_pairs={{0,2},{1,3},{2,0},{3,1},{4,6},{5,7},{6,4},{7,5},{8,10},{9,11},{10,... | collective-permute-start | bytes 1216520 | tf_op jit(solution)/shard_map/ppermute | solution.py:407
  22.0 28.2 %collective-permute-start.5 = (bf16[520,768]{1,0:T(8,128)(2,1)S(1)}, bf16[520,768]{1,0:T(8,128)(2,1)S(1)}, u32[]{:S(2)}, u32[]{:S(2)}) collective-permute-start(bf16[520,768]{1,0:T(8,128)(2,1)S(1)} %arrived.1.ridge_ref.refs_0_.refs_2_), channel_id=1, source_target_pairs={{0,1},{1,0},{2,3},{3,2},{4,5},{5,4},{6,7},{7,6},{8,9},{9,8},{10,11... | collective-permute-start | bytes 2396168 | tf_op jit(solution)/shard_map/ppermute | solution.py:407
  23.4 16.8 %collective-permute-start.10 = (bf16[264,768]{1,0:T(8,128)(2,1)S(1)}, bf16[264,768]{1,0:T(8,128)(2,1)S(1)}, u32[]{:S(2)}, u32[]{:S(2)}) collective-permute-start(bf16[264,768]{1,0:T(8,128)(2,1)S(1)} %collective-permute-done.6.head_ref.refs_6_.refs_2_), channel_id=1, source_target_pairs={{0,1},{1,0},{2,3},{3,2},{4,8},{5,9},{6,10},{7,11},{8,4},{9,5},{10,... | collective-permute-start | bytes 1216520 | tf_op jit(solution)/shard_map/ppermute | solution.py:407
  31.9 18.2 %collective-permute-start.7 = (bf16[264,768]{1,0:T(8,128)(2,1)S(1)}, bf16[264,768]{1,0:T(8,128)(2,1)S(1)}, u32[]{:S(2)}, u32[]{:S(2)}) collective-permute-start(bf16[264,768]{1,0:T(8,128)(2,1)S(1)} %collective-permute-done.6.head_ref.refs_6_.refs_2_), channel_id=1, source_target_pairs={{0,1},{1,0},{2,3},{3,2},{4,5},{5,4},{6,7},{7,6},{8,9},{9,8},{10,11... | collective-permute-start | bytes 1216520 | tf_op jit(solution)/shard_map/ppermute | solution.py:407
  38.6 2.5 %collective-permute-start.9 = (bf16[256,768]{1,0:T(8,128)(2,1)S(1)}, bf16[256,768]{1,0:T(8,128)(2,1)S(1)}, u32[]{:S(2)}, u32[]{:S(2)}) collective-permute-start(bf16[256,768]{1,0:T(8,128)(2,1)S(1)} %collective-permute-done.8.tail_ref.refs_7_.refs_3_), channel_id=1, source_target_pairs={{0,1},{1,0},{2,3},{3,2},{4,5},{5,4},{6,7},{7,6},{8,9},{9,8},{10,11... | collective-permute-start | bytes 1179656 | tf_op jit(solution)/shard_map/ppermute | solution.py:407
  38.6 11.5 %collective-permute-start.17 = (bf16[256,768]{1,0:T(8,128)(2,1)S(1)}, bf16[256,768]{1,0:T(8,128)(2,1)S(1)}, u32[]{:S(2)}, u32[]{:S(2)}) collective-permute-start(bf16[256,768]{1,0:T(8,128)(2,1)S(1)} %collective-permute-done.8.tail_ref.refs_7_.refs_3_), channel_id=1, source_target_pairs={{0,1},{1,0},{2,3},{3,2},{4,8},{5,9},{6,10},{7,11},{8,4},{9,5},{10,... | collective-permute-start | bytes 1179656 | tf_op jit(solution)/shard_map/ppermute | solution.py:407
  40.2 11.9 %collective-permute-start.11 = (bf16[264,768]{1,0:T(8,128)(2,1)S(1)}, bf16[264,768]{1,0:T(8,128)(2,1)S(1)}, u32[]{:S(2)}, u32[]{:S(2)}) collective-permute-start(bf16[264,768]{1,0:T(8,128)(2,1)S(1)} %collective-permute-done.10.refs_8_.refs_4_.refs_6_), channel_id=1, source_target_pairs={{0,1},{1,0},{2,3},{3,2},{4,5},{5,4},{6,7},{7,6},{8,9},{9,8},{10,11... | collective-permute-start | bytes 1216520 | tf_op jit(solution)/shard_map/ppermute | solution.py:407
  41.2 12.0 %collective-permute-start.13 = (bf16[256,768]{1,0:T(8,128)(2,1)S(1)}, bf16[256,768]{1,0:T(8,128)(2,1)S(1)}, u32[]{:S(2)}, u32[]{:S(2)}) collective-permute-start(bf16[256,768]{1,0:T(8,128)(2,1)S(1)} %slice.4), channel_id=1, source_target_pairs={{0,2},{1,3},{2,0},{3,1},{4,6},{5,7},{6,4},{7,5},{8,10},{9,11},{10,... | collective-permute-start | bytes 1179656 | tf_op jit(solution)/shard_map/ppermute | solution.py:407
  50.2 10.9 %collective-permute-start.14 = (bf16[264,768]{1,0:T(8,128)(2,1)S(1)}, bf16[264,768]{1,0:T(8,128)(2,1)S(1)}, u32[]{:S(2)}, u32[]{:S(2)}) collective-permute-start(bf16[264,768]{1,0:T(8,128)(2,1)S(1)} %collective-permute-done.2.side_low_ref.refs_5_), channel_id=1, source_target_pairs={{0,4},{1,5},{2,6},{3,7},{4,0},{5,1},{6,2},{7,3},{8,12},{9,13},{10,... | collective-permute-start | bytes 1216520 | tf_op jit(solution)/shard_map/ppermute | solution.py:407
  50.2 10.9 %collective-permute-start.18 = (bf16[256,768]{1,0:T(8,128)(2,1)S(1)}, bf16[256,768]{1,0:T(8,128)(2,1)S(1)}, u32[]{:S(2)}, u32[]{:S(2)}) collective-permute-start(bf16[256,768]{1,0:T(8,128)(2,1)S(1)} %collective-permute-done.17.refs_7_), channel_id=1, source_target_pairs={{0,1},{1,0},{2,3},{3,2},{4,5},{5,4},{6,7},{7,6},{8,9},{9,8},{10,11... | collective-permute-start | bytes 1179656 | tf_op jit(solution)/shard_map/ppermute | solution.py:407
  61.1 7.5 %collective-permute-start.19 = (f32[1,512]{1,0:T(1,128)S(1)}, f32[1,512]{1,0:T(1,128)S(1)}, u32[]{:S(2)}, u32[]{:S(2)}) collective-permute-start(f32[1,512]{1,0:T(1,128)S(1)} %get-tuple-element.43), channel_id=1, source_target_pairs={{8,12},{9,13},{10,14},{11,15},{24,28},{25,29},{26,30},{27,31}} | collective-permute-start | bytes 6152 | tf_op jit(solution)/shard_map/ppermute | solution.py:407
  61.8 6.9 %collective-permute-start.20 = (f32[1,512]{1,0:T(1,128)S(1)}, f32[1,512]{1,0:T(1,128)S(1)}, u32[]{:S(2)}, u32[]{:S(2)}) collective-permute-start(f32[1,512]{1,0:T(1,128)S(1)} %get-tuple-element.44), channel_id=1, source_target_pairs={{8,14},{9,15},{10,12},{11,13},{24,30},{25,31},{26,28},{27,29}} | collective-permute-start | bytes 6152 | tf_op jit(solution)/shard_map/ppermute | solution.py:407
  63.5 6.2 %collective-permute-start.15 = (f32[1,512]{1,0:T(1,128)S(1)}, f32[1,512]{1,0:T(1,128)S(1)}, u32[]{:S(2)}, u32[]{:S(2)}) collective-permute-start(f32[1,512]{1,0:T(1,128)S(1)} %get-tuple-element.38), channel_id=1, source_target_pairs={{0,1},{1,0},{2,3},{3,2},{4,8},{5,9},{6,10},{7,11},{8,4},{9,5},{10,... | collective-permute-start | bytes 6152 | tf_op jit(solution)/shard_map/ppermute | solution.py:407
  68.1 3.0 %collective-permute-start.16 = (f32[1,512]{1,0:T(1,128)S(1)}, f32[1,512]{1,0:T(1,128)S(1)}, u32[]{:S(2)}, u32[]{:S(2)}) collective-permute-start(f32[1,512]{1,0:T(1,128)S(1)} %get-tuple-element.39), channel_id=1, source_target_pairs={{0,1},{1,0},{2,3},{3,2},{4,9},{5,8},{6,11},{7,10},{8,5},{9,4},{10,... | collective-permute-start | bytes 6152 | tf_op jit(solution)/shard_map/ppermute | solution.py:407
  68.1 3.6 %collective-permute-start.12 = (f32[1,512]{1,0:T(1,128)S(1)}, f32[1,512]{1,0:T(1,128)S(1)}, u32[]{:S(2)}, u32[]{:S(2)}) collective-permute-start(f32[1,512]{1,0:T(1,128)S(1)} %get-tuple-element.37), channel_id=1, source_target_pairs={{0,2},{1,3},{2,0},{3,1},{4,6},{5,7},{6,4},{7,5},{8,10},{9,11},{10,... | collective-permute-start | bytes 6152 | tf_op jit(solution)/shard_map/ppermute | solution.py:407

commit v5 on v4

--- a/solution.py
+++ b/solution.py
@@ -332,6 +332,7 @@
     "halves": halves,
     "paired": paired,
     "end": lambda head_ref, tail_ref: split(head_ref, tail_ref)[1:],
+    "first": lambda head_ref, spare_ref: whole(head_ref),
     "low": lambda upper_ref, lower_ref: halves(upper_ref, lower_ref)[1:],
 }
 
@@ -399,9 +400,8 @@
     beside = hops(lambda z, x, c: (z, x, 1 - c))
     outer = hops(lambda z, x, c: (z ^ 1, x, c))
     inner = hops(lambda z, x, c: (z, x, 1 - c) if z in (0, 3) else (3 - z, x, c))
-    cross = hops(lambda z, x, c: (z if z in (0, 3) else 3 - z, x, 1 - c))
-    lift = [hop for hop in outer if hop[0] // 4 == 2]
-    tilt = [(source, target ^ 2) for source, target in lift]
+    slant = hops(lambda z, x, c: (z ^ 1, 1 - x, c))
+    spring = hops(lambda z, x, c: ((z, x, 1 - c), (3, x, c), (1, x, c), (2, x, c))[z])
 
     def sent(value, pairs):
         return lax.ppermute(value, "wide", pairs)
@@ -422,7 +422,7 @@
     near_tail_twin = sent(near_tail, beside)
     ridge_twin = sent(ridge, beside)
     deep_head_twin = sent(deep_head, beside)
-    deep_tail_twin = sent(deep_tail, beside)
+    lower_twin = sent(lower, beside)
 
     square = rows * rows
     (own,) = scored(own_kernel, [rows], 2 * square, mine, twin)
@@ -433,25 +433,26 @@
     flat = [("whole", mine), ("paired", side, side_low)]
     steep = [("split", near_head, near_tail), ("halves", upper, lower)]
     deep, deep_twin = ("whole", deep_head), ("whole", deep_head_twin)
-    third, fourth = ("end", deep_head, deep_tail), ("end", deep_head_twin, deep_tail_twin)
     best = deepened(best, flat + steep[:1], [deep])
     best = deepened(best, flat + steep[:1], [deep_twin])
     keys = [("whole", ridge), ("whole", ridge_twin), deep, deep_twin]
     first, second = best[:2]
     from_side = sent(second, across)
-    best = best[2:] + deepened(None, steep[1:], keys)
-    ends = [("end", near_head, near_tail), ("low", upper, lower)]
-    lent, lent_twin = deepened(None, keys[:2], ends, worker=1)
+    third, fourth = best[2:] + deepened(None, steep[1:], keys)
+    from_below = sent(third, outer)
+    from_far = sent(fourth, slant)
+    ends = [
+        ("end", near_head, near_tail), ("end", near_head_twin, near_tail_twin),
+        ("low", upper, lower), ("low", upper, lower_twin),
+    ]
+    guests = [("whole", ridge), ("first", deep_head, near_tail)]
+    begun = deepened(None, guests, ends[:2], worker=1)
+    lent, lifted = deepened(begun, guests, ends[2:], worker=1)
+    (lifted,) = deepened([lifted], [("end", deep_head, deep_tail)], ends, worker=1)
+    from_lifted = sent(lifted, spring)
     from_lent = sent(lent, inner)
-    from_twin = sent(lent_twin, cross)
-    best = deepened(best, steep, [third])
-    third, fourth = deepened(best, steep, [fourth])
-    from_below = sent(third, lift)
-    from_slant = sent(fourth, tilt)
-    top = lax.axis_index("wide") // 4 == LAYERS - 1
-    under = jnp.where(top, jnp.maximum(from_below, from_slant), -1.0)
-    early = jnp.maximum(jnp.maximum(first, from_side), jnp.maximum(from_lent, from_twin))
-    return jnp.maximum(early, under)[0]
+    parts = (first, from_side, from_below, from_far, from_lent, from_lifted)
+    return functools.reduce(jnp.maximum, parts)[0]
 
 
 def per_device(embeddings, cluster_id):

time: 72.5 us -> 71.8 us (level)
  the two profiles are of different devices: /device:TPU:14 before, /device:TPU:0 now
where the time goes in v5:
time: 71.8 us; the launch traced here: 70.6 us
  waiting for transfers between devices  38.1 us (53%)
  starting transfers between devices  28.1 us (39%)
  Pallas kernels  3.6 us (5%)
    ppermute x21, waiting for transfers between devices, sent(): return lax.ppermute(value, 'wide', pairs)  38.1 us
    ppermute x21, starting transfers between devices, sent(): return lax.ppermute(value, 'wide', pairs)  28.1 us
    pallas_call x8, Pallas kernels, scored(): pl.pallas_call(body, out_shape=[pltpu.VMEM((1, count), jnp.float32) for c...  1.76 us
    pallas_call x1, Pallas kernels, tagged(): pl.pallas_call(tag_kernel, out_shape=[pltpu.VMEM(shape, jnp.bfloat16) for...  1.54 us
  transfers between devices with their start and end apart: 21, of which 7 were waited for; matrix products, arithmetic and copies ran while one was open for 0% of the time, Pallas kernels for 5%

profile of v5, /device:TPU:0, one launch (start us, length us, event | category | flops | bytes accessed | tf_op | source)
XLA Modules:
  0.0 70.6 jit_solution(5551252146773125413)
XLA Ops:
  0.0 0.5 collective-permute-start.3
  0.5 1.5 %tagged.1 = (bf16[520,768]{1,0:T(8,128)(2,1)S(1)}, bf16[264,768]{1,0:T(8,128)(2,1)S(1)}, bf16[256,768]{1,0:T(8,128)(2,1)S(1)}, bf16[264,768]{1,0:T(8,128)(2,1)S(1)}, bf16[8,512]{1,0:T(8,128)(2,1)S(1)}) custom-call(bf16[512,768]{1,0:T(8,128)(2,1)} %rows_hbm.1, s32[1,512]{1,0:T(1,128)} %bitcast.2), custom_call_target="tpu_custom_call" | custom-call | tf_op jit(solution)/shard_map/tagged/pallas_call | solution.py:175
  2.0 4.2 %collective-permute-start.8 = (bf16[256,768]{1,0:T(8,128)(2,1)S(1)}, bf16[256,768]{1,0:T(8,128)(2,1)S(1)}, u32[]{:S(2)}, u32[]{:S(2)}) collective-permute-start(bf16[256,768]{1,0:T(8,128)(2,1)S(1)} %get-tuple-element.27), channel_id=1, source_target_pairs={{0,4},{1,5},{2,6},{3,7},{4,0},{5,1},{6,2},{7,3},{8,12},{9,13},{10,... | collective-permute-start | bytes 1179656 | tf_op jit(solution)/shard_map/ppermute | solution.py:407
  6.3 1.5 %collective-permute-start.2 = (bf16[264,768]{1,0:T(8,128)(2,1)S(1)}, bf16[264,768]{1,0:T(8,128)(2,1)S(1)}, u32[]{:S(2)}, u32[]{:S(2)}) collective-permute-start(bf16[264,768]{1,0:T(8,128)(2,1)S(1)} %get-tuple-element.25), channel_id=1, source_target_pairs={{0,2},{1,3},{2,0},{3,1},{4,6},{5,7},{6,4},{7,5},{8,10},{9,11},{10,... | collective-permute-start | bytes 1216520 | tf_op jit(solution)/shard_map/ppermute | solution.py:407
  7.8 0.0 collective-permute-start
  7.8 0.5 collective-permute-start.4
  8.3 1.8 %collective-permute-done.4.mark_ref = bf16[8,512]{1,0:T(8,128)(2,1)S(1)} collective-permute-done((bf16[8,512]{1,0:T(8,128)(2,1)S(1)}, bf16[8,512]{1,0:T(8,128)(2,1)S(1)}, u32[]{:S(2)}, u32[]{:S(2)}) %collective-permute-start.4) | collective-permute-done | bytes 8224 | tf_op jit(solution)/shard_map/ppermute | solution.py:407
  10.1 12.7 %collective-permute-start.6 = (bf16[264,768]{1,0:T(8,128)(2,1)S(1)}, bf16[264,768]{1,0:T(8,128)(2,1)S(1)}, u32[]{:S(2)}, u32[]{:S(2)}) collective-permute-start(bf16[264,768]{1,0:T(8,128)(2,1)S(1)} %get-tuple-element.24), channel_id=1, source_target_pairs={{0,4},{1,5},{2,6},{3,7},{4,0},{5,1},{6,2},{7,3},{8,12},{9,13},{10,... | collective-permute-start | bytes 1216520 | tf_op jit(solution)/shard_map/ppermute | solution.py:407
  22.7 0.0 collective-permute-done.8.tail_ref.refs_7_.refs_2_.refs_4_
  22.7 0.0 collective-permute-start.9
  22.7 0.0 collective-permute-done.2.side_low_ref.refs_5_
  22.7 0.1 collective-permute-start.15
  22.8 10.1 %collective-permute-done.6.head_ref.refs_6_.refs_3_ = bf16[264,768]{1,0:T(8,128)(2,1)S(1)} collective-permute-done((bf16[264,768]{1,0:T(8,128)(2,1)S(1)}, bf16[264,768]{1,0:T(8,128)(2,1)S(1)}, u32[]{:S(2)}, u32[]{:S(2)}) %collective-permute-start.6) | collective-permute-done | bytes 405536 | tf_op jit(solution)/shard_map/ppermute | solution.py:407
  32.9 0.0 collective-permute-start.7
  33.0 0.0 collective-permute-done.3.rows_ref
  33.0 0.5 collective-permute-start.10
  33.5 0.3 arrived.1.ridge_ref.refs_2_.refs_0_
  33.8 0.0 collective-permute-done.9.tail_twin_ref.refs_6_
  33.8 0.1 collective-permute-start.5
  33.9 6.1 %collective-permute-done.15.refs_1_.refs_6_.refs_8_ = bf16[264,768]{1,0:T(8,128)(2,1)S(1)} collective-permute-done((bf16[264,768]{1,0:T(8,128)(2,1)S(1)}, bf16[264,768]{1,0:T(8,128)(2,1)S(1)}, u32[]{:S(2)}, u32[]{:S(2)}) %collective-permute-start.15) | collective-permute-done | bytes 405536 | tf_op jit(solution)/shard_map/ppermute | solution.py:407
  39.9 0.0 collective-permute-start.17
  40.0 0.0 collective-permute-done.twin_ref
  40.0 1.6 %collective-permute-start.14 = (bf16[256,768]{1,0:T(8,128)(2,1)S(1)}, bf16[256,768]{1,0:T(8,128)(2,1)S(1)}, u32[]{:S(2)}, u32[]{:S(2)}) collective-permute-start(bf16[256,768]{1,0:T(8,128)(2,1)S(1)} %slice.4), channel_id=1, source_target_pairs={{0,2},{1,3},{2,0},{3,1},{4,6},{5,7},{6,4},{7,5},{8,10},{9,11},{10,... | collective-permute-start | bytes 1179656 | tf_op jit(solution)/shard_map/ppermute | solution.py:407
  41.5 0.0 collective-permute-done.7.head_twin_ref.refs_5_
  41.5 0.2 collective-permute-start.19
  41.8 0.0 collective-permute-done.10.refs_8_.refs_4_.refs_1_.refs_3_
  41.8 0.5 collective-permute-start.1
  42.3 0.6 shard_map.28.own_ref
  42.9 9.1 %collective-permute-done.14.refs_0_.refs_5_.refs_7_.refs_9_ = bf16[256,768]{1,0:T(8,128)(2,1)S(1)} collective-permute-done((bf16[256,768]{1,0:T(8,128)(2,1)S(1)}, bf16[256,768]{1,0:T(8,128)(2,1)S(1)}, u32[]{:S(2)}, u32[]{:S(2)}) %collective-permute-start.14) | collective-permute-done | bytes 393248 | tf_op jit(solution)/shard_map/ppermute | solution.py:407
  52.0 0.0 collective-permute-start.11
  52.0 0.0 collective-permute-done.17.refs_8_.refs_10_
  52.1 0.0 collective-permute-done.19.refs_2_
  52.1 0.5 collective-permute-start.20
  52.6 0.1 collective-permute-start.18
  52.7 7.5 %collective-permute-done.1.side_ref.refs_4_ = bf16[264,768]{1,0:T(8,128)(2,1)S(1)} collective-permute-done((bf16[264,768]{1,0:T(8,128)(2,1)S(1)}, bf16[264,768]{1,0:T(8,128)(2,1)S(1)}, u32[]{:S(2)}, u32[]{:S(2)}) %collective-permute-start.1) | collective-permute-done | bytes 405536 | tf_op jit(solution)/shard_map/ppermute | solution.py:407
  60.3 0.0 collective-permute-done.5.ridge_twin_ref.refs_3_
  60.3 1.0 %shard_map.29 = (f32[1,512]{1,0:T(1,128)S(1)}, f32[1,512]{1,0:T(1,128)S(1)}, f32[1,512]{1,0:T(1,128)S(1)}) custom-call(f32[1,512]{1,0:T(1,128)S(1)} %shard_map.28.own_ref, bf16[520,768]{1,0:T(8,128)(2,1)S(1)} %get-tuple-element.23.mine_ref.refs_3_, bf16[520,768]{1,0:T(8,128)(2,1)S(1)} %collective-permute-done.twin_ref, ...), custom_call_target="tpu_custom_call" | custom-call | flops 3221225472 | bytes 5605376 | tf_op jit(solution)/shard_map/pallas_call | solution.py:363
  61.3 0.0 collective-permute-done.11.refs_8_.refs_5_
  61.4 0.5 collective-permute-start.12
  61.9 3.6 %collective-permute-start.13 = (f32[1,512]{1,0:T(1,128)S(1)}, f32[1,512]{1,0:T(1,128)S(1)}, u32[]{:S(2)}, u32[]{:S(2)}) collective-permute-start(f32[1,512]{1,0:T(1,128)S(1)} %get-tuple-element.36), channel_id=1, source_target_pairs={{0,4},{1,5},{2,6},{3,7},{4,0},{5,1},{6,2},{7,3},{8,12},{9,13},{10,... | collective-permute-start | bytes 6152 | tf_op jit(solution)/shard_map/ppermute | solution.py:407
  65.5 1.0 %collective-permute-start.16 = (f32[1,512]{1,0:T(1,128)S(1)}, f32[1,512]{1,0:T(1,128)S(1)}, u32[]{:S(2)}, u32[]{:S(2)}) collective-permute-start(f32[1,512]{1,0:T(1,128)S(1)} %shard_map.32), channel_id=1, source_target_pairs={{0,6},{1,7},{2,4},{3,5},{4,2},{5,3},{6,0},{7,1},{8,14},{9,15},{10,... | collective-permute-start | bytes 6152 | tf_op jit(solution)/shard_map/ppermute | solution.py:407
  66.5 0.0 collective-permute-done.20
  66.5 0.0 collective-permute-done.18
  66.5 0.0 collective-permute-done.12
  66.5 0.5 collective-permute-done.13
  67.1 2.9 %collective-permute-done.16 = f32[1,512]{1,0:T(1,128)S(1)} collective-permute-done((f32[1,512]{1,0:T(1,128)S(1)}, f32[1,512]{1,0:T(1,128)S(1)}, u32[]{:S(2)}, u32[]{:S(2)}) %collective-permute-start.16) | collective-permute-done | bytes 2080 | tf_op jit(solution)/shard_map/ppermute | solution.py:407
  70.0 0.6 maximum_maximum_fusion
  (7 shorter events, 0.1 us)
Async XLA Ops:
  0.0 33.0 %collective-permute-start.3 = (bf16[512,768]{1,0:T(8,128)(2,1)}, bf16[512,768]{1,0:T(8,128)(2,1)S(1)}, u32[]{:S(2)}, u32[]{:S(2)}) collective-permute-start(bf16[512,768]{1,0:T(8,128)(2,1)} %rows_hbm.1), channel_id=1, source_target_pairs={{0,1},{1,0},{2,3},{3,2},{4,8},{5,9},{6,10},{7,11},{8,4},{9,5},{10,... | collective-permute-start | bytes 2359304 | tf_op jit(solution)/shard_map/ppermute | solution.py:407
  2.0 20.7 %collective-permute-start.8 = (bf16[256,768]{1,0:T(8,128)(2,1)S(1)}, bf16[256,768]{1,0:T(8,128)(2,1)S(1)}, u32[]{:S(2)}, u32[]{:S(2)}) collective-permute-start(bf16[256,768]{1,0:T(8,128)(2,1)S(1)} %get-tuple-element.27), channel_id=1, source_target_pairs={{0,4},{1,5},{2,6},{3,7},{4,0},{5,1},{6,2},{7,3},{8,12},{9,13},{10,... | collective-permute-start | bytes 1179656 | tf_op jit(solution)/shard_map/ppermute | solution.py:407
  6.3 16.5 %collective-permute-start.2 = (bf16[264,768]{1,0:T(8,128)(2,1)S(1)}, bf16[264,768]{1,0:T(8,128)(2,1)S(1)}, u32[]{:S(2)}, u32[]{:S(2)}) collective-permute-start(bf16[264,768]{1,0:T(8,128)(2,1)S(1)} %get-tuple-element.25), channel_id=1, source_target_pairs={{0,2},{1,3},{2,0},{3,1},{4,6},{5,7},{6,4},{7,5},{8,10},{9,11},{10,... | collective-permute-start | bytes 1216520 | tf_op jit(solution)/shard_map/ppermute | solution.py:407
  7.8 32.2 %collective-permute-start = (bf16[520,768]{1,0:T(8,128)(2,1)S(1)}, bf16[520,768]{1,0:T(8,128)(2,1)S(1)}, u32[]{:S(2)}, u32[]{:S(2)}) collective-permute-start(bf16[520,768]{1,0:T(8,128)(2,1)S(1)} %get-tuple-element.23.mine_ref.refs_3_), channel_id=1, source_target_pairs={{0,1},{1,0},{2,3},{3,2},{4,5},{5,4},{6,7},{7,6},{8,9},{9,8},{10,11... | collective-permute-start | bytes 2396168 | tf_op jit(solution)/shard_map/ppermute | solution.py:407
  7.8 2.3 %collective-permute-start.4 = (bf16[8,512]{1,0:T(8,128)(2,1)S(1)}, bf16[8,512]{1,0:T(8,128)(2,1)S(1)}, u32[]{:S(2)}, u32[]{:S(2)}) collective-permute-start(bf16[8,512]{1,0:T(8,128)(2,1)S(1)} %get-tuple-element.26), channel_id=1, source_target_pairs={{0,1},{1,0},{2,3},{3,2},{4,8},{5,9},{6,10},{7,11},{8,4},{9,5},{10,... | collective-permute-start | bytes 24584 | tf_op jit(solution)/shard_map/ppermute | solution.py:407
  10.1 22.9 %collective-permute-start.6 = (bf16[264,768]{1,0:T(8,128)(2,1)S(1)}, bf16[264,768]{1,0:T(8,128)(2,1)S(1)}, u32[]{:S(2)}, u32[]{:S(2)}) collective-permute-start(bf16[264,768]{1,0:T(8,128)(2,1)S(1)} %get-tuple-element.24), channel_id=1, source_target_pairs={{0,4},{1,5},{2,6},{3,7},{4,0},{5,1},{6,2},{7,3},{8,12},{9,13},{10,... | collective-permute-start | bytes 1216520 | tf_op jit(solution)/shard_map/ppermute | solution.py:407
  22.7 11.0 %collective-permute-start.9 = (bf16[256,768]{1,0:T(8,128)(2,1)S(1)}, bf16[256,768]{1,0:T(8,128)(2,1)S(1)}, u32[]{:S(2)}, u32[]{:S(2)}) collective-permute-start(bf16[256,768]{1,0:T(8,128)(2,1)S(1)} %collective-permute-done.8.tail_ref.refs_7_.refs_2_.refs_4_), channel_id=1, source_target_pairs={{0,1},{1,0},{2,3},{3,2},{4,5},{5,4},{6,7},{7,6},{8,9},{9,8},{10,11... | collective-permute-start | bytes 1179656 | tf_op jit(solution)/shard_map/ppermute | solution.py:407
  22.7 17.2 %collective-permute-start.15 = (bf16[264,768]{1,0:T(8,128)(2,1)S(1)}, bf16[264,768]{1,0:T(8,128)(2,1)S(1)}, u32[]{:S(2)}, u32[]{:S(2)}) collective-permute-start(bf16[264,768]{1,0:T(8,128)(2,1)S(1)} %collective-permute-done.2.side_low_ref.refs_5_), channel_id=1, source_target_pairs={{0,4},{1,5},{2,6},{3,7},{4,0},{5,1},{6,2},{7,3},{8,12},{9,13},{10,... | collective-permute-start | bytes 1216520 | tf_op jit(solution)/shard_map/ppermute | solution.py:407
  32.9 8.6 %collective-permute-start.7 = (bf16[264,768]{1,0:T(8,128)(2,1)S(1)}, bf16[264,768]{1,0:T(8,128)(2,1)S(1)}, u32[]{:S(2)}, u32[]{:S(2)}) collective-permute-start(bf16[264,768]{1,0:T(8,128)(2,1)S(1)} %collective-permute-done.6.head_ref.refs_6_.refs_3_), channel_id=1, source_target_pairs={{0,1},{1,0},{2,3},{3,2},{4,5},{5,4},{6,7},{7,6},{8,9},{9,8},{10,11... | collective-permute-start | bytes 1216520 | tf_op jit(solution)/shard_map/ppermute | solution.py:407
  33.0 8.8 %collective-permute-start.10 = (bf16[264,768]{1,0:T(8,128)(2,1)S(1)}, bf16[264,768]{1,0:T(8,128)(2,1)S(1)}, u32[]{:S(2)}, u32[]{:S(2)}) collective-permute-start(bf16[264,768]{1,0:T(8,128)(2,1)S(1)} %collective-permute-done.6.head_ref.refs_6_.refs_3_), channel_id=1, source_target_pairs={{0,1},{1,0},{2,3},{3,2},{4,8},{5,9},{6,10},{7,11},{8,4},{9,5},{10,... | collective-permute-start | bytes 1216520 | tf_op jit(solution)/shard_map/ppermute | solution.py:407
  33.8 26.5 %collective-permute-start.5 = (bf16[520,768]{1,0:T(8,128)(2,1)S(1)}, bf16[520,768]{1,0:T(8,128)(2,1)S(1)}, u32[]{:S(2)}, u32[]{:S(2)}) collective-permute-start(bf16[520,768]{1,0:T(8,128)(2,1)S(1)} %arrived.1.ridge_ref.refs_2_.refs_0_), channel_id=1, source_target_pairs={{0,1},{1,0},{2,3},{3,2},{4,5},{5,4},{6,7},{7,6},{8,9},{9,8},{10,11... | collective-permute-start | bytes 2396168 | tf_op jit(solution)/shard_map/ppermute | solution.py:407
  39.9 12.1 %collective-permute-start.17 = (bf16[264,768]{1,0:T(8,128)(2,1)S(1)}, bf16[264,768]{1,0:T(8,128)(2,1)S(1)}, u32[]{:S(2)}, u32[]{:S(2)}) collective-permute-start(bf16[264,768]{1,0:T(8,128)(2,1)S(1)} %collective-permute-done.15.refs_1_.refs_6_.refs_8_), channel_id=1, source_target_pairs={{0,1},{1,0},{2,3},{3,2},{4,5},{5,4},{6,7},{7,6},{8,9},{9,8},{10,11... | collective-permute-start | bytes 1216520 | tf_op jit(solution)/shard_map/ppermute | solution.py:407
  40.0 12.1 %collective-permute-start.14 = (bf16[256,768]{1,0:T(8,128)(2,1)S(1)}, bf16[256,768]{1,0:T(8,128)(2,1)S(1)}, u32[]{:S(2)}, u32[]{:S(2)}) collective-permute-start(bf16[256,768]{1,0:T(8,128)(2,1)S(1)} %slice.4), channel_id=1, source_target_pairs={{0,2},{1,3},{2,0},{3,1},{4,6},{5,7},{6,4},{7,5},{8,10},{9,11},{10,... | collective-permute-start | bytes 1179656 | tf_op jit(solution)/shard_map/ppermute | solution.py:407
  41.5 10.5 %collective-permute-start.19 = (bf16[256,768]{1,0:T(8,128)(2,1)S(1)}, bf16[256,768]{1,0:T(8,128)(2,1)S(1)}, u32[]{:S(2)}, u32[]{:S(2)}) collective-permute-start(bf16[256,768]{1,0:T(8,128)(2,1)S(1)} %collective-permute-done.8.tail_ref.refs_7_.refs_2_.refs_4_), channel_id=1, source_target_pairs={{0,1},{1,0},{2,3},{3,2},{4,8},{5,9},{6,10},{7,11},{8,4},{9,5},{10,... | collective-permute-start | bytes 1179656 | tf_op jit(solution)/shard_map/ppermute | solution.py:407
  41.8 18.5 %collective-permute-start.1 = (bf16[264,768]{1,0:T(8,128)(2,1)S(1)}, bf16[264,768]{1,0:T(8,128)(2,1)S(1)}, u32[]{:S(2)}, u32[]{:S(2)}) collective-permute-start(bf16[264,768]{1,0:T(8,128)(2,1)S(1)} %get-tuple-element.24), channel_id=1, source_target_pairs={{0,2},{1,3},{2,0},{3,1},{4,6},{5,7},{6,4},{7,5},{8,10},{9,11},{10,... | collective-permute-start | bytes 1216520 | tf_op jit(solution)/shard_map/ppermute | solution.py:407
  52.0 9.3 %collective-permute-start.11 = (bf16[264,768]{1,0:T(8,128)(2,1)S(1)}, bf16[264,768]{1,0:T(8,128)(2,1)S(1)}, u32[]{:S(2)}, u32[]{:S(2)}) collective-permute-start(bf16[264,768]{1,0:T(8,128)(2,1)S(1)} %collective-permute-done.10.refs_8_.refs_4_.refs_1_.refs_3_), channel_id=1, source_target_pairs={{0,1},{1,0},{2,3},{3,2},{4,5},{5,4},{6,7},{7,6},{8,9},{9,8},{10,11... | collective-permute-start | bytes 1216520 | tf_op jit(solution)/shard_map/ppermute | solution.py:407
  52.1 14.4 %collective-permute-start.20 = (f32[1,512]{1,0:T(1,128)S(1)}, f32[1,512]{1,0:T(1,128)S(1)}, u32[]{:S(2)}, u32[]{:S(2)}) collective-permute-start(f32[1,512]{1,0:T(1,128)S(1)} %shard_map.35), channel_id=1, source_target_pairs={{0,1},{1,0},{2,3},{3,2},{4,12},{5,13},{6,14},{7,15},{8,4},{9,5},{1... | collective-permute-start | bytes 6152 | tf_op jit(solution)/shard_map/ppermute | solution.py:407
  52.6 13.9 %collective-permute-start.18 = (f32[1,512]{1,0:T(1,128)S(1)}, f32[1,512]{1,0:T(1,128)S(1)}, u32[]{:S(2)}, u32[]{:S(2)}) collective-permute-start(f32[1,512]{1,0:T(1,128)S(1)} %get-tuple-element.39), channel_id=1, source_target_pairs={{0,1},{1,0},{2,3},{3,2},{4,8},{5,9},{6,10},{7,11},{8,4},{9,5},{10,... | collective-permute-start | bytes 6152 | tf_op jit(solution)/shard_map/ppermute | solution.py:407
  61.4 5.1 %collective-permute-start.12 = (f32[1,512]{1,0:T(1,128)S(1)}, f32[1,512]{1,0:T(1,128)S(1)}, u32[]{:S(2)}, u32[]{:S(2)}) collective-permute-start(f32[1,512]{1,0:T(1,128)S(1)} %get-tuple-element.35), channel_id=1, source_target_pairs={{0,2},{1,3},{2,0},{3,1},{4,6},{5,7},{6,4},{7,5},{8,10},{9,11},{10,... | collective-permute-start | bytes 6152 | tf_op jit(solution)/shard_map/ppermute | solution.py:407
  61.9 5.2 %collective-permute-start.13 = (f32[1,512]{1,0:T(1,128)S(1)}, f32[1,512]{1,0:T(1,128)S(1)}, u32[]{:S(2)}, u32[]{:S(2)}) collective-permute-start(f32[1,512]{1,0:T(1,128)S(1)} %get-tuple-element.36), channel_id=1, source_target_pairs={{0,4},{1,5},{2,6},{3,7},{4,0},{5,1},{6,2},{7,3},{8,12},{9,13},{10,... | collective-permute-start | bytes 6152 | tf_op jit(solution)/shard_map/ppermute | solution.py:407
  65.5 4.5 %collective-permute-start.16 = (f32[1,512]{1,0:T(1,128)S(1)}, f32[1,512]{1,0:T(1,128)S(1)}, u32[]{:S(2)}, u32[]{:S(2)}) collective-permute-start(f32[1,512]{1,0:T(1,128)S(1)} %shard_map.32), channel_id=1, source_target_pairs={{0,6},{1,7},{2,4},{3,5},{4,2},{5,3},{6,0},{7,1},{8,14},{9,15},{10,... | collective-permute-start | bytes 6152 | tf_op jit(solution)/shard_map/ppermute | solution.py:407

commit v6 on v5

--- a/solution.py
+++ b/solution.py
@@ -302,7 +302,7 @@
 
 def here_kernel(
     own_ref, mine_ref, twin_ref, side_ref, side_low_ref, ridge_ref, ridge_twin_ref,
-    head_ref, head_twin_ref, tail_ref, tail_twin_ref, mine_out, side_out, above_out,
+    head_ref, tail_ref, mine_out, side_out, above_out,
 ):
     layer, column, _ = place()
     mine_out[...] = own_ref[...]
@@ -313,11 +313,6 @@
     @pl.when(column == 0)
     def _():
         raise_all([side_out], near[1:], whole(mine_ref) + whole(twin_ref))
-
-    @pl.when(layer % 2 == 1)
-    def _():
-        keys = split(head_ref, tail_ref) + split(head_twin_ref, tail_twin_ref)
-        raise_all([mine_out, side_out], near, keys)
 
     @pl.when(layer == 2)
     def _():
@@ -353,7 +348,7 @@
     for at, ref in enumerate(outs):
         ref[...] = begun[at][...] if started else jnp.full(ref.shape, -1.0, jnp.float32)
 
-    @pl.when(layer == worker)
+    @pl.when((layer == worker) if worker else (layer % 2 == 1))
     def _():
         raise_all(outs, query_blocks, [block for blocks in key_blocks for block in blocks])
 
@@ -428,10 +423,12 @@
     (own,) = scored(own_kernel, [rows], 2 * square, mine, twin)
     best = scored(
         here_kernel, [rows] * 3, 8 * square,
-        own, mine, twin, side, side_low, ridge, ridge_twin, near_head, near_head_twin, near_tail, near_tail_twin,
+        own, mine, twin, side, side_low, ridge, ridge_twin, near_head, near_tail,
     )
     flat = [("whole", mine), ("paired", side, side_low)]
     steep = [("split", near_head, near_tail), ("halves", upper, lower)]
+    layers = [("split", near_head, near_tail), ("split", near_head_twin, near_tail_twin)]
+    best = deepened(best[:2], flat, layers, worker=None) + best[2:]
     deep, deep_twin = ("whole", deep_head), ("whole", deep_head_twin)
     best = deepened(best, flat + steep[:1], [deep])
     best = deepened(best, flat + steep[:1], [deep_twin])

time: 71.8 us -> 71.8 us (level)
    pallas_call x8 -> x9, Pallas kernels: 1.76 us -> 1.78 us  [scored(): pl.pallas_call(body, out_shape=[pltpu.VMEM((1, count), jnp.float32) for c...]
where the time goes in v6:
time: 71.8 us; the launch traced here: 70.6 us
  waiting for transfers between devices  38.1 us (53%)
  starting transfers between devices  28.1 us (39%)
  Pallas kernels  3.62 us (5%)
    ppermute x21, waiting for transfers between devices, sent(): return lax.ppermute(value, 'wide', pairs)  38.1 us
    ppermute x21, starting transfers between devices, sent(): return lax.ppermute(value, 'wide', pairs)  28.1 us
    pallas_call x9, Pallas kernels, scored(): pl.pallas_call(body, out_shape=[pltpu.VMEM((1, count), jnp.float32) for c...  1.78 us
    pallas_call x1, Pallas kernels, tagged(): pl.pallas_call(tag_kernel, out_shape=[pltpu.VMEM(shape, jnp.bfloat16) for...  1.54 us
  transfers between devices with their start and end apart: 21, of which 7 were waited for; matrix products, arithmetic and copies ran while one was open for 0% of the time, Pallas kernels for 5%

profile of v6, /device:TPU:0, one launch (start us, length us, event | category | flops | bytes accessed | tf_op | source)
XLA Modules:
  0.0 70.6 jit_solution(12003064605001104026)
XLA Ops:
  0.0 0.5 collective-permute-start.3
  0.5 1.5 %tagged.1 = (bf16[520,768]{1,0:T(8,128)(2,1)S(1)}, bf16[264,768]{1,0:T(8,128)(2,1)S(1)}, bf16[256,768]{1,0:T(8,128)(2,1)S(1)}, bf16[264,768]{1,0:T(8,128)(2,1)S(1)}, bf16[8,512]{1,0:T(8,128)(2,1)S(1)}) custom-call(bf16[512,768]{1,0:T(8,128)(2,1)} %rows_hbm.1, s32[1,512]{1,0:T(1,128)} %bitcast.2), custom_call_target="tpu_custom_call" | custom-call | tf_op jit(solution)/shard_map/tagged/pallas_call | solution.py:175
  2.0 4.2 %collective-permute-start.7 = (bf16[256,768]{1,0:T(8,128)(2,1)S(1)}, bf16[256,768]{1,0:T(8,128)(2,1)S(1)}, u32[]{:S(2)}, u32[]{:S(2)}) collective-permute-start(bf16[256,768]{1,0:T(8,128)(2,1)S(1)} %get-tuple-element.29), channel_id=1, source_target_pairs={{0,4},{1,5},{2,6},{3,7},{4,0},{5,1},{6,2},{7,3},{8,12},{9,13},{10,... | collective-permute-start | bytes 1179656 | tf_op jit(solution)/shard_map/ppermute | solution.py:402
  6.3 1.5 %collective-permute-start.2 = (bf16[264,768]{1,0:T(8,128)(2,1)S(1)}, bf16[264,768]{1,0:T(8,128)(2,1)S(1)}, u32[]{:S(2)}, u32[]{:S(2)}) collective-permute-start(bf16[264,768]{1,0:T(8,128)(2,1)S(1)} %get-tuple-element.27), channel_id=1, source_target_pairs={{0,2},{1,3},{2,0},{3,1},{4,6},{5,7},{6,4},{7,5},{8,10},{9,11},{10,... | collective-permute-start | bytes 1216520 | tf_op jit(solution)/shard_map/ppermute | solution.py:402
  7.8 0.0 collective-permute-start
  7.8 0.5 collective-permute-start.4
  8.3 1.8 %collective-permute-done.4.mark_ref = bf16[8,512]{1,0:T(8,128)(2,1)S(1)} collective-permute-done((bf16[8,512]{1,0:T(8,128)(2,1)S(1)}, bf16[8,512]{1,0:T(8,128)(2,1)S(1)}, u32[]{:S(2)}, u32[]{:S(2)}) %collective-permute-start.4) | collective-permute-done | bytes 8224 | tf_op jit(solution)/shard_map/ppermute | solution.py:402
  10.1 12.7 %collective-permute-start.6 = (bf16[264,768]{1,0:T(8,128)(2,1)S(1)}, bf16[264,768]{1,0:T(8,128)(2,1)S(1)}, u32[]{:S(2)}, u32[]{:S(2)}) collective-permute-start(bf16[264,768]{1,0:T(8,128)(2,1)S(1)} %get-tuple-element.26), channel_id=1, source_target_pairs={{0,4},{1,5},{2,6},{3,7},{4,0},{5,1},{6,2},{7,3},{8,12},{9,13},{10,... | collective-permute-start | bytes 1216520 | tf_op jit(solution)/shard_map/ppermute | solution.py:402
  22.7 0.0 collective-permute-done.7.tail_ref.refs_6_.refs_7_.refs_2_.refs_4_
  22.7 0.0 collective-permute-start.9
  22.7 0.0 collective-permute-done.2.side_low_ref.refs_4_.refs_5_
  22.7 0.1 collective-permute-start.15
  22.8 10.1 %collective-permute-done.6.head_ref.refs_5_.refs_6_.refs_3_ = bf16[264,768]{1,0:T(8,128)(2,1)S(1)} collective-permute-done((bf16[264,768]{1,0:T(8,128)(2,1)S(1)}, bf16[264,768]{1,0:T(8,128)(2,1)S(1)}, u32[]{:S(2)}, u32[]{:S(2)}) %collective-permute-start.6) | collective-permute-done | bytes 405536 | tf_op jit(solution)/shard_map/ppermute | solution.py:402
  32.9 0.0 collective-permute-start.8
  33.0 0.0 collective-permute-done.3.rows_ref
  33.0 0.5 collective-permute-start.10
  33.5 0.3 arrived.1.ridge_ref.refs_2_.refs_0_
  33.8 0.0 collective-permute-done.9.refs_8_.refs_6_
  33.8 0.1 collective-permute-start.5
  33.9 6.1 %collective-permute-done.15.refs_1_.refs_6_.refs_8_ = bf16[264,768]{1,0:T(8,128)(2,1)S(1)} collective-permute-done((bf16[264,768]{1,0:T(8,128)(2,1)S(1)}, bf16[264,768]{1,0:T(8,128)(2,1)S(1)}, u32[]{:S(2)}, u32[]{:S(2)}) %collective-permute-start.15) | collective-permute-done | bytes 405536 | tf_op jit(solution)/shard_map/ppermute | solution.py:402
  39.9 0.0 collective-permute-start.17
  40.0 0.0 collective-permute-done.twin_ref
  40.0 1.6 %collective-permute-start.14 = (bf16[256,768]{1,0:T(8,128)(2,1)S(1)}, bf16[256,768]{1,0:T(8,128)(2,1)S(1)}, u32[]{:S(2)}, u32[]{:S(2)}) collective-permute-start(bf16[256,768]{1,0:T(8,128)(2,1)S(1)} %slice.4), channel_id=1, source_target_pairs={{0,2},{1,3},{2,0},{3,1},{4,6},{5,7},{6,4},{7,5},{8,10},{9,11},{10,... | collective-permute-start | bytes 1179656 | tf_op jit(solution)/shard_map/ppermute | solution.py:402
  41.5 0.0 collective-permute-done.8.refs_7_.refs_5_
  41.5 0.2 collective-permute-start.19
  41.8 0.0 collective-permute-done.10.refs_8_.refs_4_.refs_1_.refs_3_
  41.8 0.5 collective-permute-start.1
  42.3 0.6 shard_map.28.own_ref
  42.9 9.1 %collective-permute-done.14.refs_0_.refs_5_.refs_7_.refs_9_ = bf16[256,768]{1,0:T(8,128)(2,1)S(1)} collective-permute-done((bf16[256,768]{1,0:T(8,128)(2,1)S(1)}, bf16[256,768]{1,0:T(8,128)(2,1)S(1)}, u32[]{:S(2)}, u32[]{:S(2)}) %collective-permute-start.14) | collective-permute-done | bytes 393248 | tf_op jit(solution)/shard_map/ppermute | solution.py:402
  52.0 0.0 collective-permute-start.11
  52.0 0.0 collective-permute-done.17.refs_8_.refs_10_
  52.1 0.0 collective-permute-done.19.refs_2_
  52.1 0.5 collective-permute-start.20
  52.6 0.1 collective-permute-start.18
  52.7 7.5 %collective-permute-done.1.side_ref.refs_3_.refs_4_ = bf16[264,768]{1,0:T(8,128)(2,1)S(1)} collective-permute-done((bf16[264,768]{1,0:T(8,128)(2,1)S(1)}, bf16[264,768]{1,0:T(8,128)(2,1)S(1)}, u32[]{:S(2)}, u32[]{:S(2)}) %collective-permute-start.1) | collective-permute-done | bytes 405536 | tf_op jit(solution)/shard_map/ppermute | solution.py:402
  60.3 0.0 collective-permute-done.5.ridge_twin_ref.refs_3_
  60.3 1.0 %shard_map.29 = (f32[1,512]{1,0:T(1,128)S(1)}, f32[1,512]{1,0:T(1,128)S(1)}, f32[1,512]{1,0:T(1,128)S(1)}) custom-call(f32[1,512]{1,0:T(1,128)S(1)} %shard_map.28.own_ref, bf16[520,768]{1,0:T(8,128)(2,1)S(1)} %get-tuple-element.25.mine_ref.refs_2_.refs_3_, bf16[520,768]{1,0:T(8,128)(2,1)S(1)} %collective-permute-done.twin_ref, ...), custom_call_target="tpu_custom_call" | custom-call | flops 3221225472 | bytes 4806656 | tf_op jit(solution)/shard_map/pallas_call | solution.py:358
  61.4 0.0 collective-permute-done.11.refs_8_.refs_5_
  61.4 0.5 collective-permute-start.12
  61.9 3.6 %collective-permute-start.13 = (f32[1,512]{1,0:T(1,128)S(1)}, f32[1,512]{1,0:T(1,128)S(1)}, u32[]{:S(2)}, u32[]{:S(2)}) collective-permute-start(f32[1,512]{1,0:T(1,128)S(1)} %get-tuple-element.40), channel_id=1, source_target_pairs={{0,4},{1,5},{2,6},{3,7},{4,0},{5,1},{6,2},{7,3},{8,12},{9,13},{10,... | collective-permute-start | bytes 6152 | tf_op jit(solution)/shard_map/ppermute | solution.py:402
  65.5 1.0 %collective-permute-start.16 = (f32[1,512]{1,0:T(1,128)S(1)}, f32[1,512]{1,0:T(1,128)S(1)}, u32[]{:S(2)}, u32[]{:S(2)}) collective-permute-start(f32[1,512]{1,0:T(1,128)S(1)} %shard_map.33), channel_id=1, source_target_pairs={{0,6},{1,7},{2,4},{3,5},{4,2},{5,3},{6,0},{7,1},{8,14},{9,15},{10,... | collective-permute-start | bytes 6152 | tf_op jit(solution)/shard_map/ppermute | solution.py:402
  66.5 0.0 collective-permute-done.20
  66.5 0.0 collective-permute-done.18
  66.5 0.0 collective-permute-done.12
  66.6 0.5 collective-permute-done.13
  67.1 2.9 %collective-permute-done.16 = f32[1,512]{1,0:T(1,128)S(1)} collective-permute-done((f32[1,512]{1,0:T(1,128)S(1)}, f32[1,512]{1,0:T(1,128)S(1)}, u32[]{:S(2)}, u32[]{:S(2)}) %collective-permute-start.16) | collective-permute-done | bytes 2080 | tf_op jit(solution)/shard_map/ppermute | solution.py:402
  70.0 0.6 maximum_maximum_fusion
  (8 shorter events, 0.2 us)
Async XLA Ops:
  0.0 33.0 %collective-permute-start.3 = (bf16[512,768]{1,0:T(8,128)(2,1)}, bf16[512,768]{1,0:T(8,128)(2,1)S(1)}, u32[]{:S(2)}, u32[]{:S(2)}) collective-permute-start(bf16[512,768]{1,0:T(8,128)(2,1)} %rows_hbm.1), channel_id=1, source_target_pairs={{0,1},{1,0},{2,3},{3,2},{4,8},{5,9},{6,10},{7,11},{8,4},{9,5},{10,... | collective-permute-start | bytes 2359304 | tf_op jit(solution)/shard_map/ppermute | solution.py:402
  2.0 20.7 %collective-permute-start.7 = (bf16[256,768]{1,0:T(8,128)(2,1)S(1)}, bf16[256,768]{1,0:T(8,128)(2,1)S(1)}, u32[]{:S(2)}, u32[]{:S(2)}) collective-permute-start(bf16[256,768]{1,0:T(8,128)(2,1)S(1)} %get-tuple-element.29), channel_id=1, source_target_pairs={{0,4},{1,5},{2,6},{3,7},{4,0},{5,1},{6,2},{7,3},{8,12},{9,13},{10,... | collective-permute-start | bytes 1179656 | tf_op jit(solution)/shard_map/ppermute | solution.py:402
  6.3 16.5 %collective-permute-start.2 = (bf16[264,768]{1,0:T(8,128)(2,1)S(1)}, bf16[264,768]{1,0:T(8,128)(2,1)S(1)}, u32[]{:S(2)}, u32[]{:S(2)}) collective-permute-start(bf16[264,768]{1,0:T(8,128)(2,1)S(1)} %get-tuple-element.27), channel_id=1, source_target_pairs={{0,2},{1,3},{2,0},{3,1},{4,6},{5,7},{6,4},{7,5},{8,10},{9,11},{10,... | collective-permute-start | bytes 1216520 | tf_op jit(solution)/shard_map/ppermute | solution.py:402
  7.8 32.2 %collective-permute-start = (bf16[520,768]{1,0:T(8,128)(2,1)S(1)}, bf16[520,768]{1,0:T(8,128)(2,1)S(1)}, u32[]{:S(2)}, u32[]{:S(2)}) collective-permute-start(bf16[520,768]{1,0:T(8,128)(2,1)S(1)} %get-tuple-element.25.mine_ref.refs_2_.refs_3_), channel_id=1, source_target_pairs={{0,1},{1,0},{2,3},{3,2},{4,5},{5,4},{6,7},{7,6},{8,9},{9,8},{10,11... | collective-permute-start | bytes 2396168 | tf_op jit(solution)/shard_map/ppermute | solution.py:402
  7.8 2.3 %collective-permute-start.4 = (bf16[8,512]{1,0:T(8,128)(2,1)S(1)}, bf16[8,512]{1,0:T(8,128)(2,1)S(1)}, u32[]{:S(2)}, u32[]{:S(2)}) collective-permute-start(bf16[8,512]{1,0:T(8,128)(2,1)S(1)} %get-tuple-element.28), channel_id=1, source_target_pairs={{0,1},{1,0},{2,3},{3,2},{4,8},{5,9},{6,10},{7,11},{8,4},{9,5},{10,... | collective-permute-start | bytes 24584 | tf_op jit(solution)/shard_map/ppermute | solution.py:402
  10.1 22.9 %collective-permute-start.6 = (bf16[264,768]{1,0:T(8,128)(2,1)S(1)}, bf16[264,768]{1,0:T(8,128)(2,1)S(1)}, u32[]{:S(2)}, u32[]{:S(2)}) collective-permute-start(bf16[264,768]{1,0:T(8,128)(2,1)S(1)} %get-tuple-element.26), channel_id=1, source_target_pairs={{0,4},{1,5},{2,6},{3,7},{4,0},{5,1},{6,2},{7,3},{8,12},{9,13},{10,... | collective-permute-start | bytes 1216520 | tf_op jit(solution)/shard_map/ppermute | solution.py:402
  22.7 11.0 %collective-permute-start.9 = (bf16[256,768]{1,0:T(8,128)(2,1)S(1)}, bf16[256,768]{1,0:T(8,128)(2,1)S(1)}, u32[]{:S(2)}, u32[]{:S(2)}) collective-permute-start(bf16[256,768]{1,0:T(8,128)(2,1)S(1)} %collective-permute-done.7.tail_ref.refs_6_.refs_7_.refs_2_.refs_4_), channel_id=1, source_target_pairs={{0,1},{1,0},{2,3},{3,2},{4,5},{5,4},{6,7},{7,6},{8,9},{9,8},{10,11... | collective-permute-start | bytes 1179656 | tf_op jit(solution)/shard_map/ppermute | solution.py:402
  22.7 17.2 %collective-permute-start.15 = (bf16[264,768]{1,0:T(8,128)(2,1)S(1)}, bf16[264,768]{1,0:T(8,128)(2,1)S(1)}, u32[]{:S(2)}, u32[]{:S(2)}) collective-permute-start(bf16[264,768]{1,0:T(8,128)(2,1)S(1)} %collective-permute-done.2.side_low_ref.refs_4_.refs_5_), channel_id=1, source_target_pairs={{0,4},{1,5},{2,6},{3,7},{4,0},{5,1},{6,2},{7,3},{8,12},{9,13},{10,... | collective-permute-start | bytes 1216520 | tf_op jit(solution)/shard_map/ppermute | solution.py:402
  32.9 8.6 %collective-permute-start.8 = (bf16[264,768]{1,0:T(8,128)(2,1)S(1)}, bf16[264,768]{1,0:T(8,128)(2,1)S(1)}, u32[]{:S(2)}, u32[]{:S(2)}) collective-permute-start(bf16[264,768]{1,0:T(8,128)(2,1)S(1)} %collective-permute-done.6.head_ref.refs_5_.refs_6_.refs_3_), channel_id=1, source_target_pairs={{0,1},{1,0},{2,3},{3,2},{4,5},{5,4},{6,7},{7,6},{8,9},{9,8},{10,11... | collective-permute-start | bytes 1216520 | tf_op jit(solution)/shard_map/ppermute | solution.py:402
  33.0 8.8 %collective-permute-start.10 = (bf16[264,768]{1,0:T(8,128)(2,1)S(1)}, bf16[264,768]{1,0:T(8,128)(2,1)S(1)}, u32[]{:S(2)}, u32[]{:S(2)}) collective-permute-start(bf16[264,768]{1,0:T(8,128)(2,1)S(1)} %collective-permute-done.6.head_ref.refs_5_.refs_6_.refs_3_), channel_id=1, source_target_pairs={{0,1},{1,0},{2,3},{3,2},{4,8},{5,9},{6,10},{7,11},{8,4},{9,5},{10,... | collective-permute-start | bytes 1216520 | tf_op jit(solution)/shard_map/ppermute | solution.py:402
  33.8 26.5 %collective-permute-start.5 = (bf16[520,768]{1,0:T(8,128)(2,1)S(1)}, bf16[520,768]{1,0:T(8,128)(2,1)S(1)}, u32[]{:S(2)}, u32[]{:S(2)}) collective-permute-start(bf16[520,768]{1,0:T(8,128)(2,1)S(1)} %arrived.1.ridge_ref.refs_2_.refs_0_), channel_id=1, source_target_pairs={{0,1},{1,0},{2,3},{3,2},{4,5},{5,4},{6,7},{7,6},{8,9},{9,8},{10,11... | collective-permute-start | bytes 2396168 | tf_op jit(solution)/shard_map/ppermute | solution.py:402
  39.9 12.1 %collective-permute-start.17 = (bf16[264,768]{1,0:T(8,128)(2,1)S(1)}, bf16[264,768]{1,0:T(8,128)(2,1)S(1)}, u32[]{:S(2)}, u32[]{:S(2)}) collective-permute-start(bf16[264,768]{1,0:T(8,128)(2,1)S(1)} %collective-permute-done.15.refs_1_.refs_6_.refs_8_), channel_id=1, source_target_pairs={{0,1},{1,0},{2,3},{3,2},{4,5},{5,4},{6,7},{7,6},{8,9},{9,8},{10,11... | collective-permute-start | bytes 1216520 | tf_op jit(solution)/shard_map/ppermute | solution.py:402
  40.0 12.1 %collective-permute-start.14 = (bf16[256,768]{1,0:T(8,128)(2,1)S(1)}, bf16[256,768]{1,0:T(8,128)(2,1)S(1)}, u32[]{:S(2)}, u32[]{:S(2)}) collective-permute-start(bf16[256,768]{1,0:T(8,128)(2,1)S(1)} %slice.4), channel_id=1, source_target_pairs={{0,2},{1,3},{2,0},{3,1},{4,6},{5,7},{6,4},{7,5},{8,10},{9,11},{10,... | collective-permute-start | bytes 1179656 | tf_op jit(solution)/shard_map/ppermute | solution.py:402
  41.5 10.5 %collective-permute-start.19 = (bf16[256,768]{1,0:T(8,128)(2,1)S(1)}, bf16[256,768]{1,0:T(8,128)(2,1)S(1)}, u32[]{:S(2)}, u32[]{:S(2)}) collective-permute-start(bf16[256,768]{1,0:T(8,128)(2,1)S(1)} %collective-permute-done.7.tail_ref.refs_6_.refs_7_.refs_2_.refs_4_), channel_id=1, source_target_pairs={{0,1},{1,0},{2,3},{3,2},{4,8},{5,9},{6,10},{7,11},{8,4},{9,5},{10,... | collective-permute-start | bytes 1179656 | tf_op jit(solution)/shard_map/ppermute | solution.py:402
  41.8 18.5 %collective-permute-start.1 = (bf16[264,768]{1,0:T(8,128)(2,1)S(1)}, bf16[264,768]{1,0:T(8,128)(2,1)S(1)}, u32[]{:S(2)}, u32[]{:S(2)}) collective-permute-start(bf16[264,768]{1,0:T(8,128)(2,1)S(1)} %get-tuple-element.26), channel_id=1, source_target_pairs={{0,2},{1,3},{2,0},{3,1},{4,6},{5,7},{6,4},{7,5},{8,10},{9,11},{10,... | collective-permute-start | bytes 1216520 | tf_op jit(solution)/shard_map/ppermute | solution.py:402
  52.0 9.3 %collective-permute-start.11 = (bf16[264,768]{1,0:T(8,128)(2,1)S(1)}, bf16[264,768]{1,0:T(8,128)(2,1)S(1)}, u32[]{:S(2)}, u32[]{:S(2)}) collective-permute-start(bf16[264,768]{1,0:T(8,128)(2,1)S(1)} %collective-permute-done.10.refs_8_.refs_4_.refs_1_.refs_3_), channel_id=1, source_target_pairs={{0,1},{1,0},{2,3},{3,2},{4,5},{5,4},{6,7},{7,6},{8,9},{9,8},{10,11... | collective-permute-start | bytes 1216520 | tf_op jit(solution)/shard_map/ppermute | solution.py:402
  52.1 14.4 %collective-permute-start.20 = (f32[1,512]{1,0:T(1,128)S(1)}, f32[1,512]{1,0:T(1,128)S(1)}, u32[]{:S(2)}, u32[]{:S(2)}) collective-permute-start(f32[1,512]{1,0:T(1,128)S(1)} %shard_map.36), channel_id=1, source_target_pairs={{0,1},{1,0},{2,3},{3,2},{4,12},{5,13},{6,14},{7,15},{8,4},{9,5},{1... | collective-permute-start | bytes 6152 | tf_op jit(solution)/shard_map/ppermute | solution.py:402
  52.6 13.9 %collective-permute-start.18 = (f32[1,512]{1,0:T(1,128)S(1)}, f32[1,512]{1,0:T(1,128)S(1)}, u32[]{:S(2)}, u32[]{:S(2)}) collective-permute-start(f32[1,512]{1,0:T(1,128)S(1)} %get-tuple-element.43), channel_id=1, source_target_pairs={{0,1},{1,0},{2,3},{3,2},{4,8},{5,9},{6,10},{7,11},{8,4},{9,5},{10,... | collective-permute-start | bytes 6152 | tf_op jit(solution)/shard_map/ppermute | solution.py:402
  61.4 5.1 %collective-permute-start.12 = (f32[1,512]{1,0:T(1,128)S(1)}, f32[1,512]{1,0:T(1,128)S(1)}, u32[]{:S(2)}, u32[]{:S(2)}) collective-permute-start(f32[1,512]{1,0:T(1,128)S(1)} %get-tuple-element.39), channel_id=1, source_target_pairs={{0,2},{1,3},{2,0},{3,1},{4,6},{5,7},{6,4},{7,5},{8,10},{9,11},{10,... | collective-permute-start | bytes 6152 | tf_op jit(solution)/shard_map/ppermute | solution.py:402
  61.9 5.2 %collective-permute-start.13 = (f32[1,512]{1,0:T(1,128)S(1)}, f32[1,512]{1,0:T(1,128)S(1)}, u32[]{:S(2)}, u32[]{:S(2)}) collective-permute-start(f32[1,512]{1,0:T(1,128)S(1)} %get-tuple-element.40), channel_id=1, source_target_pairs={{0,4},{1,5},{2,6},{3,7},{4,0},{5,1},{6,2},{7,3},{8,12},{9,13},{10,... | collective-permute-start | bytes 6152 | tf_op jit(solution)/shard_map/ppermute | solution.py:402
  65.5 4.5 %collective-permute-start.16 = (f32[1,512]{1,0:T(1,128)S(1)}, f32[1,512]{1,0:T(1,128)S(1)}, u32[]{:S(2)}, u32[]{:S(2)}) collective-permute-start(f32[1,512]{1,0:T(1,128)S(1)} %shard_map.33), channel_id=1, source_target_pairs={{0,6},{1,7},{2,4},{3,5},{4,2},{5,3},{6,0},{7,1},{8,14},{9,15},{10,... | collective-permute-start | bytes 6152 | tf_op jit(solution)/shard_map/ppermute | solution.py:402

commit v7 on v6

--- a/solution.py
+++ b/solution.py
@@ -284,6 +284,10 @@
             raise_best(out_ref, block.low, block, keys)
 
 
+def finish_kernel(*refs):
+    refs[-1][...] = functools.reduce(jnp.maximum, [ref[...] for ref in refs[:-1]])
+
+
 def place():
     index = lax.axis_index("wide")
     return index // 4, (index // 2) % 2, index % 2
@@ -449,7 +453,14 @@
     from_lifted = sent(lifted, spring)
     from_lent = sent(lent, inner)
     parts = (first, from_side, from_below, from_far, from_lent, from_lifted)
-    return functools.reduce(jnp.maximum, parts)[0]
+    (best,) = pl.pallas_call(
+        finish_kernel,
+        out_shape=[jax.ShapeDtypeStruct((1, rows), jnp.float32)],
+        in_specs=[pl.BlockSpec(memory_space=pltpu.VMEM)] * len(parts),
+        compiler_params=PARAMS,
+        name="finish",
+    )(*[pltpu.with_memory_space_constraint(value, pltpu.VMEM) for value in parts])
+    return best.reshape(rows)
 
 
 def per_device(embeddings, cluster_id):

time: 71.8 us -> 71.8 us (level)
  no operation moved by 1% of the time
where the time goes in v7:
time: 71.8 us; the launch traced here: 70.6 us
  waiting for transfers between devices  38.2 us (53%)
  starting transfers between devices  28.1 us (39%)
  Pallas kernels  4.18 us (6%)
    ppermute x21, waiting for transfers between devices, sent(): return lax.ppermute(value, 'wide', pairs)  38.2 us
    ppermute x21, starting transfers between devices, sent(): return lax.ppermute(value, 'wide', pairs)  28.1 us
    pallas_call x9, Pallas kernels, scored(): pl.pallas_call(body, out_shape=[pltpu.VMEM((1, count), jnp.float32) for c...  1.76 us
    pallas_call x1, Pallas kernels, tagged(): pl.pallas_call(tag_kernel, out_shape=[pltpu.VMEM(shape, jnp.bfloat16) for...  1.54 us
  transfers between devices with their start and end apart: 21, of which 7 were waited for; matrix products, arithmetic and copies ran while one was open for 0% of the time, Pallas kernels for 5%

profile of v7, /device:TPU:0, one launch (start us, length us, event | category | flops | bytes accessed | tf_op | source)
XLA Modules:
  0.0 70.6 jit_solution(1149819714824069779)
XLA Ops:
  0.0 0.5 collective-permute-start.3
  0.5 1.5 %tagged.1 = (bf16[520,768]{1,0:T(8,128)(2,1)S(1)}, bf16[264,768]{1,0:T(8,128)(2,1)S(1)}, bf16[256,768]{1,0:T(8,128)(2,1)S(1)}, bf16[264,768]{1,0:T(8,128)(2,1)S(1)}, bf16[8,512]{1,0:T(8,128)(2,1)S(1)}) custom-call(bf16[512,768]{1,0:T(8,128)(2,1)} %rows_hbm.1, s32[1,512]{1,0:T(1,128)} %bitcast.2), custom_call_target="tpu_custom_call" | custom-call | tf_op jit(solution)/shard_map/tagged/pallas_call | solution.py:175
  2.0 4.2 %collective-permute-start.7 = (bf16[256,768]{1,0:T(8,128)(2,1)S(1)}, bf16[256,768]{1,0:T(8,128)(2,1)S(1)}, u32[]{:S(2)}, u32[]{:S(2)}) collective-permute-start(bf16[256,768]{1,0:T(8,128)(2,1)S(1)} %get-tuple-element.29), channel_id=1, source_target_pairs={{0,4},{1,5},{2,6},{3,7},{4,0},{5,1},{6,2},{7,3},{8,12},{9,13},{10,... | collective-permute-start | bytes 1179656 | tf_op jit(solution)/shard_map/ppermute | solution.py:406
  6.3 1.5 %collective-permute-start.2 = (bf16[264,768]{1,0:T(8,128)(2,1)S(1)}, bf16[264,768]{1,0:T(8,128)(2,1)S(1)}, u32[]{:S(2)}, u32[]{:S(2)}) collective-permute-start(bf16[264,768]{1,0:T(8,128)(2,1)S(1)} %get-tuple-element.27), channel_id=1, source_target_pairs={{0,2},{1,3},{2,0},{3,1},{4,6},{5,7},{6,4},{7,5},{8,10},{9,11},{10,... | collective-permute-start | bytes 1216520 | tf_op jit(solution)/shard_map/ppermute | solution.py:406
  7.8 0.0 collective-permute-start
  7.8 0.5 collective-permute-start.4
  8.3 1.8 %collective-permute-done.4.mark_ref = bf16[8,512]{1,0:T(8,128)(2,1)S(1)} collective-permute-done((bf16[8,512]{1,0:T(8,128)(2,1)S(1)}, bf16[8,512]{1,0:T(8,128)(2,1)S(1)}, u32[]{:S(2)}, u32[]{:S(2)}) %collective-permute-start.4) | collective-permute-done | bytes 8224 | tf_op jit(solution)/shard_map/ppermute | solution.py:406
  10.1 12.7 %collective-permute-start.6 = (bf16[264,768]{1,0:T(8,128)(2,1)S(1)}, bf16[264,768]{1,0:T(8,128)(2,1)S(1)}, u32[]{:S(2)}, u32[]{:S(2)}) collective-permute-start(bf16[264,768]{1,0:T(8,128)(2,1)S(1)} %get-tuple-element.26), channel_id=1, source_target_pairs={{0,4},{1,5},{2,6},{3,7},{4,0},{5,1},{6,2},{7,3},{8,12},{9,13},{10,... | collective-permute-start | bytes 1216520 | tf_op jit(solution)/shard_map/ppermute | solution.py:406
  22.7 0.0 collective-permute-done.7.tail_ref.refs_6_.refs_7_.refs_2_.refs_4_
  22.7 0.0 collective-permute-start.9
  22.7 0.0 collective-permute-done.2.side_low_ref.refs_4_.refs_5_
  22.7 0.1 collective-permute-start.15
  22.8 10.1 %collective-permute-done.6.head_ref.refs_5_.refs_6_.refs_3_ = bf16[264,768]{1,0:T(8,128)(2,1)S(1)} collective-permute-done((bf16[264,768]{1,0:T(8,128)(2,1)S(1)}, bf16[264,768]{1,0:T(8,128)(2,1)S(1)}, u32[]{:S(2)}, u32[]{:S(2)}) %collective-permute-start.6) | collective-permute-done | bytes 405536 | tf_op jit(solution)/shard_map/ppermute | solution.py:406
  32.9 0.0 collective-permute-start.8
  33.0 0.0 collective-permute-done.3.rows_ref
  33.0 0.5 collective-permute-start.10
  33.5 0.3 arrived.1.ridge_ref.refs_2_.refs_0_
  33.8 0.0 collective-permute-done.9.refs_8_.refs_6_
  33.8 0.1 collective-permute-start.5
  33.9 6.1 %collective-permute-done.15.refs_1_.refs_6_.refs_8_ = bf16[264,768]{1,0:T(8,128)(2,1)S(1)} collective-permute-done((bf16[264,768]{1,0:T(8,128)(2,1)S(1)}, bf16[264,768]{1,0:T(8,128)(2,1)S(1)}, u32[]{:S(2)}, u32[]{:S(2)}) %collective-permute-start.15) | collective-permute-done | bytes 405536 | tf_op jit(solution)/shard_map/ppermute | solution.py:406
  39.9 0.0 collective-permute-start.17
  40.0 0.0 collective-permute-done.twin_ref
  40.0 1.6 %collective-permute-start.14 = (bf16[256,768]{1,0:T(8,128)(2,1)S(1)}, bf16[256,768]{1,0:T(8,128)(2,1)S(1)}, u32[]{:S(2)}, u32[]{:S(2)}) collective-permute-start(bf16[256,768]{1,0:T(8,128)(2,1)S(1)} %slice.4), channel_id=1, source_target_pairs={{0,2},{1,3},{2,0},{3,1},{4,6},{5,7},{6,4},{7,5},{8,10},{9,11},{10,... | collective-permute-start | bytes 1179656 | tf_op jit(solution)/shard_map/ppermute | solution.py:406
  41.5 0.0 collective-permute-done.8.refs_7_.refs_5_
  41.5 0.2 collective-permute-start.19
  41.8 0.0 collective-permute-done.10.refs_8_.refs_4_.refs_1_.refs_3_
  41.8 0.5 collective-permute-start.1
  42.3 0.6 shard_map.28.own_ref
  42.9 9.1 %collective-permute-done.14.refs_0_.refs_5_.refs_7_.refs_9_ = bf16[256,768]{1,0:T(8,128)(2,1)S(1)} collective-permute-done((bf16[256,768]{1,0:T(8,128)(2,1)S(1)}, bf16[256,768]{1,0:T(8,128)(2,1)S(1)}, u32[]{:S(2)}, u32[]{:S(2)}) %collective-permute-start.14) | collective-permute-done | bytes 393248 | tf_op jit(solution)/shard_map/ppermute | solution.py:406
  52.0 0.0 collective-permute-start.11
  52.0 0.0 collective-permute-done.17.refs_8_.refs_10_
  52.1 0.5 collective-permute-start.18
  52.5 0.0 collective-permute-done.19.refs_2_
  52.6 0.1 collective-permute-start.20
  52.6 7.6 %collective-permute-done.1.side_ref.refs_3_.refs_4_ = bf16[264,768]{1,0:T(8,128)(2,1)S(1)} collective-permute-done((bf16[264,768]{1,0:T(8,128)(2,1)S(1)}, bf16[264,768]{1,0:T(8,128)(2,1)S(1)}, u32[]{:S(2)}, u32[]{:S(2)}) %collective-permute-start.1) | collective-permute-done | bytes 405536 | tf_op jit(solution)/shard_map/ppermute | solution.py:406
  60.3 0.0 collective-permute-done.5.ridge_twin_ref.refs_3_
  60.3 1.0 %shard_map.29 = (f32[1,512]{1,0:T(1,128)S(1)}, f32[1,512]{1,0:T(1,128)S(1)}, f32[1,512]{1,0:T(1,128)S(1)}) custom-call(f32[1,512]{1,0:T(1,128)S(1)} %shard_map.28.own_ref, bf16[520,768]{1,0:T(8,128)(2,1)S(1)} %get-tuple-element.25.mine_ref.refs_2_.refs_3_, bf16[520,768]{1,0:T(8,128)(2,1)S(1)} %collective-permute-done.twin_ref, ...), custom_call_target="tpu_custom_call" | custom-call | flops 3221225472 | bytes 4806656 | tf_op jit(solution)/shard_map/pallas_call | solution.py:362
  61.4 0.0 collective-permute-done.11.refs_8_.refs_5_
  61.4 0.5 collective-permute-start.12
  61.9 3.6 %collective-permute-start.13 = (f32[1,512]{1,0:T(1,128)S(1)}, f32[1,512]{1,0:T(1,128)S(1)}, u32[]{:S(2)}, u32[]{:S(2)}) collective-permute-start(f32[1,512]{1,0:T(1,128)S(1)} %get-tuple-element.40), channel_id=1, source_target_pairs={{0,4},{1,5},{2,6},{3,7},{4,0},{5,1},{6,2},{7,3},{8,12},{9,13},{10,... | collective-permute-start | bytes 6152 | tf_op jit(solution)/shard_map/ppermute | solution.py:406
  65.5 1.0 %collective-permute-start.16 = (f32[1,512]{1,0:T(1,128)S(1)}, f32[1,512]{1,0:T(1,128)S(1)}, u32[]{:S(2)}, u32[]{:S(2)}) collective-permute-start(f32[1,512]{1,0:T(1,128)S(1)} %shard_map.33), channel_id=1, source_target_pairs={{0,6},{1,7},{2,4},{3,5},{4,2},{5,3},{6,0},{7,1},{8,14},{9,15},{10,... | collective-permute-start | bytes 6152 | tf_op jit(solution)/shard_map/ppermute | solution.py:406
  66.5 0.0 collective-permute-done.18.refs_4_
  66.5 0.0 collective-permute-done.20.refs_5_
  66.6 0.0 collective-permute-done.12.refs_1_
  66.6 0.5 collective-permute-done.13.refs_2_
  67.1 2.9 %collective-permute-done.16.refs_3_ = f32[1,512]{1,0:T(1,128)S(1)} collective-permute-done((f32[1,512]{1,0:T(1,128)S(1)}, f32[1,512]{1,0:T(1,128)S(1)}, u32[]{:S(2)}, u32[]{:S(2)}) %collective-permute-start.16) | collective-permute-done | bytes 2080 | tf_op jit(solution)/shard_map/ppermute | solution.py:406
  70.0 0.6 finish.1
  (8 shorter events, 0.1 us)
Async XLA Ops:
  0.0 33.0 %collective-permute-start.3 = (bf16[512,768]{1,0:T(8,128)(2,1)}, bf16[512,768]{1,0:T(8,128)(2,1)S(1)}, u32[]{:S(2)}, u32[]{:S(2)}) collective-permute-start(bf16[512,768]{1,0:T(8,128)(2,1)} %rows_hbm.1), channel_id=1, source_target_pairs={{0,1},{1,0},{2,3},{3,2},{4,8},{5,9},{6,10},{7,11},{8,4},{9,5},{10,... | collective-permute-start | bytes 2359304 | tf_op jit(solution)/shard_map/ppermute | solution.py:406
  2.0 20.7 %collective-permute-start.7 = (bf16[256,768]{1,0:T(8,128)(2,1)S(1)}, bf16[256,768]{1,0:T(8,128)(2,1)S(1)}, u32[]{:S(2)}, u32[]{:S(2)}) collective-permute-start(bf16[256,768]{1,0:T(8,128)(2,1)S(1)} %get-tuple-element.29), channel_id=1, source_target_pairs={{0,4},{1,5},{2,6},{3,7},{4,0},{5,1},{6,2},{7,3},{8,12},{9,13},{10,... | collective-permute-start | bytes 1179656 | tf_op jit(solution)/shard_map/ppermute | solution.py:406
  6.3 16.5 %collective-permute-start.2 = (bf16[264,768]{1,0:T(8,128)(2,1)S(1)}, bf16[264,768]{1,0:T(8,128)(2,1)S(1)}, u32[]{:S(2)}, u32[]{:S(2)}) collective-permute-start(bf16[264,768]{1,0:T(8,128)(2,1)S(1)} %get-tuple-element.27), channel_id=1, source_target_pairs={{0,2},{1,3},{2,0},{3,1},{4,6},{5,7},{6,4},{7,5},{8,10},{9,11},{10,... | collective-permute-start | bytes 1216520 | tf_op jit(solution)/shard_map/ppermute | solution.py:406
  7.8 32.2 %collective-permute-start = (bf16[520,768]{1,0:T(8,128)(2,1)S(1)}, bf16[520,768]{1,0:T(8,128)(2,1)S(1)}, u32[]{:S(2)}, u32[]{:S(2)}) collective-permute-start(bf16[520,768]{1,0:T(8,128)(2,1)S(1)} %get-tuple-element.25.mine_ref.refs_2_.refs_3_), channel_id=1, source_target_pairs={{0,1},{1,0},{2,3},{3,2},{4,5},{5,4},{6,7},{7,6},{8,9},{9,8},{10,11... | collective-permute-start | bytes 2396168 | tf_op jit(solution)/shard_map/ppermute | solution.py:406
  7.8 2.3 %collective-permute-start.4 = (bf16[8,512]{1,0:T(8,128)(2,1)S(1)}, bf16[8,512]{1,0:T(8,128)(2,1)S(1)}, u32[]{:S(2)}, u32[]{:S(2)}) collective-permute-start(bf16[8,512]{1,0:T(8,128)(2,1)S(1)} %get-tuple-element.28), channel_id=1, source_target_pairs={{0,1},{1,0},{2,3},{3,2},{4,8},{5,9},{6,10},{7,11},{8,4},{9,5},{10,... | collective-permute-start | bytes 24584 | tf_op jit(solution)/shard_map/ppermute | solution.py:406
  10.1 22.9 %collective-permute-start.6 = (bf16[264,768]{1,0:T(8,128)(2,1)S(1)}, bf16[264,768]{1,0:T(8,128)(2,1)S(1)}, u32[]{:S(2)}, u32[]{:S(2)}) collective-permute-start(bf16[264,768]{1,0:T(8,128)(2,1)S(1)} %get-tuple-element.26), channel_id=1, source_target_pairs={{0,4},{1,5},{2,6},{3,7},{4,0},{5,1},{6,2},{7,3},{8,12},{9,13},{10,... | collective-permute-start | bytes 1216520 | tf_op jit(solution)/shard_map/ppermute | solution.py:406
  22.7 11.0 %collective-permute-start.9 = (bf16[256,768]{1,0:T(8,128)(2,1)S(1)}, bf16[256,768]{1,0:T(8,128)(2,1)S(1)}, u32[]{:S(2)}, u32[]{:S(2)}) collective-permute-start(bf16[256,768]{1,0:T(8,128)(2,1)S(1)} %collective-permute-done.7.tail_ref.refs_6_.refs_7_.refs_2_.refs_4_), channel_id=1, source_target_pairs={{0,1},{1,0},{2,3},{3,2},{4,5},{5,4},{6,7},{7,6},{8,9},{9,8},{10,11... | collective-permute-start | bytes 1179656 | tf_op jit(solution)/shard_map/ppermute | solution.py:406
  22.7 17.2 %collective-permute-start.15 = (bf16[264,768]{1,0:T(8,128)(2,1)S(1)}, bf16[264,768]{1,0:T(8,128)(2,1)S(1)}, u32[]{:S(2)}, u32[]{:S(2)}) collective-permute-start(bf16[264,768]{1,0:T(8,128)(2,1)S(1)} %collective-permute-done.2.side_low_ref.refs_4_.refs_5_), channel_id=1, source_target_pairs={{0,4},{1,5},{2,6},{3,7},{4,0},{5,1},{6,2},{7,3},{8,12},{9,13},{10,... | collective-permute-start | bytes 1216520 | tf_op jit(solution)/shard_map/ppermute | solution.py:406
  32.9 8.6 %collective-permute-start.8 = (bf16[264,768]{1,0:T(8,128)(2,1)S(1)}, bf16[264,768]{1,0:T(8,128)(2,1)S(1)}, u32[]{:S(2)}, u32[]{:S(2)}) collective-permute-start(bf16[264,768]{1,0:T(8,128)(2,1)S(1)} %collective-permute-done.6.head_ref.refs_5_.refs_6_.refs_3_), channel_id=1, source_target_pairs={{0,1},{1,0},{2,3},{3,2},{4,5},{5,4},{6,7},{7,6},{8,9},{9,8},{10,11... | collective-permute-start | bytes 1216520 | tf_op jit(solution)/shard_map/ppermute | solution.py:406
  33.0 8.8 %collective-permute-start.10 = (bf16[264,768]{1,0:T(8,128)(2,1)S(1)}, bf16[264,768]{1,0:T(8,128)(2,1)S(1)}, u32[]{:S(2)}, u32[]{:S(2)}) collective-permute-start(bf16[264,768]{1,0:T(8,128)(2,1)S(1)} %collective-permute-done.6.head_ref.refs_5_.refs_6_.refs_3_), channel_id=1, source_target_pairs={{0,1},{1,0},{2,3},{3,2},{4,8},{5,9},{6,10},{7,11},{8,4},{9,5},{10,... | collective-permute-start | bytes 1216520 | tf_op jit(solution)/shard_map/ppermute | solution.py:406
  33.8 26.5 %collective-permute-start.5 = (bf16[520,768]{1,0:T(8,128)(2,1)S(1)}, bf16[520,768]{1,0:T(8,128)(2,1)S(1)}, u32[]{:S(2)}, u32[]{:S(2)}) collective-permute-start(bf16[520,768]{1,0:T(8,128)(2,1)S(1)} %arrived.1.ridge_ref.refs_2_.refs_0_), channel_id=1, source_target_pairs={{0,1},{1,0},{2,3},{3,2},{4,5},{5,4},{6,7},{7,6},{8,9},{9,8},{10,11... | collective-permute-start | bytes 2396168 | tf_op jit(solution)/shard_map/ppermute | solution.py:406
  39.9 12.1 %collective-permute-start.17 = (bf16[264,768]{1,0:T(8,128)(2,1)S(1)}, bf16[264,768]{1,0:T(8,128)(2,1)S(1)}, u32[]{:S(2)}, u32[]{:S(2)}) collective-permute-start(bf16[264,768]{1,0:T(8,128)(2,1)S(1)} %collective-permute-done.15.refs_1_.refs_6_.refs_8_), channel_id=1, source_target_pairs={{0,1},{1,0},{2,3},{3,2},{4,5},{5,4},{6,7},{7,6},{8,9},{9,8},{10,11... | collective-permute-start | bytes 1216520 | tf_op jit(solution)/shard_map/ppermute | solution.py:406
  40.0 12.1 %collective-permute-start.14 = (bf16[256,768]{1,0:T(8,128)(2,1)S(1)}, bf16[256,768]{1,0:T(8,128)(2,1)S(1)}, u32[]{:S(2)}, u32[]{:S(2)}) collective-permute-start(bf16[256,768]{1,0:T(8,128)(2,1)S(1)} %slice.4), channel_id=1, source_target_pairs={{0,2},{1,3},{2,0},{3,1},{4,6},{5,7},{6,4},{7,5},{8,10},{9,11},{10,... | collective-permute-start | bytes 1179656 | tf_op jit(solution)/shard_map/ppermute | solution.py:406
  41.5 11.0 %collective-permute-start.19 = (bf16[256,768]{1,0:T(8,128)(2,1)S(1)}, bf16[256,768]{1,0:T(8,128)(2,1)S(1)}, u32[]{:S(2)}, u32[]{:S(2)}) collective-permute-start(bf16[256,768]{1,0:T(8,128)(2,1)S(1)} %collective-permute-done.7.tail_ref.refs_6_.refs_7_.refs_2_.refs_4_), channel_id=1, source_target_pairs={{0,1},{1,0},{2,3},{3,2},{4,8},{5,9},{6,10},{7,11},{8,4},{9,5},{10,... | collective-permute-start | bytes 1179656 | tf_op jit(solution)/shard_map/ppermute | solution.py:406
  41.8 18.5 %collective-permute-start.1 = (bf16[264,768]{1,0:T(8,128)(2,1)S(1)}, bf16[264,768]{1,0:T(8,128)(2,1)S(1)}, u32[]{:S(2)}, u32[]{:S(2)}) collective-permute-start(bf16[264,768]{1,0:T(8,128)(2,1)S(1)} %get-tuple-element.26), channel_id=1, source_target_pairs={{0,2},{1,3},{2,0},{3,1},{4,6},{5,7},{6,4},{7,5},{8,10},{9,11},{10,... | collective-permute-start | bytes 1216520 | tf_op jit(solution)/shard_map/ppermute | solution.py:406
  52.0 9.3 %collective-permute-start.11 = (bf16[264,768]{1,0:T(8,128)(2,1)S(1)}, bf16[264,768]{1,0:T(8,128)(2,1)S(1)}, u32[]{:S(2)}, u32[]{:S(2)}) collective-permute-start(bf16[264,768]{1,0:T(8,128)(2,1)S(1)} %collective-permute-done.10.refs_8_.refs_4_.refs_1_.refs_3_), channel_id=1, source_target_pairs={{0,1},{1,0},{2,3},{3,2},{4,5},{5,4},{6,7},{7,6},{8,9},{9,8},{10,11... | collective-permute-start | bytes 1216520 | tf_op jit(solution)/shard_map/ppermute | solution.py:406
  52.1 14.5 %collective-permute-start.18 = (f32[1,512]{1,0:T(1,128)S(1)}, f32[1,512]{1,0:T(1,128)S(1)}, u32[]{:S(2)}, u32[]{:S(2)}) collective-permute-start(f32[1,512]{1,0:T(1,128)S(1)} %get-tuple-element.43), channel_id=1, source_target_pairs={{0,1},{1,0},{2,3},{3,2},{4,8},{5,9},{6,10},{7,11},{8,4},{9,5},{10,... | collective-permute-start | bytes 6152 | tf_op jit(solution)/shard_map/ppermute | solution.py:406
  52.6 14.0 %collective-permute-start.20 = (f32[1,512]{1,0:T(1,128)S(1)}, f32[1,512]{1,0:T(1,128)S(1)}, u32[]{:S(2)}, u32[]{:S(2)}) collective-permute-start(f32[1,512]{1,0:T(1,128)S(1)} %shard_map.36), channel_id=1, source_target_pairs={{0,1},{1,0},{2,3},{3,2},{4,12},{5,13},{6,14},{7,15},{8,4},{9,5},{1... | collective-permute-start | bytes 6152 | tf_op jit(solution)/shard_map/ppermute | solution.py:406
  61.4 5.1 %collective-permute-start.12 = (f32[1,512]{1,0:T(1,128)S(1)}, f32[1,512]{1,0:T(1,128)S(1)}, u32[]{:S(2)}, u32[]{:S(2)}) collective-permute-start(f32[1,512]{1,0:T(1,128)S(1)} %get-tuple-element.39), channel_id=1, source_target_pairs={{0,2},{1,3},{2,0},{3,1},{4,6},{5,7},{6,4},{7,5},{8,10},{9,11},{10,... | collective-permute-start | bytes 6152 | tf_op jit(solution)/shard_map/ppermute | solution.py:406
  61.9 5.2 %collective-permute-start.13 = (f32[1,512]{1,0:T(1,128)S(1)}, f32[1,512]{1,0:T(1,128)S(1)}, u32[]{:S(2)}, u32[]{:S(2)}) collective-permute-start(f32[1,512]{1,0:T(1,128)S(1)} %get-tuple-element.40), channel_id=1, source_target_pairs={{0,4},{1,5},{2,6},{3,7},{4,0},{5,1},{6,2},{7,3},{8,12},{9,13},{10,... | collective-permute-start | bytes 6152 | tf_op jit(solution)/shard_map/ppermute | solution.py:406
  65.5 4.5 %collective-permute-start.16 = (f32[1,512]{1,0:T(1,128)S(1)}, f32[1,512]{1,0:T(1,128)S(1)}, u32[]{:S(2)}, u32[]{:S(2)}) collective-permute-start(f32[1,512]{1,0:T(1,128)S(1)} %shard_map.33), channel_id=1, source_target_pairs={{0,6},{1,7},{2,4},{3,5},{4,2},{5,3},{6,0},{7,1},{8,14},{9,15},{10,... | collective-permute-start | bytes 6152 | tf_op jit(solution)/shard_map/ppermute | solution.py:406
